TPU v7x, 512 devices: a whole 4x8x8 slice. The times are simulated.
512 devices in a mesh: section: 4 (over y_lo), row: 16 (over z, core), col: 8 (over y_hi, x).
Axes of the slice: x: 4, y: 8 (y_hi: 2, y_lo: 4; y = y_hi * 4 + y_lo), z: 8, core: 2. Of those that a mesh axis runs over, the one named last changes fastest.
Arguments:
- section_input: bfloat16 [4, 2, 128, 128, 128], P('section', None, 'row', 'col'), may hold values from -6 to 6
- first_pre: bfloat16 [4, 2, 128, 128, 128], P('section', None, 'row', 'col'), may hold values from -6 to 6
- second_pre: bfloat16 [4, 2, 128, 128, 128], P('section', None, 'row', 'col'), may hold values from -6 to 6
- out_grad: bfloat16 [2, 128, 128, 128], P(None, 'row', 'col'), may hold values from -6 to 6
- kernels: bfloat16 [4, 2, 3, 3, 128, 128], P('section'), may hold values from -0.1875 to 0.1875
- bn_scale: float32 [4, 2, 128], P('section'), may hold values from 0.5 to 2
- bn_shift: float32 [4, 2, 128], P('section'), may hold values from -3 to 3
Outputs:
- input_grad: bfloat16 [4, 2, 128, 128, 128], P('section', None, 'row', 'col')
- filter_grad: float32 [4, 2, 3, 3, 128, 128], P('section')
All inputs are finite; a program needn't handle non-finite values.
Results may differ from a plain program's by a relative error of at most 0.013.
Values may be sent and summed in bfloat16 or wider, within the bound.
No kernel may reach another device: no remote copies, remote signals or barrier semaphores. Data moves between devices by JAX's collectives and lax.ppermute only.
A program may use at most 64 MiB of HBM per device.

v0:
```python
import jax
import jax.numpy as jnp
from jax import lax
from jax.sharding import Mesh
from jax.sharding import PartitionSpec as P

ROW = ("row_0", "row_1")
COL = ("col_0", "col_1")


def padded_2(cells, sides, width):
    for axis, dim in sides:
        count = lax.axis_size(axis)
        ends = count - 1
        head = lax.slice_in_dim(cells, 0, width, axis=dim)
        tail = lax.slice_in_dim(cells, cells.shape[dim] - width, cells.shape[dim], axis=dim)
        cells = jnp.concatenate(
            [
                lax.ppermute(tail, axis, [(i, (i + 1) % count) for i in range(ends)]),
                cells,
                lax.ppermute(head, axis, [((i + 1) % count, i) for i in range(ends)]),
            ],
            axis=dim,
        )
    return cells


def from_behind(value, axis, steps):
    count = lax.axis_size(axis)
    first, last = (max(0, -steps), min(count, count - steps))
    return lax.ppermute(value, axis, [(source, source + steps) for source in range(first, last)])


def cut_along(x, dim, devices):
    before, after = (x.shape[:dim], x.shape[dim + 1 :])
    return jnp.moveaxis(x.reshape(*before, devices, -1, *after), dim, 0)


def sum_at_owner(x, axis, dim):
    devices = lax.axis_size(axis)
    blocks = lax.all_to_all(cut_along(x, dim, devices), axis, 0, 0, tiled=True)
    return jnp.sum(blocks, axis=0)


def sum_in_two_steps(x, axes, dim):
    far, near = axes
    own = sum_at_owner(cut_along(x, dim, lax.axis_size(far)), near, dim + 1)
    return jnp.sum(lax.all_to_all(own, far, 0, 0, tiled=True), axis=0)


def filled_up(lines, devices):
    spare = -lines.shape[0] % devices
    if not spare:
        return lines
    return jnp.concatenate([lines, jnp.zeros((spare, *lines.shape[1:]), lines.dtype)])


def copy_for_each(x, axis):
    devices = lax.axis_size(axis)
    return lax.all_to_all(jnp.broadcast_to(x[None], (devices, *x.shape)), axis, 0, 0, tiled=True)


def in_order(blocks, dim):
    blocks = jnp.moveaxis(blocks, 0, dim)
    shape = blocks.shape
    return blocks.reshape(*shape[:dim], shape[dim] * shape[dim + 1], *shape[dim + 2 :])


def gather_axes(x, axes, dim):
    far, near = axes
    first = copy_for_each(x, far)
    blocks = jnp.swapaxes(copy_for_each(first, near), 0, 1)
    return in_order(blocks.reshape(-1, *x.shape), dim)


def total_of(x, axes):
    lines = x.reshape(-1, x.shape[-1])
    own = sum_in_two_steps(
        filled_up(lines, lax.axis_size(axes[0]) * lax.axis_size(axes[1])), axes, 0
    )
    whole = gather_axes(own, axes, 0)
    return whole[: len(lines)].reshape(x.shape)


def correlate(padded, kernel):
    result = lax.conv_general_dilated(
        padded[None],
        kernel,
        (1, 1),
        "VALID",
        dimension_numbers=("NHWC", "HWIO", "NHWC"),
        preferred_element_type=jnp.float32,
    )
    return result[0]


def flip_kernel(kernel):
    return jnp.transpose(jnp.flip(kernel, (0, 1)), (0, 1, 3, 2))


def batched_kernel_grad(padded, gradient):
    rows_here, cols_here = (gradient.shape[1], gradient.shape[2])
    windows = jnp.stack(
        [
            padded[:, row_off : row_off + rows_here, col_off : col_off + cols_here]
            for row_off in range(3)
            for col_off in range(3)
        ]
    )
    summed = jnp.einsum("kmhwc,mhwd->kcd", windows, gradient, preferred_element_type=jnp.float32)
    return summed.reshape(3, 3, gradient.shape[3], gradient.shape[3])


def pick_micro(values, picked):
    return lax.dynamic_index_in_dim(values, picked, 0, keepdims=False)


def store_micro(buffer, value, picked, active):
    return jnp.where(active, lax.dynamic_update_index_in_dim(buffer, value, picked, 0), buffer)


def on_device(section_input, first_pre, second_pre, out_grad, kernels, bn_scale, bn_shift):
    section_index = lax.axis_index("section")
    sections = lax.axis_size("section")
    micros = out_grad.shape[0]
    rows_here, cols_here, width = (out_grad.shape[1], out_grad.shape[2], out_grad.shape[3])
    inputs_all = section_input[0]
    kernel = kernels[0]
    scales = bn_scale[0]
    shifts = bn_shift[0]
    first_norm_all = scales[0] * first_pre[0].astype(jnp.float32) + shifts[0]
    first_act_all = jnp.maximum(first_norm_all, 0.0).astype(jnp.bfloat16)
    second_norm_all = scales[1] * second_pre[0].astype(jnp.float32) + shifts[1]
    flip_first = flip_kernel(kernel[0])
    flip_second = flip_kernel(kernel[1])
    padded_inputs_all = jnp.zeros((micros, rows_here + 2, cols_here + 2, width), jnp.bfloat16)
    padded_act_all = jnp.zeros((micros, rows_here + 2, cols_here + 2, width), jnp.bfloat16)
    received = jnp.zeros(out_grad.shape[1:], jnp.bfloat16)
    outputs = jnp.zeros(out_grad.shape, jnp.bfloat16)
    first_grads = jnp.zeros(out_grad.shape, jnp.bfloat16)
    second_grads = jnp.zeros(out_grad.shape, jnp.bfloat16)
    for ticker in range(micros + sections - 1):
        micro_index = ticker - (sections - 1 - section_index)
        active = jnp.logical_and(micro_index >= 0, micro_index < micros)
        picked = jnp.clip(micro_index, 0, micros - 1)
        inputs = pick_micro(inputs_all, picked)
        first_norm = pick_micro(first_norm_all, picked)
        first_act = pick_micro(first_act_all, picked)
        second_norm = pick_micro(second_norm_all, picked)
        incoming = jnp.where(section_index == sections - 1, pick_micro(out_grad, picked), received)
        masked = jnp.where(
            second_norm + inputs.astype(jnp.float32) > 0, incoming.astype(jnp.float32), 0.0
        )
        second_grad = (scales[1] * masked).astype(jnp.bfloat16)
        stacked = padded_2(jnp.stack([first_act, second_grad]), ((ROW, 1), (COL, 2)), 1)
        pad_second = stacked[1]
        padded_act_all = store_micro(padded_act_all, stacked[0], picked, active)
        act_grad = correlate(pad_second, flip_second)
        first_grad = (scales[0] * jnp.where(first_norm > 0, act_grad, 0.0)).astype(jnp.bfloat16)
        stacked_in = padded_2(jnp.stack([inputs, first_grad]), ((ROW, 1), (COL, 2)), 1)
        pad_first = stacked_in[1]
        padded_inputs_all = store_micro(padded_inputs_all, stacked_in[0], picked, active)
        input_grad = (masked + correlate(pad_first, flip_first)).astype(jnp.bfloat16)
        first_grads = store_micro(first_grads, first_grad, picked, active)
        second_grads = store_micro(second_grads, second_grad, picked, active)
        outputs = store_micro(outputs, input_grad, picked, active)
        if ticker + 2 < micros + sections:
            received = from_behind(input_grad, "section", -1)
    filter_acc = jnp.stack(
        [
            batched_kernel_grad(padded_inputs_all, first_grads),
            batched_kernel_grad(padded_act_all, second_grads),
        ]
    )
    pixels = micros * rows_here * lax.axis_size(ROW) * cols_here * lax.axis_size(COL)
    factor = 1.0 / jnp.sqrt(jnp.float32(pixels))
    summed = total_of(filter_acc, (("row_0", "row_1", "col_0"), "col_1"))
    return (outputs[None], (summed * factor)[None])


def solution(mesh):
    split = Mesh(
        mesh.devices.reshape(mesh.shape["section"], 8, 2, 2, 4),
        ("section", "row_0", "row_1", "col_0", "col_1"),
    )
    in_specs = (
        P("section", None, ROW, COL, None),
        P("section", None, ROW, COL, None),
        P("section", None, ROW, COL, None),
        P(None, ROW, COL, None),
        P("section", None, None, None, None, None),
        P("section", None, None),
        P("section", None, None),
    )
    out_specs = (P("section", None, ROW, COL, None), P("section", None, None, None, None, None))
    return jax.shard_map(
        on_device, mesh=split, in_specs=in_specs, out_specs=out_specs, check_vma=False
    )
```

profile of v0, /device:TPU:1, one launch (start us, length us, event | category | flops | bytes accessed | tf_op | source)
XLA Modules:
  0.0 350.1 jit_solution(8105211868701949614)
XLA Ops:
  4.8 5.4 %collective-permute-start = (bf16[2,1,16,128]{3,2,0,1:T(8,128)(2,1)S(1)}, bf16[2,1,16,128]{3,2,0,1:T(8,128)(2,1)S(1)}, u32[]{:S(2)}, u32[]{:S(2)}) collective-permute-start(bf16[2,1,16,128]{3,2,0,1:T(8,128)(2,1)S(1)} %get-tuple-element.93), channel_id=1, source_target_pairs={{0,8},{8,16},{16,24},{24,32},{32,40},{40,48},{48,56},{56,64},{64,7... | collective-permute-start | bytes 24584 | tf_op jit(solution)/shard_map/ppermute | solution.py:19
  10.2 4.7 %collective-permute-start.1 = (bf16[2,1,16,128]{3,2,0,1:T(8,128)(2,1)S(1)}, bf16[2,1,16,128]{3,2,0,1:T(8,128)(2,1)S(1)}, u32[]{:S(2)}, u32[]{:S(2)}) collective-permute-start(bf16[2,1,16,128]{3,2,0,1:T(8,128)(2,1)S(1)} %get-tuple-element.94), channel_id=1, source_target_pairs={{8,0},{16,8},{24,16},{32,24},{40,32},{48,40},{56,48},{64,56},{72,6... | collective-permute-start | bytes 24584 | tf_op jit(solution)/shard_map/ppermute | solution.py:21
  23.4 3.6 %collective-permute-start.4 = (bf16[2,1,16,128]{3,2,0,1:T(8,128)(2,1)S(1)}, bf16[2,1,16,128]{3,2,0,1:T(8,128)(2,1)S(1)}, u32[]{:S(2)}, u32[]{:S(2)}) collective-permute-start(bf16[2,1,16,128]{3,2,0,1:T(8,128)(2,1)S(1)} %get-tuple-element.91), channel_id=1, source_target_pairs={{0,8},{8,16},{16,24},{24,32},{32,40},{40,48},{48,56},{56,64},{64,7... | collective-permute-start | bytes 24584 | tf_op jit(solution)/shard_map/ppermute | solution.py:19
  36.4 6.3 %collective-permute-done.7 = bf16[2,10,1,128]{3,2,0,1:T(2,128)(2,1)S(1)} collective-permute-done((bf16[2,10,1,128]{3,2,0,1:T(2,128)(2,1)S(1)}, bf16[2,10,1,128]{3,2,0,1:T(2,128)(2,1)S(1)}, u32[]{:S(2)}, u32[]{:S(2)}) %collective-permute-start.7) | collective-permute-done | bytes 5152 | tf_op jit(solution)/shard_map/ppermute | solution.py:21
  44.6 3.4 collective-permute-done.8
  48.1 4.3 %collective-permute-start.9 = (bf16[2,1,16,128]{3,2,1,0:T(8,128)(2,1)S(1)}, bf16[2,1,16,128]{3,2,1,0:T(8,128)(2,1)S(1)}, u32[]{:S(2)}, u32[]{:S(2)}) collective-permute-start(bf16[2,1,16,128]{3,2,1,0:T(8,128)(2,1)S(1)} %get-tuple-element.89), channel_id=1, source_target_pairs={{0,8},{8,16},{16,24},{24,32},{32,40},{40,48},{48,56},{56,64},{64,7... | collective-permute-start | bytes 24584 | tf_op jit(solution)/shard_map/ppermute | solution.py:19
  57.4 9.7 %collective-permute-start.11 = (bf16[2,10,1,128]{3,2,1,0:T(2,128)(2,1)S(1)}, bf16[2,10,1,128]{3,2,1,0:T(2,128)(2,1)S(1)}, u32[]{:S(2)}, u32[]{:S(2)}) collective-permute-start(bf16[2,10,1,128]{3,2,1,0:T(2,128)(2,1)S(1)} %get-tuple-element.57), channel_id=1, source_target_pairs={{0,1},{1,2},{2,3},{3,4},{4,5},{5,6},{6,7},{8,9},{9,10},{10,11},{11... | collective-permute-start | bytes 15368 | tf_op jit(solution)/shard_map/ppermute | solution.py:19
  68.5 3.6 %collective-permute-done.12 = bf16[2,10,1,128]{3,2,1,0:T(2,128)(2,1)S(1)} collective-permute-done((bf16[2,10,1,128]{3,2,1,0:T(2,128)(2,1)S(1)}, bf16[2,10,1,128]{3,2,1,0:T(2,128)(2,1)S(1)}, u32[]{:S(2)}, u32[]{:S(2)}) %collective-permute-start.12) | collective-permute-done | bytes 5152 | tf_op jit(solution)/shard_map/ppermute | solution.py:21
  72.7 4.0 %collective-permute-start.13 = (bf16[2,1,16,128]{3,2,1,0:T(8,128)(2,1)S(1)}, bf16[2,1,16,128]{3,2,1,0:T(8,128)(2,1)S(1)}, u32[]{:S(2)}, u32[]{:S(2)}) collective-permute-start(bf16[2,1,16,128]{3,2,1,0:T(8,128)(2,1)S(1)} %get-tuple-element.87), channel_id=1, source_target_pairs={{0,8},{8,16},{16,24},{24,32},{32,40},{40,48},{48,56},{56,64},{64,7... | collective-permute-start | bytes 24584 | tf_op jit(solution)/shard_map/ppermute | solution.py:19
  81.7 7.7 %collective-permute-start.15 = (bf16[2,10,1,128]{3,2,1,0:T(2,128)(2,1)S(1)}, bf16[2,10,1,128]{3,2,1,0:T(2,128)(2,1)S(1)}, u32[]{:S(2)}, u32[]{:S(2)}) collective-permute-start(bf16[2,10,1,128]{3,2,1,0:T(2,128)(2,1)S(1)} %get-tuple-element.55), channel_id=1, source_target_pairs={{0,1},{1,2},{2,3},{3,4},{4,5},{5,6},{6,7},{8,9},{9,10},{10,11},{11... | collective-permute-start | bytes 15368 | tf_op jit(solution)/shard_map/ppermute | solution.py:19
  95.9 3.4 collective-permute-done.17
  99.4 5.4 %collective-permute-start.18 = (bf16[2,1,16,128]{3,2,1,0:T(8,128)(2,1)S(1)}, bf16[2,1,16,128]{3,2,1,0:T(8,128)(2,1)S(1)}, u32[]{:S(2)}, u32[]{:S(2)}) collective-permute-start(bf16[2,1,16,128]{3,2,1,0:T(8,128)(2,1)S(1)} %get-tuple-element.85), channel_id=1, source_target_pairs={{0,8},{8,16},{16,24},{24,32},{32,40},{40,48},{48,56},{56,64},{64,7... | collective-permute-start | bytes 24584 | tf_op jit(solution)/shard_map/ppermute | solution.py:19
  109.9 7.7 %collective-permute-start.20 = (bf16[2,10,1,128]{3,2,1,0:T(2,128)(2,1)S(1)}, bf16[2,10,1,128]{3,2,1,0:T(2,128)(2,1)S(1)}, u32[]{:S(2)}, u32[]{:S(2)}) collective-permute-start(bf16[2,10,1,128]{3,2,1,0:T(2,128)(2,1)S(1)} %get-tuple-element.53), channel_id=1, source_target_pairs={{0,1},{1,2},{2,3},{3,4},{4,5},{5,6},{6,7},{8,9},{9,10},{10,11},{11... | collective-permute-start | bytes 15368 | tf_op jit(solution)/shard_map/ppermute | solution.py:19
  118.8 3.7 %collective-permute-done.21 = bf16[2,10,1,128]{3,2,1,0:T(2,128)(2,1)S(1)} collective-permute-done((bf16[2,10,1,128]{3,2,1,0:T(2,128)(2,1)S(1)}, bf16[2,10,1,128]{3,2,1,0:T(2,128)(2,1)S(1)}, u32[]{:S(2)}, u32[]{:S(2)}) %collective-permute-start.21) | collective-permute-done | bytes 5152 | tf_op jit(solution)/shard_map/ppermute | solution.py:21
  123.1 4.0 %collective-permute-start.22 = (bf16[2,1,16,128]{3,2,1,0:T(8,128)(2,1)S(1)}, bf16[2,1,16,128]{3,2,1,0:T(8,128)(2,1)S(1)}, u32[]{:S(2)}, u32[]{:S(2)}) collective-permute-start(bf16[2,1,16,128]{3,2,1,0:T(8,128)(2,1)S(1)} %get-tuple-element.83), channel_id=1, source_target_pairs={{0,8},{8,16},{16,24},{24,32},{32,40},{40,48},{48,56},{56,64},{64,7... | collective-permute-start | bytes 24584 | tf_op jit(solution)/shard_map/ppermute | solution.py:19
  132.0 7.7 %collective-permute-start.24 = (bf16[2,10,1,128]{3,2,1,0:T(2,128)(2,1)S(1)}, bf16[2,10,1,128]{3,2,1,0:T(2,128)(2,1)S(1)}, u32[]{:S(2)}, u32[]{:S(2)}) collective-permute-start(bf16[2,10,1,128]{3,2,1,0:T(2,128)(2,1)S(1)} %get-tuple-element.51), channel_id=1, source_target_pairs={{0,1},{1,2},{2,3},{3,4},{4,5},{5,6},{6,7},{8,9},{9,10},{10,11},{11... | collective-permute-start | bytes 15368 | tf_op jit(solution)/shard_map/ppermute | solution.py:19
  146.3 3.4 collective-permute-done.26
  149.8 5.4 %collective-permute-start.27 = (bf16[2,1,16,128]{3,2,1,0:T(8,128)(2,1)S(1)}, bf16[2,1,16,128]{3,2,1,0:T(8,128)(2,1)S(1)}, u32[]{:S(2)}, u32[]{:S(2)}) collective-permute-start(bf16[2,1,16,128]{3,2,1,0:T(8,128)(2,1)S(1)} %get-tuple-element.81), channel_id=1, source_target_pairs={{0,8},{8,16},{16,24},{24,32},{32,40},{40,48},{48,56},{56,64},{64,7... | collective-permute-start | bytes 24584 | tf_op jit(solution)/shard_map/ppermute | solution.py:19
  160.2 7.7 %collective-permute-start.29 = (bf16[2,10,1,128]{3,2,1,0:T(2,128)(2,1)S(1)}, bf16[2,10,1,128]{3,2,1,0:T(2,128)(2,1)S(1)}, u32[]{:S(2)}, u32[]{:S(2)}) collective-permute-start(bf16[2,10,1,128]{3,2,1,0:T(2,128)(2,1)S(1)} %get-tuple-element.49), channel_id=1, source_target_pairs={{0,1},{1,2},{2,3},{3,4},{4,5},{5,6},{6,7},{8,9},{9,10},{10,11},{11... | collective-permute-start | bytes 15368 | tf_op jit(solution)/shard_map/ppermute | solution.py:19
  169.2 3.7 %collective-permute-done.30 = bf16[2,10,1,128]{3,2,1,0:T(2,128)(2,1)S(1)} collective-permute-done((bf16[2,10,1,128]{3,2,1,0:T(2,128)(2,1)S(1)}, bf16[2,10,1,128]{3,2,1,0:T(2,128)(2,1)S(1)}, u32[]{:S(2)}, u32[]{:S(2)}) %collective-permute-start.30) | collective-permute-done | bytes 5152 | tf_op jit(solution)/shard_map/ppermute | solution.py:21
  173.5 4.0 %collective-permute-start.31 = (bf16[2,1,16,128]{3,2,1,0:T(8,128)(2,1)S(1)}, bf16[2,1,16,128]{3,2,1,0:T(8,128)(2,1)S(1)}, u32[]{:S(2)}, u32[]{:S(2)}) collective-permute-start(bf16[2,1,16,128]{3,2,1,0:T(8,128)(2,1)S(1)} %get-tuple-element.79), channel_id=1, source_target_pairs={{0,8},{8,16},{16,24},{24,32},{32,40},{40,48},{48,56},{56,64},{64,7... | collective-permute-start | bytes 24584 | tf_op jit(solution)/shard_map/ppermute | solution.py:19
  182.4 7.7 %collective-permute-start.33 = (bf16[2,10,1,128]{3,2,1,0:T(2,128)(2,1)S(1)}, bf16[2,10,1,128]{3,2,1,0:T(2,128)(2,1)S(1)}, u32[]{:S(2)}, u32[]{:S(2)}) collective-permute-start(bf16[2,10,1,128]{3,2,1,0:T(2,128)(2,1)S(1)} %get-tuple-element.47), channel_id=1, source_target_pairs={{0,1},{1,2},{2,3},{3,4},{4,5},{5,6},{6,7},{8,9},{9,10},{10,11},{11... | collective-permute-start | bytes 15368 | tf_op jit(solution)/shard_map/ppermute | solution.py:19
  200.2 5.4 %collective-permute-start.36 = (bf16[2,1,16,128]{3,2,1,0:T(8,128)(2,1)S(1)}, bf16[2,1,16,128]{3,2,1,0:T(8,128)(2,1)S(1)}, u32[]{:S(2)}, u32[]{:S(2)}) collective-permute-start(bf16[2,1,16,128]{3,2,1,0:T(8,128)(2,1)S(1)} %get-tuple-element.72), channel_id=1, source_target_pairs={{0,8},{8,16},{16,24},{24,32},{32,40},{40,48},{48,56},{56,64},{64,7... | collective-permute-start | bytes 24584 | tf_op jit(solution)/shard_map/ppermute | solution.py:19
  210.6 7.7 %collective-permute-start.38 = (bf16[2,10,1,128]{3,2,1,0:T(2,128)(2,1)S(1)}, bf16[2,10,1,128]{3,2,1,0:T(2,128)(2,1)S(1)}, u32[]{:S(2)}, u32[]{:S(2)}) collective-permute-start(bf16[2,10,1,128]{3,2,1,0:T(2,128)(2,1)S(1)} %get-tuple-element.45), channel_id=1, source_target_pairs={{0,1},{1,2},{2,3},{3,4},{4,5},{5,6},{6,7},{8,9},{9,10},{10,11},{11... | collective-permute-start | bytes 15368 | tf_op jit(solution)/shard_map/ppermute | solution.py:19
  219.6 3.6 %collective-permute-done.39 = bf16[2,10,1,128]{3,2,1,0:T(2,128)(2,1)S(1)} collective-permute-done((bf16[2,10,1,128]{3,2,1,0:T(2,128)(2,1)S(1)}, bf16[2,10,1,128]{3,2,1,0:T(2,128)(2,1)S(1)}, u32[]{:S(2)}, u32[]{:S(2)}) %collective-permute-start.39) | collective-permute-done | bytes 5152 | tf_op jit(solution)/shard_map/ppermute | solution.py:21
  223.8 4.0 %collective-permute-start.40 = (bf16[2,1,16,128]{3,2,1,0:T(8,128)(2,1)S(1)}, bf16[2,1,16,128]{3,2,1,0:T(8,128)(2,1)S(1)}, u32[]{:S(2)}, u32[]{:S(2)}) collective-permute-start(bf16[2,1,16,128]{3,2,1,0:T(8,128)(2,1)S(1)} %get-tuple-element.65), channel_id=1, source_target_pairs={{0,8},{8,16},{16,24},{24,32},{32,40},{40,48},{48,56},{56,64},{64,7... | collective-permute-start | bytes 24584 | tf_op jit(solution)/shard_map/ppermute | solution.py:19
  232.8 7.7 %collective-permute-start.42 = (bf16[2,10,1,128]{3,2,1,0:T(2,128)(2,1)S(1)}, bf16[2,10,1,128]{3,2,1,0:T(2,128)(2,1)S(1)}, u32[]{:S(2)}, u32[]{:S(2)}) collective-permute-start(bf16[2,10,1,128]{3,2,1,0:T(2,128)(2,1)S(1)} %get-tuple-element.43), channel_id=1, source_target_pairs={{0,1},{1,2},{2,3},{3,4},{4,5},{5,6},{6,7},{8,9},{9,10},{10,11},{11... | collective-permute-start | bytes 15368 | tf_op jit(solution)/shard_map/ppermute | solution.py:19
  246.8 30.5 %all_to_all.20 = f32[4,32,18,128]{3,1,2,0:T(8,128)S(1)} all-to-all(f32[4,32,18,128]{3,1,2,0:T(8,128)S(1)} %copy.310), channel_id=1, replica_groups=mesh['section'=4,'row_0'=8,'row_1'=2,'col_0'=2,'col_1'=4] {'col_1'}, dimensions={0} | all-to-all | bytes 2359296 | tf_op jit(solution)/shard_map/all_to_all | solution.py:41
  277.6 26.6 %all_to_all.21 = f32[32,18,128]{2,1,0:T(8,128)S(1)} all-to-all(f32[32,18,128]{2,1,0:T(8,128)S(1)} %copy.311), channel_id=1, replica_groups=mesh['section'=4,'row_0'=8,'row_1'=2,'col_0'=2,'col_1'=4] {'row_0','row_..., dimensions={0} | all-to-all | bytes 589824 | tf_op jit(solution)/shard_map/all_to_all | solution.py:48
  304.3 21.9 %all_to_all.22 = f32[32,18,128]{2,1,0:T(8,128)S(1)} all-to-all(f32[32,18,128]{2,1,0:T(8,128)S(1)} %broadcast_in_dim.74), channel_id=1, replica_groups=mesh['section'=4,'row_0'=8,'row_1'=2,'col_0'=2,'col_1'=4] {'row_0','row_..., dimensions={0} | all-to-all | bytes 589824 | tf_op jit(solution)/shard_map/all_to_all | solution.py:60
  327.4 3.7 %all-to-all-start.3 = ((f32[4,32,18,128]{3,1,2,0:T(8,128)}), f32[4,32,18,128]{3,1,2,0:T(8,128)S(1)}, u32[]{:S(2)}, u32[]{:S(2)}) async-start(f32[4,32,18,128]{3,1,2,0:T(8,128)} %broadcast_in_dim.75), calls=%async_computation.3 | async-start | bytes 2359296 | tf_op jit(solution)/shard_map/all_to_all | solution.py:60
  331.7 16.4 %all-to-all-done.3 = f32[4,32,18,128]{3,1,2,0:T(8,128)S(1)} async-done(((f32[4,32,18,128]{3,1,2,0:T(8,128)}), f32[4,32,18,128]{3,1,2,0:T(8,128)S(1)}, u32[]{:S(2)}, u32[]{:S(2)}) %all-to-all-start.3) | async-done | bytes 1179680 | tf_op jit(solution)/shard_map/all_to_all | solution.py:60
  (246 shorter events, 104.2 us)
Async XLA Ops:
  4.8 10.1 %collective-permute-start = (bf16[2,1,16,128]{3,2,0,1:T(8,128)(2,1)S(1)}, bf16[2,1,16,128]{3,2,0,1:T(8,128)(2,1)S(1)}, u32[]{:S(2)}, u32[]{:S(2)}) collective-permute-start(bf16[2,1,16,128]{3,2,0,1:T(8,128)(2,1)S(1)} %get-tuple-element.93), channel_id=1, source_target_pairs={{0,8},{8,16},{16,24},{24,32},{32,40},{40,48},{48,56},{56,64},{64,7... | collective-permute-start | bytes 24584 | tf_op jit(solution)/shard_map/ppermute | solution.py:19
  10.2 5.5 %collective-permute-start.1 = (bf16[2,1,16,128]{3,2,0,1:T(8,128)(2,1)S(1)}, bf16[2,1,16,128]{3,2,0,1:T(8,128)(2,1)S(1)}, u32[]{:S(2)}, u32[]{:S(2)}) collective-permute-start(bf16[2,1,16,128]{3,2,0,1:T(8,128)(2,1)S(1)} %get-tuple-element.94), channel_id=1, source_target_pairs={{8,0},{16,8},{24,16},{32,24},{40,32},{48,40},{56,48},{64,56},{72,6... | collective-permute-start | bytes 24584 | tf_op jit(solution)/shard_map/ppermute | solution.py:21
  23.4 5.5 %collective-permute-start.4 = (bf16[2,1,16,128]{3,2,0,1:T(8,128)(2,1)S(1)}, bf16[2,1,16,128]{3,2,0,1:T(8,128)(2,1)S(1)}, u32[]{:S(2)}, u32[]{:S(2)}) collective-permute-start(bf16[2,1,16,128]{3,2,0,1:T(8,128)(2,1)S(1)} %get-tuple-element.91), channel_id=1, source_target_pairs={{0,8},{8,16},{16,24},{24,32},{32,40},{40,48},{48,56},{56,64},{64,7... | collective-permute-start | bytes 24584 | tf_op jit(solution)/shard_map/ppermute | solution.py:19
  26.9 5.0 %collective-permute-start.5 = (bf16[2,1,16,128]{3,2,0,1:T(8,128)(2,1)S(1)}, bf16[2,1,16,128]{3,2,0,1:T(8,128)(2,1)S(1)}, u32[]{:S(2)}, u32[]{:S(2)}) collective-permute-start(bf16[2,1,16,128]{3,2,0,1:T(8,128)(2,1)S(1)} %get-tuple-element.92), channel_id=1, source_target_pairs={{8,0},{16,8},{24,16},{32,24},{40,32},{48,40},{56,48},{64,56},{72,6... | collective-permute-start | bytes 24584 | tf_op jit(solution)/shard_map/ppermute | solution.py:21
  35.1 7.6 %collective-permute-start.7 = (bf16[2,10,1,128]{3,2,0,1:T(2,128)(2,1)S(1)}, bf16[2,10,1,128]{3,2,0,1:T(2,128)(2,1)S(1)}, u32[]{:S(2)}, u32[]{:S(2)}) collective-permute-start(bf16[2,10,1,128]{3,2,0,1:T(2,128)(2,1)S(1)} %get-tuple-element.60), channel_id=1, source_target_pairs={{1,0},{2,1},{3,2},{4,3},{5,4},{6,5},{7,6},{9,8},{10,9},{11,10},{12... | collective-permute-start | bytes 15368 | tf_op jit(solution)/shard_map/ppermute | solution.py:21
  48.1 6.2 %collective-permute-start.9 = (bf16[2,1,16,128]{3,2,1,0:T(8,128)(2,1)S(1)}, bf16[2,1,16,128]{3,2,1,0:T(8,128)(2,1)S(1)}, u32[]{:S(2)}, u32[]{:S(2)}) collective-permute-start(bf16[2,1,16,128]{3,2,1,0:T(8,128)(2,1)S(1)} %get-tuple-element.89), channel_id=1, source_target_pairs={{0,8},{8,16},{16,24},{24,32},{32,40},{40,48},{48,56},{56,64},{64,7... | collective-permute-start | bytes 24584 | tf_op jit(solution)/shard_map/ppermute | solution.py:19
  52.4 5.0 %collective-permute-start.10 = (bf16[2,1,16,128]{3,2,1,0:T(8,128)(2,1)S(1)}, bf16[2,1,16,128]{3,2,1,0:T(8,128)(2,1)S(1)}, u32[]{:S(2)}, u32[]{:S(2)}) collective-permute-start(bf16[2,1,16,128]{3,2,1,0:T(8,128)(2,1)S(1)} %get-tuple-element.90), channel_id=1, source_target_pairs={{8,0},{16,8},{24,16},{32,24},{40,32},{48,40},{56,48},{64,56},{72,6... | collective-permute-start | bytes 24584 | tf_op jit(solution)/shard_map/ppermute | solution.py:21
  57.4 11.0 %collective-permute-start.11 = (bf16[2,10,1,128]{3,2,1,0:T(2,128)(2,1)S(1)}, bf16[2,10,1,128]{3,2,1,0:T(2,128)(2,1)S(1)}, u32[]{:S(2)}, u32[]{:S(2)}) collective-permute-start(bf16[2,10,1,128]{3,2,1,0:T(2,128)(2,1)S(1)} %get-tuple-element.57), channel_id=1, source_target_pairs={{0,1},{1,2},{2,3},{3,4},{4,5},{5,6},{6,7},{8,9},{9,10},{10,11},{11... | collective-permute-start | bytes 15368 | tf_op jit(solution)/shard_map/ppermute | solution.py:19
  67.1 5.0 %collective-permute-start.12 = (bf16[2,10,1,128]{3,2,1,0:T(2,128)(2,1)S(1)}, bf16[2,10,1,128]{3,2,1,0:T(2,128)(2,1)S(1)}, u32[]{:S(2)}, u32[]{:S(2)}) collective-permute-start(bf16[2,10,1,128]{3,2,1,0:T(2,128)(2,1)S(1)} %get-tuple-element.58), channel_id=1, source_target_pairs={{1,0},{2,1},{3,2},{4,3},{5,4},{6,5},{7,6},{9,8},{10,9},{11,10},{12... | collective-permute-start | bytes 15368 | tf_op jit(solution)/shard_map/ppermute | solution.py:21
  72.7 5.9 %collective-permute-start.13 = (bf16[2,1,16,128]{3,2,1,0:T(8,128)(2,1)S(1)}, bf16[2,1,16,128]{3,2,1,0:T(8,128)(2,1)S(1)}, u32[]{:S(2)}, u32[]{:S(2)}) collective-permute-start(bf16[2,1,16,128]{3,2,1,0:T(8,128)(2,1)S(1)} %get-tuple-element.87), channel_id=1, source_target_pairs={{0,8},{8,16},{16,24},{24,32},{32,40},{40,48},{48,56},{56,64},{64,7... | collective-permute-start | bytes 24584 | tf_op jit(solution)/shard_map/ppermute | solution.py:19
  76.7 5.0 %collective-permute-start.14 = (bf16[2,1,16,128]{3,2,1,0:T(8,128)(2,1)S(1)}, bf16[2,1,16,128]{3,2,1,0:T(8,128)(2,1)S(1)}, u32[]{:S(2)}, u32[]{:S(2)}) collective-permute-start(bf16[2,1,16,128]{3,2,1,0:T(8,128)(2,1)S(1)} %get-tuple-element.88), channel_id=1, source_target_pairs={{8,0},{16,8},{24,16},{32,24},{40,32},{48,40},{56,48},{64,56},{72,6... | collective-permute-start | bytes 24584 | tf_op jit(solution)/shard_map/ppermute | solution.py:21
  81.7 9.0 %collective-permute-start.15 = (bf16[2,10,1,128]{3,2,1,0:T(2,128)(2,1)S(1)}, bf16[2,10,1,128]{3,2,1,0:T(2,128)(2,1)S(1)}, u32[]{:S(2)}, u32[]{:S(2)}) collective-permute-start(bf16[2,10,1,128]{3,2,1,0:T(2,128)(2,1)S(1)} %get-tuple-element.55), channel_id=1, source_target_pairs={{0,1},{1,2},{2,3},{3,4},{4,5},{5,6},{6,7},{8,9},{9,10},{10,11},{11... | collective-permute-start | bytes 15368 | tf_op jit(solution)/shard_map/ppermute | solution.py:19
  99.4 7.4 %collective-permute-start.18 = (bf16[2,1,16,128]{3,2,1,0:T(8,128)(2,1)S(1)}, bf16[2,1,16,128]{3,2,1,0:T(8,128)(2,1)S(1)}, u32[]{:S(2)}, u32[]{:S(2)}) collective-permute-start(bf16[2,1,16,128]{3,2,1,0:T(8,128)(2,1)S(1)} %get-tuple-element.85), channel_id=1, source_target_pairs={{0,8},{8,16},{16,24},{24,32},{32,40},{40,48},{48,56},{56,64},{64,7... | collective-permute-start | bytes 24584 | tf_op jit(solution)/shard_map/ppermute | solution.py:19
  104.9 5.0 %collective-permute-start.19 = (bf16[2,1,16,128]{3,2,1,0:T(8,128)(2,1)S(1)}, bf16[2,1,16,128]{3,2,1,0:T(8,128)(2,1)S(1)}, u32[]{:S(2)}, u32[]{:S(2)}) collective-permute-start(bf16[2,1,16,128]{3,2,1,0:T(8,128)(2,1)S(1)} %get-tuple-element.86), channel_id=1, source_target_pairs={{8,0},{16,8},{24,16},{32,24},{40,32},{48,40},{56,48},{64,56},{72,6... | collective-permute-start | bytes 24584 | tf_op jit(solution)/shard_map/ppermute | solution.py:21
  109.9 9.0 %collective-permute-start.20 = (bf16[2,10,1,128]{3,2,1,0:T(2,128)(2,1)S(1)}, bf16[2,10,1,128]{3,2,1,0:T(2,128)(2,1)S(1)}, u32[]{:S(2)}, u32[]{:S(2)}) collective-permute-start(bf16[2,10,1,128]{3,2,1,0:T(2,128)(2,1)S(1)} %get-tuple-element.53), channel_id=1, source_target_pairs={{0,1},{1,2},{2,3},{3,4},{4,5},{5,6},{6,7},{8,9},{9,10},{10,11},{11... | collective-permute-start | bytes 15368 | tf_op jit(solution)/shard_map/ppermute | solution.py:19
  117.5 5.0 %collective-permute-start.21 = (bf16[2,10,1,128]{3,2,1,0:T(2,128)(2,1)S(1)}, bf16[2,10,1,128]{3,2,1,0:T(2,128)(2,1)S(1)}, u32[]{:S(2)}, u32[]{:S(2)}) collective-permute-start(bf16[2,10,1,128]{3,2,1,0:T(2,128)(2,1)S(1)} %get-tuple-element.54), channel_id=1, source_target_pairs={{1,0},{2,1},{3,2},{4,3},{5,4},{6,5},{7,6},{9,8},{10,9},{11,10},{12... | collective-permute-start | bytes 15368 | tf_op jit(solution)/shard_map/ppermute | solution.py:21
  123.1 5.9 %collective-permute-start.22 = (bf16[2,1,16,128]{3,2,1,0:T(8,128)(2,1)S(1)}, bf16[2,1,16,128]{3,2,1,0:T(8,128)(2,1)S(1)}, u32[]{:S(2)}, u32[]{:S(2)}) collective-permute-start(bf16[2,1,16,128]{3,2,1,0:T(8,128)(2,1)S(1)} %get-tuple-element.83), channel_id=1, source_target_pairs={{0,8},{8,16},{16,24},{24,32},{32,40},{40,48},{48,56},{56,64},{64,7... | collective-permute-start | bytes 24584 | tf_op jit(solution)/shard_map/ppermute | solution.py:19
  127.1 5.0 %collective-permute-start.23 = (bf16[2,1,16,128]{3,2,1,0:T(8,128)(2,1)S(1)}, bf16[2,1,16,128]{3,2,1,0:T(8,128)(2,1)S(1)}, u32[]{:S(2)}, u32[]{:S(2)}) collective-permute-start(bf16[2,1,16,128]{3,2,1,0:T(8,128)(2,1)S(1)} %get-tuple-element.84), channel_id=1, source_target_pairs={{8,0},{16,8},{24,16},{32,24},{40,32},{48,40},{56,48},{64,56},{72,6... | collective-permute-start | bytes 24584 | tf_op jit(solution)/shard_map/ppermute | solution.py:21
  132.0 9.0 %collective-permute-start.24 = (bf16[2,10,1,128]{3,2,1,0:T(2,128)(2,1)S(1)}, bf16[2,10,1,128]{3,2,1,0:T(2,128)(2,1)S(1)}, u32[]{:S(2)}, u32[]{:S(2)}) collective-permute-start(bf16[2,10,1,128]{3,2,1,0:T(2,128)(2,1)S(1)} %get-tuple-element.51), channel_id=1, source_target_pairs={{0,1},{1,2},{2,3},{3,4},{4,5},{5,6},{6,7},{8,9},{9,10},{10,11},{11... | collective-permute-start | bytes 15368 | tf_op jit(solution)/shard_map/ppermute | solution.py:19
  149.8 7.4 %collective-permute-start.27 = (bf16[2,1,16,128]{3,2,1,0:T(8,128)(2,1)S(1)}, bf16[2,1,16,128]{3,2,1,0:T(8,128)(2,1)S(1)}, u32[]{:S(2)}, u32[]{:S(2)}) collective-permute-start(bf16[2,1,16,128]{3,2,1,0:T(8,128)(2,1)S(1)} %get-tuple-element.81), channel_id=1, source_target_pairs={{0,8},{8,16},{16,24},{24,32},{32,40},{40,48},{48,56},{56,64},{64,7... | collective-permute-start | bytes 24584 | tf_op jit(solution)/shard_map/ppermute | solution.py:19
  155.2 5.0 %collective-permute-start.28 = (bf16[2,1,16,128]{3,2,1,0:T(8,128)(2,1)S(1)}, bf16[2,1,16,128]{3,2,1,0:T(8,128)(2,1)S(1)}, u32[]{:S(2)}, u32[]{:S(2)}) collective-permute-start(bf16[2,1,16,128]{3,2,1,0:T(8,128)(2,1)S(1)} %get-tuple-element.82), channel_id=1, source_target_pairs={{8,0},{16,8},{24,16},{32,24},{40,32},{48,40},{56,48},{64,56},{72,6... | collective-permute-start | bytes 24584 | tf_op jit(solution)/shard_map/ppermute | solution.py:21
  160.2 9.0 %collective-permute-start.29 = (bf16[2,10,1,128]{3,2,1,0:T(2,128)(2,1)S(1)}, bf16[2,10,1,128]{3,2,1,0:T(2,128)(2,1)S(1)}, u32[]{:S(2)}, u32[]{:S(2)}) collective-permute-start(bf16[2,10,1,128]{3,2,1,0:T(2,128)(2,1)S(1)} %get-tuple-element.49), channel_id=1, source_target_pairs={{0,1},{1,2},{2,3},{3,4},{4,5},{5,6},{6,7},{8,9},{9,10},{10,11},{11... | collective-permute-start | bytes 15368 | tf_op jit(solution)/shard_map/ppermute | solution.py:19
  167.9 5.0 %collective-permute-start.30 = (bf16[2,10,1,128]{3,2,1,0:T(2,128)(2,1)S(1)}, bf16[2,10,1,128]{3,2,1,0:T(2,128)(2,1)S(1)}, u32[]{:S(2)}, u32[]{:S(2)}) collective-permute-start(bf16[2,10,1,128]{3,2,1,0:T(2,128)(2,1)S(1)} %get-tuple-element.50), channel_id=1, source_target_pairs={{1,0},{2,1},{3,2},{4,3},{5,4},{6,5},{7,6},{9,8},{10,9},{11,10},{12... | collective-permute-start | bytes 15368 | tf_op jit(solution)/shard_map/ppermute | solution.py:21
  173.5 5.9 %collective-permute-start.31 = (bf16[2,1,16,128]{3,2,1,0:T(8,128)(2,1)S(1)}, bf16[2,1,16,128]{3,2,1,0:T(8,128)(2,1)S(1)}, u32[]{:S(2)}, u32[]{:S(2)}) collective-permute-start(bf16[2,1,16,128]{3,2,1,0:T(8,128)(2,1)S(1)} %get-tuple-element.79), channel_id=1, source_target_pairs={{0,8},{8,16},{16,24},{24,32},{32,40},{40,48},{48,56},{56,64},{64,7... | collective-permute-start | bytes 24584 | tf_op jit(solution)/shard_map/ppermute | solution.py:19
  177.4 5.0 %collective-permute-start.32 = (bf16[2,1,16,128]{3,2,1,0:T(8,128)(2,1)S(1)}, bf16[2,1,16,128]{3,2,1,0:T(8,128)(2,1)S(1)}, u32[]{:S(2)}, u32[]{:S(2)}) collective-permute-start(bf16[2,1,16,128]{3,2,1,0:T(8,128)(2,1)S(1)} %get-tuple-element.80), channel_id=1, source_target_pairs={{8,0},{16,8},{24,16},{32,24},{40,32},{48,40},{56,48},{64,56},{72,6... | collective-permute-start | bytes 24584 | tf_op jit(solution)/shard_map/ppermute | solution.py:21
  182.4 9.0 %collective-permute-start.33 = (bf16[2,10,1,128]{3,2,1,0:T(2,128)(2,1)S(1)}, bf16[2,10,1,128]{3,2,1,0:T(2,128)(2,1)S(1)}, u32[]{:S(2)}, u32[]{:S(2)}) collective-permute-start(bf16[2,10,1,128]{3,2,1,0:T(2,128)(2,1)S(1)} %get-tuple-element.47), channel_id=1, source_target_pairs={{0,1},{1,2},{2,3},{3,4},{4,5},{5,6},{6,7},{8,9},{9,10},{10,11},{11... | collective-permute-start | bytes 15368 | tf_op jit(solution)/shard_map/ppermute | solution.py:19
  200.2 7.4 %collective-permute-start.36 = (bf16[2,1,16,128]{3,2,1,0:T(8,128)(2,1)S(1)}, bf16[2,1,16,128]{3,2,1,0:T(8,128)(2,1)S(1)}, u32[]{:S(2)}, u32[]{:S(2)}) collective-permute-start(bf16[2,1,16,128]{3,2,1,0:T(8,128)(2,1)S(1)} %get-tuple-element.72), channel_id=1, source_target_pairs={{0,8},{8,16},{16,24},{24,32},{32,40},{40,48},{48,56},{56,64},{64,7... | collective-permute-start | bytes 24584 | tf_op jit(solution)/shard_map/ppermute | solution.py:19
  210.6 9.0 %collective-permute-start.38 = (bf16[2,10,1,128]{3,2,1,0:T(2,128)(2,1)S(1)}, bf16[2,10,1,128]{3,2,1,0:T(2,128)(2,1)S(1)}, u32[]{:S(2)}, u32[]{:S(2)}) collective-permute-start(bf16[2,10,1,128]{3,2,1,0:T(2,128)(2,1)S(1)} %get-tuple-element.45), channel_id=1, source_target_pairs={{0,1},{1,2},{2,3},{3,4},{4,5},{5,6},{6,7},{8,9},{9,10},{10,11},{11... | collective-permute-start | bytes 15368 | tf_op jit(solution)/shard_map/ppermute | solution.py:19
  218.3 5.0 %collective-permute-start.39 = (bf16[2,10,1,128]{3,2,1,0:T(2,128)(2,1)S(1)}, bf16[2,10,1,128]{3,2,1,0:T(2,128)(2,1)S(1)}, u32[]{:S(2)}, u32[]{:S(2)}) collective-permute-start(bf16[2,10,1,128]{3,2,1,0:T(2,128)(2,1)S(1)} %get-tuple-element.46), channel_id=1, source_target_pairs={{1,0},{2,1},{3,2},{4,3},{5,4},{6,5},{7,6},{9,8},{10,9},{11,10},{12... | collective-permute-start | bytes 15368 | tf_op jit(solution)/shard_map/ppermute | solution.py:21
  223.8 6.2 %collective-permute-start.40 = (bf16[2,1,16,128]{3,2,1,0:T(8,128)(2,1)S(1)}, bf16[2,1,16,128]{3,2,1,0:T(8,128)(2,1)S(1)}, u32[]{:S(2)}, u32[]{:S(2)}) collective-permute-start(bf16[2,1,16,128]{3,2,1,0:T(8,128)(2,1)S(1)} %get-tuple-element.65), channel_id=1, source_target_pairs={{0,8},{8,16},{16,24},{24,32},{32,40},{40,48},{48,56},{56,64},{64,7... | collective-permute-start | bytes 24584 | tf_op jit(solution)/shard_map/ppermute | solution.py:19
  232.8 9.3 %collective-permute-start.42 = (bf16[2,10,1,128]{3,2,1,0:T(2,128)(2,1)S(1)}, bf16[2,10,1,128]{3,2,1,0:T(2,128)(2,1)S(1)}, u32[]{:S(2)}, u32[]{:S(2)}) collective-permute-start(bf16[2,10,1,128]{3,2,1,0:T(2,128)(2,1)S(1)} %get-tuple-element.43), channel_id=1, source_target_pairs={{0,1},{1,2},{2,3},{3,4},{4,5},{5,6},{6,7},{8,9},{9,10},{10,11},{11... | collective-permute-start | bytes 15368 | tf_op jit(solution)/shard_map/ppermute | solution.py:19
  327.4 20.7 %all-to-all-start.3 = ((f32[4,32,18,128]{3,1,2,0:T(8,128)}), f32[4,32,18,128]{3,1,2,0:T(8,128)S(1)}, u32[]{:S(2)}, u32[]{:S(2)}) async-start(f32[4,32,18,128]{3,1,2,0:T(8,128)} %broadcast_in_dim.75), calls=%async_computation.3 | async-start | bytes 2359296 | tf_op jit(solution)/shard_map/all_to_all | solution.py:60
  (19 other events, 161.3 us)
where the time goes:
time: 352 us; the launch traced here: 350 us
  starting transfers between devices  158 us (45%)
  waiting for transfers between devices  95.1 us (27%)
  blocking collectives  79.1 us (22%)
  local copies, waits for them, and re-layouts  7.21 us (2%)
  other arithmetic  4.79 us (1%)
  matrix products  3.62 us (1%)
    ppermute x20, starting transfers between devices, padded_2(): lax.ppermute(tail, axis, [(i, (i + 1) % count) for i in range(ends)])  114 us
    ppermute x20, waiting for transfers between devices, padded_2(): lax.ppermute(head, axis, [((i + 1) % count, i) for i in range(ends)])  64.9 us
    ppermute x20, starting transfers between devices, padded_2(): lax.ppermute(head, axis, [((i + 1) % count, i) for i in range(ends)])  34.9 us
    all_to_all x1, blocking collectives, sum_at_owner(): blocks = lax.all_to_all(cut_along(x, dim, devices), axis, 0, 0, tiled=True)  30.5 us
    all_to_all x1, blocking collectives, sum_in_two_steps(): return jnp.sum(lax.all_to_all(own, far, 0, 0, tiled=True), axis=0)  26.6 us
    all_to_all x1, blocking collectives, copy_for_each(): lax.all_to_all(jnp.broadcast_to(x[None], (devices, *x.shape)), axis, 0, 0...  21.9 us
    all_to_all x1, waiting for transfers between devices, copy_for_each(): lax.all_to_all(jnp.broadcast_to(x[None], (devices, *x.shape)), axis, 0, 0...  16.4 us
    ppermute x4, waiting for transfers between devices, from_behind(): lax.ppermute(value, axis, [(source, source + steps) for source in range(f...  13.7 us
  transfers between devices with their start and end apart: 45, of which 25 were waited for; matrix products, arithmetic and copies ran while one was open for 0% of the time, Pallas kernels for 0%

commit v1 on v0

v1 whole, which is shorter than its diff:
```python
import jax
import jax.numpy as jnp
from jax import lax
from jax.sharding import Mesh
from jax.sharding import PartitionSpec as P

ROW = ("row_0", "row_1")
COL = ("col_0", "col_1")
NEAR = ("row_1", "col_1")
FAR = ("row_0", "col_0")


def with_halo(cells, axis, dim, width):
    count = lax.axis_size(axis)
    size = cells.shape[dim]
    head = lax.slice_in_dim(cells, 0, width, axis=dim)
    tail = lax.slice_in_dim(cells, size - width, size, axis=dim)
    before = lax.ppermute(tail, axis, [(i, i + 1) for i in range(count - 1)])
    after = lax.ppermute(head, axis, [(i + 1, i) for i in range(count - 1)])
    return jnp.concatenate([before, cells, after], axis=dim)


def crop(field, cut):
    if cut == 0:
        return field
    return field[:, cut:-cut, cut:-cut]


def correlate(padded, kernel):
    return lax.conv_general_dilated(
        padded,
        kernel,
        (1, 1),
        "VALID",
        dimension_numbers=("NHWC", "HWIO", "NHWC"),
        preferred_element_type=jnp.float32,
    )


def flip_kernel(kernel):
    return jnp.transpose(jnp.flip(kernel, (0, 1)), (0, 1, 3, 2))


def kernel_grad(cells, padded):
    rows_here, cols_here = (cells.shape[1], cells.shape[2])
    windows = jnp.stack(
        [
            padded[:, 2 - i : 2 - i + rows_here, 2 - j : 2 - j + cols_here]
            for i in range(3)
            for j in range(3)
        ]
    )
    return jnp.einsum("mhwc,kmhwd->kcd", cells, windows, preferred_element_type=jnp.float32)


def sum_of_blocks(blocks, axes):
    parts = lax.all_to_all(blocks, axes, 0, 0, tiled=True)
    return jnp.sum(parts.astype(jnp.float32), axis=0)


def copies(block, axes):
    count = lax.axis_size(axes)
    return lax.all_to_all(jnp.broadcast_to(block[None], (count, *block.shape)), axes, 0, 0, tiled=True)


def total_of(x, factor):
    near, far = (lax.axis_size(NEAR), lax.axis_size(FAR))
    width = x.shape[-1]
    lines = x.astype(jnp.bfloat16).reshape(near, -1, width)
    part = sum_of_blocks(lines, NEAR).astype(jnp.bfloat16)
    own = sum_of_blocks(part.reshape(far, -1, width), FAR)
    own = (own * factor).astype(jnp.bfloat16)
    part = copies(own, FAR).reshape(-1, width)
    return copies(part, NEAR).reshape(x.shape).astype(jnp.float32)


def on_device(section_input, first_pre, second_pre, out_grad, kernels, bn_scale, bn_shift):
    section_index = lax.axis_index("section")
    sections = lax.axis_size("section")
    last = section_index == sections - 1
    micros, rows_here, cols_here, width = out_grad.shape
    inputs = section_input[0]
    kernel = kernels[0]
    scales = bn_scale[0]
    shifts = bn_shift[0]
    first_norm = scales[0] * first_pre[0].astype(jnp.float32) + shifts[0]
    first_act = jnp.maximum(first_norm, 0.0).astype(jnp.bfloat16)
    second_norm = scales[1] * second_pre[0].astype(jnp.float32) + shifts[1]
    alive = second_norm + inputs.astype(jnp.float32) > 0
    one = jnp.ones((), jnp.bfloat16)
    zero = jnp.zeros((), jnp.bfloat16)
    passed = jnp.where(alive, jnp.where(last, out_grad, one), zero)
    first_on = jnp.where(first_norm > 0, one, zero)
    depth = 2 * sections
    masks = jnp.stack([passed, first_on])
    masks = with_halo(masks, COL, 3, depth)
    masks = with_halo(masks, ROW, 2, depth)
    passed, first_on = (masks[0], masks[1])
    flip_first = flip_kernel(kernel[0])
    flip_second = flip_kernel(kernel[1])

    def unit(incoming, reach):
        masked = crop(passed, depth - reach - 2)
        if incoming is not None:
            masked = masked * incoming
        masked = masked.astype(jnp.float32)
        second_grad = (scales[1] * masked).astype(jnp.bfloat16)
        act_grad = correlate(second_grad, flip_second)
        on = crop(first_on, depth - reach - 1).astype(jnp.float32)
        first_grad = (scales[0] * (act_grad * on)).astype(jnp.bfloat16)
        result = crop(masked, 2) + correlate(first_grad, flip_first)
        return (result.astype(jnp.bfloat16), first_grad, second_grad)

    received = None
    own_incoming = jnp.where(last, one, zero)
    for step in range(sections - 1):
        reach = 2 * (sections - 1 - step)
        result, _, _ = unit(received, reach)
        received = lax.ppermute(result, "section", [(sections - 1 - step, sections - 2 - step)])
        own_incoming = own_incoming + crop(received, reach - 2)
    input_grad, first_grad, second_grad = unit(own_incoming, 0)
    partial = jnp.stack(
        [
            kernel_grad(inputs, first_grad),
            kernel_grad(first_act, crop(second_grad, 1)),
        ]
    )
    pixels = micros * rows_here * lax.axis_size(ROW) * cols_here * lax.axis_size(COL)
    factor = 1.0 / jnp.sqrt(jnp.float32(pixels))
    total = total_of(partial, factor).reshape(2, 3, 3, width, width)
    return (input_grad[None], total[None])


def solution(mesh):
    split = Mesh(
        mesh.devices.reshape(mesh.shape["section"], 8, 2, 2, 4),
        ("section", "row_0", "row_1", "col_0", "col_1"),
    )
    in_specs = (
        P("section", None, ROW, COL, None),
        P("section", None, ROW, COL, None),
        P("section", None, ROW, COL, None),
        P(None, ROW, COL, None),
        P("section", None, None, None, None, None),
        P("section", None, None),
        P("section", None, None),
    )
    out_specs = (P("section", None, ROW, COL, None), P("section", None, None, None, None, None))
    return jax.shard_map(
        on_device, mesh=split, in_specs=in_specs, out_specs=out_specs, check_vma=False
    )
```

time: 352 us -> 142 us (0.40)
  starting transfers between devices: 158 us -> 26.9 us
  waiting for transfers between devices: 95.1 us -> 42.1 us
  blocking collectives: 79.1 us -> 50.2 us
    ppermute x44 -> x7, starting transfers between devices: 154 us -> 17 us  [the longest x2 8.55 us: with_halo(): after = lax.ppermute(head, axis, [(i + 1, i) for i in range(count - 1)])]
    ppermute x44 -> x7, waiting for transfers between devices: 78.6 us -> 22.1 us  [the longest x3 15 us: on_device(): lax.ppermute(result, 'section', [(sections - 1 - step, sections - 2 - ste...]
    all_to_all x3 -> x2, blocking collectives: 79.1 us -> 50.2 us  [sum_of_blocks(): parts = lax.all_to_all(blocks, axes, 0, 0, tiled=True)]
    all_to_all x1 -> x2, starting transfers between devices: 3.66 us -> 9.85 us  [copies(): lax.all_to_all(jnp.broadcast_to(block[None], (count, *block.shape)), axes...]
    all_to_all x1 -> x2, waiting for transfers between devices: 16.4 us -> 20.1 us  [copies(): lax.all_to_all(jnp.broadcast_to(block[None], (count, *block.shape)), axes...]
  transfers between devices with their start and end apart: 45 -> 9, of which waited for: 25 -> 6; matrix products, arithmetic and copies ran while one was open for 0% -> 1% of each run, Pallas kernels for 0% -> 0%
where the time goes in v1:
time: 142 us
  blocking collectives  50.2 us (35%)
  waiting for transfers between devices  42.1 us (30%)
  starting transfers between devices  26.9 us (19%)
  local copies, waits for them, and re-layouts  9.25 us (7%)
  matrix products  6.12 us (4%)
  other arithmetic  5.67 us (4%)
  between operations  1.45 us (1%)
    all_to_all x2, blocking collectives, sum_of_blocks(): parts = lax.all_to_all(blocks, axes, 0, 0, tiled=True)  50.2 us
    all_to_all x2, waiting for transfers between devices, copies(): lax.all_to_all(jnp.broadcast_to(block[None], (count, *block.shape)), axes...  20.1 us
    ppermute x3, waiting for transfers between devices, on_device(): lax.ppermute(result, 'section', [(sections - 1 - step, sections - 2 - ste...  15 us
    all_to_all x2, starting transfers between devices, copies(): lax.all_to_all(jnp.broadcast_to(block[None], (count, *block.shape)), axes...  9.85 us
    ppermute x2, starting transfers between devices, with_halo(): after = lax.ppermute(head, axis, [(i + 1, i) for i in range(count - 1)])  8.55 us
    ppermute x2, starting transfers between devices, with_halo(): before = lax.ppermute(tail, axis, [(i, i + 1) for i in range(count - 1)])  5.86 us
    conv_general_dilated x8, matrix products, correlate(): lax.conv_general_dilated(padded, kernel, (1, 1), 'VALID', dimension_numbe...  5.53 us
    ppermute x2, waiting for transfers between devices, with_halo(): after = lax.ppermute(head, axis, [(i + 1, i) for i in range(count - 1)])  4.55 us
  transfers between devices with their start and end apart: 9, of which 6 were waited for; matrix products, arithmetic and copies ran while one was open for 1% of the time, Pallas kernels for 0%

profile of v1, /device:TPU:1, one launch (start us, length us, event | category | flops | bytes accessed | tf_op | source)
XLA Modules:
  0.0 141.7 jit_solution(15433367106172039698)
XLA Ops:
  0.6 0.8 slice_bitcast_fusion.26
  1.4 0.9 fusion.103
  2.3 1.0 fusion.104
  3.3 3.9 %collective-permute-start = (bf16[2,2,8,8,128]{4,3,1,2,0:T(8,128)(2,1)S(1)}, bf16[2,2,8,8,128]{4,3,1,2,0:T(8,128)(2,1)S(1)}, u32[]{:S(2)}, u32[]{:S(2)}) collective-permute-start(bf16[2,2,8,8,128]{4,3,1,2,0:T(8,128)(2,1)S(1)} %get-tuple-element.11), channel_id=1, source_target_pairs={{0,1},{1,2},{2,3},{3,4},{4,5},{5,6},{6,7},{8,9},{9,10},{10,11},{11... | collective-permute-start | bytes 196616 | tf_op jit(solution)/shard_map/ppermute | solution.py:18
  7.2 1.3 collective-permute-start.1
  8.5 3.7 %collective-permute-done.1 = bf16[2,2,8,8,128]{4,3,1,2,0:T(8,128)(2,1)S(1)} collective-permute-done((bf16[2,2,8,8,128]{4,3,1,2,0:T(8,128)(2,1)S(1)}, bf16[2,2,8,8,128]{4,3,1,2,0:T(8,128)(2,1)S(1)}, u32[]{:S(2)}, u32[]{:S(2)}) %collective-permute-start.1) | collective-permute-done | bytes 65568 | tf_op jit(solution)/shard_map/ppermute | solution.py:19
  12.3 7.3 %collective-permute-start.3 = (bf16[2,2,8,32,128]{4,3,1,2,0:T(8,128)(2,1)S(1)}, bf16[2,2,8,32,128]{4,3,1,2,0:T(8,128)(2,1)S(1)}, u32[]{:S(2)}, u32[]{:S(2)}) collective-permute-start(bf16[2,2,8,32,128]{4,3,1,2,0:T(8,128)(2,1)S(1)} %pad_maximum_fusion.2), channel_id=1, source_target_pairs={{8,0},{16,8},{24,16},{32,24},{40,32},{48,40},{56,48},{64,56},{72,6... | collective-permute-start | bytes 786440 | tf_op jit(solution)/shard_map/ppermute | solution.py:19
  19.5 1.9 %collective-permute-start.2 = (bf16[2,2,8,32,128]{4,3,1,2,0:T(8,128)(2,1)S(1)}, bf16[2,2,8,32,128]{4,3,1,2,0:T(8,128)(2,1)S(1)}, u32[]{:S(2)}, u32[]{:S(2)}) collective-permute-start(bf16[2,2,8,32,128]{4,3,1,2,0:T(8,128)(2,1)S(1)} %pad_maximum_fusion.2), channel_id=1, source_target_pairs={{0,8},{8,16},{16,24},{24,32},{32,40},{40,48},{48,56},{56,64},{64,7... | collective-permute-start | bytes 786440 | tf_op jit(solution)/shard_map/ppermute | solution.py:18
  21.4 0.8 collective-permute-done.3
  22.3 2.4 %collective-permute-done.2 = bf16[2,2,8,32,128]{4,3,1,2,0:T(8,128)(2,1)S(1)} collective-permute-done((bf16[2,2,8,32,128]{4,3,1,2,0:T(8,128)(2,1)S(1)}, bf16[2,2,8,32,128]{4,3,1,2,0:T(8,128)(2,1)S(1)}, u32[]{:S(2)}, u32[]{:S(2)}) %collective-permute-start.2) | collective-permute-done | bytes 262176 | tf_op jit(solution)/shard_map/ppermute | solution.py:18
  25.3 0.9 copy-done.2
  26.2 1.0 convolution_select_fusion
  27.9 0.5 copy-done.9
  28.4 0.9 convolution_select_fusion.1
  29.7 0.7 collective-permute-start.4
  31.0 0.9 convolution_select_fusion.2
  32.8 0.8 convolution_select_fusion.3
  34.2 0.7 collective-permute-start.5
  35.2 0.6 convolution_select_fusion.4
  36.7 0.5 convolution_select_fusion.5
  37.6 1.3 collective-permute-start.6
  38.9 15.0 %collective-permute-done.6 = bf16[2,12,20,128]{3,2,0,1:T(8,128)(2,1)S(1)} collective-permute-done((bf16[2,12,20,128]{3,2,0,1:T(8,128)(2,1)S(1)}, bf16[2,12,20,128]{3,2,0,1:T(8,128)(2,1)S(1)}, u32[]{:S(2)}, u32[]{:S(2)}) %collective-permute-start.6) | collective-permute-done | bytes 122912 | tf_op jit(solution)/shard_map/ppermute | solution.py:119
  57.1 23.5 %all_to_all.20 = bf16[8,288,128]{2,1,0:T(8,128)(2,1)S(1)} all-to-all(bf16[8,288,128]{2,1,0:T(8,128)(2,1)S(1)} %bitcast.292), channel_id=1, replica_groups=mesh['section'=4,'row_0'=8,'row_1'=2,'col_0'=2,'col_1'=4] {'row_1','col_1'}, dimensions={0} | all-to-all | bytes 1179648 | tf_op jit(solution)/shard_map/all_to_all | solution.py:57
  80.7 26.7 %all_to_all.21 = bf16[16,18,128]{2,1,0:T(8,128)(2,1)S(1)} all-to-all(bf16[16,18,128]{2,1,0:T(8,128)(2,1)S(1)} %reshape.48), channel_id=1, replica_groups=mesh['section'=4,'row_0'=8,'row_1'=2,'col_0'=2,'col_1'=4] {'row_0','col_0'}, dimensions={0} | all-to-all | bytes 147456 | tf_op jit(solution)/shard_map/all_to_all | solution.py:57
  107.4 0.7 broadcast_in_dim.37
  108.1 3.5 %all-to-all-start.2 = ((bf16[16,18,128]{2,1,0:T(8,128)(2,1)}), bf16[16,18,128]{2,1,0:T(8,128)(2,1)S(1)}, u32[]{:S(2)}, u32[]{:S(2)}) async-start(bf16[16,18,128]{2,1,0:T(8,128)(2,1)} %broadcast_in_dim.37), calls=%async_computation.2 | async-start | bytes 196608 | tf_op jit(solution)/shard_map/all_to_all | solution.py:63
  111.9 11.4 %all-to-all-done.2 = bf16[16,18,128]{2,1,0:T(8,128)(2,1)S(1)} async-done(((bf16[16,18,128]{2,1,0:T(8,128)(2,1)}), bf16[16,18,128]{2,1,0:T(8,128)(2,1)S(1)}, u32[]{:S(2)}, u32[]{:S(2)}) %all-to-all-start.2) | async-done | bytes 73760 | tf_op jit(solution)/shard_map/all_to_all | solution.py:63
  123.3 0.9 broadcast_in_dim.39
  124.2 6.3 %all-to-all-start.3 = ((bf16[8,288,128]{2,1,0:T(8,128)(2,1)}), bf16[8,288,128]{2,1,0:T(8,128)(2,1)S(1)}, u32[]{:S(2)}, u32[]{:S(2)}) async-start(bf16[8,288,128]{2,1,0:T(8,128)(2,1)} %broadcast_in_dim.39), calls=%async_computation.3 | async-start | bytes 1179648 | tf_op jit(solution)/shard_map/all_to_all | solution.py:63
  131.2 0.6 copy.61
  131.9 8.7 %all-to-all-done.3 = bf16[8,288,128]{2,1,0:T(8,128)(2,1)S(1)} async-done(((bf16[8,288,128]{2,1,0:T(8,128)(2,1)}), bf16[8,288,128]{2,1,0:T(8,128)(2,1)S(1)}, u32[]{:S(2)}, u32[]{:S(2)}) %all-to-all-start.3) | async-done | bytes 589856 | tf_op jit(solution)/shard_map/all_to_all | solution.py:63
  140.6 1.1 convert.17
  (108 shorter events, 9.1 us)
Async XLA Ops:
  3.3 5.3 %collective-permute-start = (bf16[2,2,8,8,128]{4,3,1,2,0:T(8,128)(2,1)S(1)}, bf16[2,2,8,8,128]{4,3,1,2,0:T(8,128)(2,1)S(1)}, u32[]{:S(2)}, u32[]{:S(2)}) collective-permute-start(bf16[2,2,8,8,128]{4,3,1,2,0:T(8,128)(2,1)S(1)} %get-tuple-element.11), channel_id=1, source_target_pairs={{0,1},{1,2},{2,3},{3,4},{4,5},{5,6},{6,7},{8,9},{9,10},{10,11},{11... | collective-permute-start | bytes 196616 | tf_op jit(solution)/shard_map/ppermute | solution.py:18
  7.2 5.0 %collective-permute-start.1 = (bf16[2,2,8,8,128]{4,3,1,2,0:T(8,128)(2,1)S(1)}, bf16[2,2,8,8,128]{4,3,1,2,0:T(8,128)(2,1)S(1)}, u32[]{:S(2)}, u32[]{:S(2)}) collective-permute-start(bf16[2,2,8,8,128]{4,3,1,2,0:T(8,128)(2,1)S(1)} %get-tuple-element.12), channel_id=1, source_target_pairs={{1,0},{2,1},{3,2},{4,3},{5,4},{6,5},{7,6},{9,8},{10,9},{11,10},{12... | collective-permute-start | bytes 196616 | tf_op jit(solution)/shard_map/ppermute | solution.py:19
  12.3 10.0 %collective-permute-start.3 = (bf16[2,2,8,32,128]{4,3,1,2,0:T(8,128)(2,1)S(1)}, bf16[2,2,8,32,128]{4,3,1,2,0:T(8,128)(2,1)S(1)}, u32[]{:S(2)}, u32[]{:S(2)}) collective-permute-start(bf16[2,2,8,32,128]{4,3,1,2,0:T(8,128)(2,1)S(1)} %pad_maximum_fusion.2), channel_id=1, source_target_pairs={{8,0},{16,8},{24,16},{32,24},{40,32},{48,40},{56,48},{64,56},{72,6... | collective-permute-start | bytes 786440 | tf_op jit(solution)/shard_map/ppermute | solution.py:19
  19.5 5.2 %collective-permute-start.2 = (bf16[2,2,8,32,128]{4,3,1,2,0:T(8,128)(2,1)S(1)}, bf16[2,2,8,32,128]{4,3,1,2,0:T(8,128)(2,1)S(1)}, u32[]{:S(2)}, u32[]{:S(2)}) collective-permute-start(bf16[2,2,8,32,128]{4,3,1,2,0:T(8,128)(2,1)S(1)} %pad_maximum_fusion.2), channel_id=1, source_target_pairs={{0,8},{8,16},{16,24},{24,32},{32,40},{40,48},{48,56},{56,64},{64,7... | collective-permute-start | bytes 786440 | tf_op jit(solution)/shard_map/ppermute | solution.py:18
  25.1 1.1 copy-start.2
  25.2 1.1 copy-start.10
  27.7 0.7 copy-start.9
  29.7 0.7 collective-permute-start.4
  30.4 0.7 copy-start.8
  32.2 0.7 copy-start.7
  34.1 1.1 copy-start.6
  34.2 0.7 collective-permute-start.5
  35.9 0.8 copy-start.5
  37.6 16.4 %collective-permute-start.6 = (bf16[2,12,20,128]{3,2,0,1:T(8,128)(2,1)S(1)}, bf16[2,12,20,128]{3,2,0,1:T(8,128)(2,1)S(1)}, u32[]{:S(2)}, u32[]{:S(2)}) collective-permute-start(bf16[2,12,20,128]{3,2,0,1:T(8,128)(2,1)S(1)} %fusion.53), channel_id=1, source_target_pairs={{128,0},{129,1},{130,2},{131,3},{132,4},{133,5},{134,6},{135,7},{1... | collective-permute-start | bytes 368648 | tf_op jit(solution)/shard_map/ppermute | solution.py:119
  38.9 15.7 %copy-start.4 = (pred[16,3]{0,1:T(4,128)(4,1)S(1)}, pred[16,3]{0,1:T(4,128)(4,1)}, u32[]{:S(2)}) copy-start(pred[16,3]{0,1:T(4,128)(4,1)} %constant.62) | copy-start | bytes 148
  55.3 0.8 copy-start.1
  55.7 1.1 copy-start
  108.1 15.2 %all-to-all-start.2 = ((bf16[16,18,128]{2,1,0:T(8,128)(2,1)}), bf16[16,18,128]{2,1,0:T(8,128)(2,1)S(1)}, u32[]{:S(2)}, u32[]{:S(2)}) async-start(bf16[16,18,128]{2,1,0:T(8,128)(2,1)} %broadcast_in_dim.37), calls=%async_computation.2 | async-start | bytes 196608 | tf_op jit(solution)/shard_map/all_to_all | solution.py:63
  111.8 18.8 %copy-start.3 = (pred[16,3]{0,1:T(4,128)(4,1)S(1)}, pred[16,3]{0,1:T(4,128)(4,1)}, u32[]{:S(2)}) copy-start(pred[16,3]{0,1:T(4,128)(4,1)} %constant.61) | copy-start | bytes 148
  124.2 16.4 %all-to-all-start.3 = ((bf16[8,288,128]{2,1,0:T(8,128)(2,1)}), bf16[8,288,128]{2,1,0:T(8,128)(2,1)S(1)}, u32[]{:S(2)}, u32[]{:S(2)}) async-start(bf16[8,288,128]{2,1,0:T(8,128)(2,1)} %broadcast_in_dim.39), calls=%async_computation.3 | async-start | bytes 1179648 | tf_op jit(solution)/shard_map/all_to_all | solution.py:63

commit v2 on v1

--- a/solution.py
+++ b/solution.py
@@ -64,13 +64,14 @@
 
 
 def total_of(x, factor):
-    near, far = (lax.axis_size(NEAR), lax.axis_size(FAR))
+    near, stack = (lax.axis_size(NEAR), lax.axis_size("row_0"))
     width = x.shape[-1]
     lines = x.astype(jnp.bfloat16).reshape(near, -1, width)
-    part = sum_of_blocks(lines, NEAR).astype(jnp.bfloat16)
-    own = sum_of_blocks(part.reshape(far, -1, width), FAR)
+    part = sum_of_blocks(lines, NEAR).astype(jnp.bfloat16).reshape(stack, 1, -1, width)
+    twice = jnp.broadcast_to(part, (stack, lax.axis_size("col_0"), *part.shape[2:]))
+    own = sum_of_blocks(twice.reshape(-1, *part.shape[2:]), FAR)
     own = (own * factor).astype(jnp.bfloat16)
-    part = copies(own, FAR).reshape(-1, width)
+    part = lax.all_gather(own, "row_0", axis=0, tiled=True)
     return copies(part, NEAR).reshape(x.shape).astype(jnp.float32)
 
 

time: 142 us -> 151 us (1.063)
  starting transfers between devices: 26.9 us -> 43.3 us
  blocking collectives: 50.2 us -> 42 us
    all_to_all x2 -> x1, blocking collectives: 50.2 us -> 23.5 us  [sum_of_blocks(): parts = lax.all_to_all(blocks, axes, 0, 0, tiled=True)]
    all_gather x0 -> x1, blocking collectives: none -> 18.5 us  [total_of(): part = lax.all_gather(own, 'row_0', axis=0, tiled=True)]
    all_to_all x0 -> x1, starting transfers between devices: none -> 15.1 us  [sum_of_blocks(): parts = lax.all_to_all(blocks, axes, 0, 0, tiled=True)]
    all_to_all x0 -> x1, waiting for transfers between devices: none -> 12 us  [sum_of_blocks(): parts = lax.all_to_all(blocks, axes, 0, 0, tiled=True)]
    all_to_all x2 -> x1, waiting for transfers between devices: 20.1 us -> 8.7 us  [copies(): lax.all_to_all(jnp.broadcast_to(block[None], (count, *block.shape)), axes...]
    all_to_all x2 -> x1, starting transfers between devices: 9.85 us -> 11.2 us  [copies(): lax.all_to_all(jnp.broadcast_to(block[None], (count, *block.shape)), axes...]
    unnamed x42 -> x43, local copies, waits for them, and re-layouts: 3.86 us -> 3.88 us
where the time goes in v2:
time: 151 us
  starting transfers between devices  43.3 us (29%)
  waiting for transfers between devices  42.7 us (28%)
  blocking collectives  42 us (28%)
  local copies, waits for them, and re-layouts  9.26 us (6%)
  matrix products  6.13 us (4%)
  other arithmetic  5.69 us (4%)
    all_to_all x1, blocking collectives, sum_of_blocks(): parts = lax.all_to_all(blocks, axes, 0, 0, tiled=True)  23.5 us
    all_gather x1, blocking collectives, total_of(): part = lax.all_gather(own, 'row_0', axis=0, tiled=True)  18.5 us
    all_to_all x1, starting transfers between devices, sum_of_blocks(): parts = lax.all_to_all(blocks, axes, 0, 0, tiled=True)  15.1 us
    ppermute x3, waiting for transfers between devices, on_device(): lax.ppermute(result, 'section', [(sections - 1 - step, sections - 2 - ste...  15 us
    all_to_all x1, waiting for transfers between devices, sum_of_blocks(): parts = lax.all_to_all(blocks, axes, 0, 0, tiled=True)  12 us
    all_to_all x1, starting transfers between devices, copies(): lax.all_to_all(jnp.broadcast_to(block[None], (count, *block.shape)), axes...  11.2 us
    all_to_all x1, waiting for transfers between devices, copies(): lax.all_to_all(jnp.broadcast_to(block[None], (count, *block.shape)), axes...  8.7 us
    ppermute x2, starting transfers between devices, with_halo(): after = lax.ppermute(head, axis, [(i + 1, i) for i in range(count - 1)])  8.55 us
  transfers between devices with their start and end apart: 9, of which 6 were waited for; matrix products, arithmetic and copies ran while one was open for 1% of the time, Pallas kernels for 0%

profile of v2, /device:TPU:1, one launch (start us, length us, event | category | flops | bytes accessed | tf_op | source)
XLA Modules:
  0.0 150.6 jit_solution(10677023709551831681)
XLA Ops:
  0.6 0.8 slice_bitcast_fusion.26
  1.4 0.9 fusion.103
  2.3 1.0 fusion.104
  3.3 3.9 %collective-permute-start = (bf16[2,2,8,8,128]{4,3,1,2,0:T(8,128)(2,1)S(1)}, bf16[2,2,8,8,128]{4,3,1,2,0:T(8,128)(2,1)S(1)}, u32[]{:S(2)}, u32[]{:S(2)}) collective-permute-start(bf16[2,2,8,8,128]{4,3,1,2,0:T(8,128)(2,1)S(1)} %get-tuple-element.19), channel_id=1, source_target_pairs={{0,1},{1,2},{2,3},{3,4},{4,5},{5,6},{6,7},{8,9},{9,10},{10,11},{11... | collective-permute-start | bytes 196616 | tf_op jit(solution)/shard_map/ppermute | solution.py:18
  7.2 1.3 collective-permute-start.1
  8.5 3.7 %collective-permute-done.1 = bf16[2,2,8,8,128]{4,3,1,2,0:T(8,128)(2,1)S(1)} collective-permute-done((bf16[2,2,8,8,128]{4,3,1,2,0:T(8,128)(2,1)S(1)}, bf16[2,2,8,8,128]{4,3,1,2,0:T(8,128)(2,1)S(1)}, u32[]{:S(2)}, u32[]{:S(2)}) %collective-permute-start.1) | collective-permute-done | bytes 65568 | tf_op jit(solution)/shard_map/ppermute | solution.py:19
  12.3 7.3 %collective-permute-start.3 = (bf16[2,2,8,32,128]{4,3,1,2,0:T(8,128)(2,1)S(1)}, bf16[2,2,8,32,128]{4,3,1,2,0:T(8,128)(2,1)S(1)}, u32[]{:S(2)}, u32[]{:S(2)}) collective-permute-start(bf16[2,2,8,32,128]{4,3,1,2,0:T(8,128)(2,1)S(1)} %pad_maximum_fusion.2), channel_id=1, source_target_pairs={{8,0},{16,8},{24,16},{32,24},{40,32},{48,40},{56,48},{64,56},{72,6... | collective-permute-start | bytes 786440 | tf_op jit(solution)/shard_map/ppermute | solution.py:19
  19.5 1.9 %collective-permute-start.2 = (bf16[2,2,8,32,128]{4,3,1,2,0:T(8,128)(2,1)S(1)}, bf16[2,2,8,32,128]{4,3,1,2,0:T(8,128)(2,1)S(1)}, u32[]{:S(2)}, u32[]{:S(2)}) collective-permute-start(bf16[2,2,8,32,128]{4,3,1,2,0:T(8,128)(2,1)S(1)} %pad_maximum_fusion.2), channel_id=1, source_target_pairs={{0,8},{8,16},{16,24},{24,32},{32,40},{40,48},{48,56},{56,64},{64,7... | collective-permute-start | bytes 786440 | tf_op jit(solution)/shard_map/ppermute | solution.py:18
  21.4 0.8 collective-permute-done.3
  22.3 2.4 %collective-permute-done.2 = bf16[2,2,8,32,128]{4,3,1,2,0:T(8,128)(2,1)S(1)} collective-permute-done((bf16[2,2,8,32,128]{4,3,1,2,0:T(8,128)(2,1)S(1)}, bf16[2,2,8,32,128]{4,3,1,2,0:T(8,128)(2,1)S(1)}, u32[]{:S(2)}, u32[]{:S(2)}) %collective-permute-start.2) | collective-permute-done | bytes 262176 | tf_op jit(solution)/shard_map/ppermute | solution.py:18
  25.3 0.9 copy-done.2
  26.2 1.0 convolution_select_fusion
  27.9 0.5 copy-done.9
  28.4 0.9 convolution_select_fusion.1
  29.7 0.7 collective-permute-start.4
  31.0 0.9 convolution_select_fusion.2
  32.8 0.8 convolution_select_fusion.3
  34.2 0.7 collective-permute-start.5
  35.2 0.6 convolution_select_fusion.4
  36.7 0.5 convolution_select_fusion.5
  37.6 1.3 collective-permute-start.6
  38.9 15.0 %collective-permute-done.6 = bf16[2,12,20,128]{3,2,0,1:T(8,128)(2,1)S(1)} collective-permute-done((bf16[2,12,20,128]{3,2,0,1:T(8,128)(2,1)S(1)}, bf16[2,12,20,128]{3,2,0,1:T(8,128)(2,1)S(1)}, u32[]{:S(2)}, u32[]{:S(2)}) %collective-permute-start.6) | collective-permute-done | bytes 122912 | tf_op jit(solution)/shard_map/ppermute | solution.py:120
  57.1 23.5 %all_to_all.15 = bf16[8,288,128]{2,1,0:T(8,128)(2,1)S(1)} all-to-all(bf16[8,288,128]{2,1,0:T(8,128)(2,1)S(1)} %bitcast.307), channel_id=1, replica_groups=mesh['section'=4,'row_0'=8,'row_1'=2,'col_0'=2,'col_1'=4] {'row_1','col_1'}, dimensions={0} | all-to-all | bytes 1179648 | tf_op jit(solution)/shard_map/all_to_all | solution.py:57
  80.7 0.7 broadcast_in_dim.38
  81.4 15.1 %all-to-all-start.1 = ((bf16[16,36,128]{2,1,0:T(8,128)(2,1)}), bf16[16,36,128]{2,1,0:T(8,128)(2,1)S(1)}, u32[]{:S(2)}, u32[]{:S(2)}) async-start(bf16[16,36,128]{2,1,0:T(8,128)(2,1)} %bitcast.91), calls=%async_computation.1 | async-start | bytes 327680 | tf_op jit(solution)/shard_map/all_to_all | solution.py:57
  96.7 12.0 %all-to-all-done.1 = bf16[16,36,128]{2,1,0:T(8,128)(2,1)S(1)} async-done(((bf16[16,36,128]{2,1,0:T(8,128)(2,1)}), bf16[16,36,128]{2,1,0:T(8,128)(2,1)S(1)}, u32[]{:S(2)}, u32[]{:S(2)}) %all-to-all-start.1) | async-done | bytes 147488 | tf_op jit(solution)/shard_map/all_to_all | solution.py:57
  108.8 18.5 %all-gather = bf16[8,36,128]{2,1,0:T(8,128)(2,1)S(1)} all-gather(bf16[1,36,128]{2,1,0:T(8,128)(2,1)S(1)} %fusion.133), channel_id=1, replica_groups=mesh['section'=4,'row_0'=8,'row_1'=2,'col_0'=2,'col_1'=4] {'row_0'}, dimensions={0}, use_global_device_ids=true | all-gather | bytes 82944 | tf_op jit(solution)/shard_map/all_gather | solution.py:74
  127.3 0.9 broadcast_in_dim.39
  128.2 11.2 %all-to-all-start.2 = ((bf16[8,288,128]{2,1,0:T(8,128)(2,1)}), bf16[8,288,128]{2,1,0:T(8,128)(2,1)S(1)}, u32[]{:S(2)}, u32[]{:S(2)}) async-start(bf16[8,288,128]{2,1,0:T(8,128)(2,1)} %broadcast_in_dim.39), calls=%async_computation.2 | async-start | bytes 1179648 | tf_op jit(solution)/shard_map/all_to_all | solution.py:63
  140.1 0.6 copy.228
  140.7 8.7 %all-to-all-done.2 = bf16[8,288,128]{2,1,0:T(8,128)(2,1)S(1)} async-done(((bf16[8,288,128]{2,1,0:T(8,128)(2,1)}), bf16[8,288,128]{2,1,0:T(8,128)(2,1)S(1)}, u32[]{:S(2)}, u32[]{:S(2)}) %all-to-all-start.2) | async-done | bytes 589856 | tf_op jit(solution)/shard_map/all_to_all | solution.py:63
  149.4 1.1 convert.17
  (108 shorter events, 9.1 us)
Async XLA Ops:
  3.3 5.3 %collective-permute-start = (bf16[2,2,8,8,128]{4,3,1,2,0:T(8,128)(2,1)S(1)}, bf16[2,2,8,8,128]{4,3,1,2,0:T(8,128)(2,1)S(1)}, u32[]{:S(2)}, u32[]{:S(2)}) collective-permute-start(bf16[2,2,8,8,128]{4,3,1,2,0:T(8,128)(2,1)S(1)} %get-tuple-element.19), channel_id=1, source_target_pairs={{0,1},{1,2},{2,3},{3,4},{4,5},{5,6},{6,7},{8,9},{9,10},{10,11},{11... | collective-permute-start | bytes 196616 | tf_op jit(solution)/shard_map/ppermute | solution.py:18
  7.2 5.0 %collective-permute-start.1 = (bf16[2,2,8,8,128]{4,3,1,2,0:T(8,128)(2,1)S(1)}, bf16[2,2,8,8,128]{4,3,1,2,0:T(8,128)(2,1)S(1)}, u32[]{:S(2)}, u32[]{:S(2)}) collective-permute-start(bf16[2,2,8,8,128]{4,3,1,2,0:T(8,128)(2,1)S(1)} %get-tuple-element.20), channel_id=1, source_target_pairs={{1,0},{2,1},{3,2},{4,3},{5,4},{6,5},{7,6},{9,8},{10,9},{11,10},{12... | collective-permute-start | bytes 196616 | tf_op jit(solution)/shard_map/ppermute | solution.py:19
  12.3 10.0 %collective-permute-start.3 = (bf16[2,2,8,32,128]{4,3,1,2,0:T(8,128)(2,1)S(1)}, bf16[2,2,8,32,128]{4,3,1,2,0:T(8,128)(2,1)S(1)}, u32[]{:S(2)}, u32[]{:S(2)}) collective-permute-start(bf16[2,2,8,32,128]{4,3,1,2,0:T(8,128)(2,1)S(1)} %pad_maximum_fusion.2), channel_id=1, source_target_pairs={{8,0},{16,8},{24,16},{32,24},{40,32},{48,40},{56,48},{64,56},{72,6... | collective-permute-start | bytes 786440 | tf_op jit(solution)/shard_map/ppermute | solution.py:19
  19.5 5.2 %collective-permute-start.2 = (bf16[2,2,8,32,128]{4,3,1,2,0:T(8,128)(2,1)S(1)}, bf16[2,2,8,32,128]{4,3,1,2,0:T(8,128)(2,1)S(1)}, u32[]{:S(2)}, u32[]{:S(2)}) collective-permute-start(bf16[2,2,8,32,128]{4,3,1,2,0:T(8,128)(2,1)S(1)} %pad_maximum_fusion.2), channel_id=1, source_target_pairs={{0,8},{8,16},{16,24},{24,32},{32,40},{40,48},{48,56},{56,64},{64,7... | collective-permute-start | bytes 786440 | tf_op jit(solution)/shard_map/ppermute | solution.py:18
  25.1 1.1 copy-start.2
  25.2 1.1 copy-start.10
  27.7 0.7 copy-start.9
  29.7 0.7 collective-permute-start.4
  30.4 0.7 copy-start.8
  32.2 0.7 copy-start.7
  34.1 1.1 copy-start.6
  34.2 0.7 collective-permute-start.5
  35.9 0.8 copy-start.5
  37.6 16.4 %collective-permute-start.6 = (bf16[2,12,20,128]{3,2,0,1:T(8,128)(2,1)S(1)}, bf16[2,12,20,128]{3,2,0,1:T(8,128)(2,1)S(1)}, u32[]{:S(2)}, u32[]{:S(2)}) collective-permute-start(bf16[2,12,20,128]{3,2,0,1:T(8,128)(2,1)S(1)} %fusion.53), channel_id=1, source_target_pairs={{128,0},{129,1},{130,2},{131,3},{132,4},{133,5},{134,6},{135,7},{1... | collective-permute-start | bytes 368648 | tf_op jit(solution)/shard_map/ppermute | solution.py:120
  38.9 15.7 %copy-start.4 = (pred[16,3]{0,1:T(4,128)(4,1)S(1)}, pred[16,3]{0,1:T(4,128)(4,1)}, u32[]{:S(2)}) copy-start(pred[16,3]{0,1:T(4,128)(4,1)} %constant.62) | copy-start | bytes 148
  55.3 0.8 copy-start.1
  55.7 1.1 copy-start
  81.4 27.3 %all-to-all-start.1 = ((bf16[16,36,128]{2,1,0:T(8,128)(2,1)}), bf16[16,36,128]{2,1,0:T(8,128)(2,1)S(1)}, u32[]{:S(2)}, u32[]{:S(2)}) async-start(bf16[16,36,128]{2,1,0:T(8,128)(2,1)} %bitcast.91), calls=%async_computation.1 | async-start | bytes 327680 | tf_op jit(solution)/shard_map/all_to_all | solution.py:57
  127.3 12.3 %copy-start.3 = (pred[16,3]{0,1:T(4,128)(4,1)S(1)}, pred[16,3]{0,1:T(4,128)(4,1)}, u32[]{:S(2)}) copy-start(pred[16,3]{0,1:T(4,128)(4,1)} %constant.61) | copy-start | bytes 148
  128.2 21.2 %all-to-all-start.2 = ((bf16[8,288,128]{2,1,0:T(8,128)(2,1)}), bf16[8,288,128]{2,1,0:T(8,128)(2,1)S(1)}, u32[]{:S(2)}, u32[]{:S(2)}) async-start(bf16[8,288,128]{2,1,0:T(8,128)(2,1)} %broadcast_in_dim.39), calls=%async_computation.2 | async-start | bytes 1179648 | tf_op jit(solution)/shard_map/all_to_all | solution.py:63

commit v3 on v2

v3 whole, which is shorter than its diff:
```python
import functools

import jax
import jax.numpy as jnp
from jax import lax
from jax.experimental import pallas as pl
from jax.experimental.pallas import tpu as pltpu
from jax.sharding import Mesh
from jax.sharding import PartitionSpec as P

ROW = ("row_0", "row_1")
COL = ("col_0", "col_1")
NEAR = ("row_1", "col_1")
FAR = ("row_0", "col_0")
VMEM = pl.BlockSpec(memory_space=pltpu.VMEM)
SMEM = pl.BlockSpec(memory_space=pltpu.SMEM)
PARAMS = pltpu.CompilerParams(vmem_limit_bytes=24 * 1024 * 1024)


DEPTH = 8
NARROW = 4


def prepare_kernel(last, inputs, first_pre, second_pre, out_grad, scale, shift, masks, head, tail, act):
    width = masks.shape[3]
    first_norm = scale[0] * first_pre[...].astype(jnp.float32) + shift[0]
    act[...] = jnp.maximum(first_norm, 0.0).astype(jnp.bfloat16)
    second_norm = scale[1] * second_pre[...].astype(jnp.float32) + shift[1]
    alive = second_norm + inputs[...].astype(jnp.float32) > 0
    passing = jnp.where(last[0] > 0, out_grad[...].astype(jnp.float32), 1.0)
    passed = jnp.where(alive, passing, 0.0).astype(jnp.bfloat16)
    on = jnp.where(first_norm > 0, 1.0, 0.0).astype(jnp.bfloat16)
    for kind, value in enumerate((passed, on)):
        masks[kind] = value
        head[kind] = value[:, :, :DEPTH]
        tail[kind] = value[:, :, width - DEPTH :]


def correlate(field, kernel):
    rows, cols, width = field.shape
    rows -= 2
    slabs = [field[i : i + rows].reshape(rows * cols, width) for i in range(3)]
    parts = jnp.dot(jnp.concatenate(slabs, axis=1), kernel[...], preferred_element_type=jnp.float32)
    before, here, after = [parts[:, j * width : (j + 1) * width] for j in range(3)]
    total = pltpu.roll(before, 1, 0) + here + pltpu.roll(after, rows * cols - 1, 0)
    return total.reshape(rows, cols, width)


def unit(masks, micro, incoming, first, second, scale, reach):
    top = DEPTH - reach - 2
    rows = masks.shape[2] - 2 * top
    masked = masks[0, micro, top : top + rows].astype(jnp.float32)
    if incoming is not None:
        masked = masked * incoming
    second_grad = (scale[1] * masked).astype(jnp.bfloat16)
    on = masks[1, micro, top + 1 : top + rows - 1].astype(jnp.float32)
    first_grad = (scale[0] * (correlate(second_grad, second) * on)).astype(jnp.bfloat16)
    result = masked[2 : rows - 2] + correlate(first_grad, first)
    return (result, first_grad, second_grad)


def widened(cells, frame, skip):
    rows = cells.shape[0] - 2 * skip
    value = cells[skip : skip + rows].astype(jnp.float32)
    if cells.shape[1] == frame.shape[1]:
        return value
    frame[:rows] = jnp.zeros((rows, *frame.shape[1:]), jnp.float32)
    frame[:rows, NARROW : frame.shape[1] - NARROW] = value
    return frame[:rows]


def stage_kernel(*refs, micro, reach, narrow):
    masks, first, second, scale, *received, out, frame = refs
    incoming = widened(received[0], frame, 0) if received else None
    result, _, _ = unit(masks, micro, incoming, first, second, scale, reach)
    if narrow:
        frame[: result.shape[0]] = result
        result = frame[: result.shape[0], NARROW : result.shape[1] - NARROW]
    out[...] = result.astype(jnp.bfloat16)


def filter_grad(cells, windows):
    spread = []
    for field in windows:
        rows, cols, width = field.shape
        flat = field.astype(jnp.float32).reshape(rows * cols, width)
        turned = (pltpu.roll(flat, rows * cols - 1, 0), flat, pltpu.roll(flat, 1, 0))
        spread.append(
            [
                t.reshape(rows, cols, width)[:, DEPTH : cols - DEPTH].astype(jnp.bfloat16)
                for t in turned
            ]
        )
    height = cells.shape[1]
    width = cells.shape[3]
    sides = []
    for i in range(3):
        for j in range(3):
            parts = [s[j][2 - i : 2 - i + height].reshape(-1, width) for s in spread]
            sides.append(jnp.concatenate(parts, axis=0))
    flat = cells[...].reshape(-1, width)
    side = jnp.concatenate(sides, axis=1)
    return lax.dot_general(
        flat, side, (((0,), (0,)), ((), ())), preferred_element_type=jnp.float32
    )


def last_kernel(*refs, micros, steps):
    last, masks, first, second, scale, inputs, act, *received = refs
    out, partial, frame = received[-3:]
    received = received[:-3]
    firsts, seconds = ([], [])
    for micro in range(micros):
        incoming = jnp.where(last[0] > 0, 1.0, 0.0)
        for step in range(steps):
            incoming = incoming + widened(
                received[step * micros + micro], frame.at[step], 2 * (steps - 1 - step)
            )
        result, first_grad, second_grad = unit(masks, micro, incoming, first, second, scale, 0)
        out[micro] = result[:, DEPTH : result.shape[1] - DEPTH].astype(jnp.bfloat16)
        firsts.append(first_grad)
        seconds.append(second_grad[1:-1])
    width = scale.shape[1]
    for which, (cells, windows) in enumerate(((inputs, firsts), (act, seconds))):
        total = filter_grad(cells, windows).astype(jnp.bfloat16)
        for k in range(9):
            partial[which, k] = total[:, k * width : (k + 1) * width]


def join_halo(before, cells, after, dim):
    return jnp.concatenate([before, cells, after], axis=dim)


def both_ways(head, tail, axis):
    count = lax.axis_size(axis)
    before = lax.ppermute(tail, axis, [(i, i + 1) for i in range(count - 1)])
    after = lax.ppermute(head, axis, [(i + 1, i) for i in range(count - 1)])
    return (before, after)


def matrix_of(kernel):
    width = kernel.shape[-1]
    return jnp.transpose(jnp.flip(kernel, (0, 1)), (0, 3, 1, 2)).reshape(3 * width, 3 * width)


def sum_of_blocks(blocks, axes):
    parts = lax.all_to_all(blocks, axes, 0, 0, tiled=True)
    return jnp.sum(parts.astype(jnp.float32), axis=0)


def copies(block, axes):
    count = lax.axis_size(axes)
    return lax.all_to_all(jnp.broadcast_to(block[None], (count, *block.shape)), axes, 0, 0, tiled=True)


def total_of(x, factor):
    near, stack = (lax.axis_size(NEAR), lax.axis_size("row_0"))
    width = x.shape[-1]
    part = sum_of_blocks(x.reshape(near, -1, width), NEAR).astype(jnp.bfloat16)
    part = part.reshape(stack, 1, -1, width)
    twice = jnp.broadcast_to(part, (stack, lax.axis_size("col_0"), *part.shape[2:]))
    own = sum_of_blocks(twice.reshape(-1, *part.shape[2:]), FAR)
    own = (own * factor).astype(jnp.bfloat16)
    part = copies(own, "row_0").reshape(-1, width)
    return copies(part, NEAR).reshape(x.shape).astype(jnp.float32)


def on_device(section_input, first_pre, second_pre, out_grad, kernels, bn_scale, bn_shift):
    sections = lax.axis_size("section")
    last = (lax.axis_index("section") == sections - 1).astype(jnp.int32).reshape(1)
    micros, rows_here, cols_here, width = out_grad.shape
    bf16 = jnp.bfloat16
    scale = bn_scale[0]
    two = (2, micros, rows_here)
    masks, head, tail, act = pl.pallas_call(
        prepare_kernel,
        name="prepare",
        in_specs=[SMEM] + [VMEM] * 6,
        out_specs=[VMEM] * 4,
        out_shape=[
            jax.ShapeDtypeStruct((*two, cols_here, width), bf16),
            jax.ShapeDtypeStruct((*two, DEPTH, width), bf16),
            jax.ShapeDtypeStruct((*two, DEPTH, width), bf16),
            jax.ShapeDtypeStruct(out_grad.shape, bf16),
        ],
        compiler_params=PARAMS,
    )(last, section_input[0], first_pre[0], second_pre[0], out_grad, scale, bn_shift[0])
    before, after = both_ways(head, tail, COL)
    first = matrix_of(kernels[0, 0])
    second = matrix_of(kernels[0, 1])
    masks = join_halo(before, masks, after, 3)
    before, after = both_ways(masks, masks, ROW)
    masks = join_halo(before, masks, after, 2)
    high, wide = masks.shape[2:4]
    frame = pltpu.VMEM((high, wide, width), jnp.float32)

    received = [[]]
    for step in range(sections - 1):
        reach = 2 * (sections - 1 - step)
        narrow = NARROW if step else 0
        sent = []
        for micro in range(micros):
            taken = [received[-1][micro]] if step else []
            result = pl.pallas_call(
                functools.partial(stage_kernel, micro=micro, reach=reach, narrow=bool(step)),
                name=f"stage_{step}_{micro}",
                in_specs=[VMEM] * (4 + len(taken)),
                out_specs=VMEM,
                out_shape=jax.ShapeDtypeStruct(
                    (rows_here + 2 * reach, wide - 2 * narrow, width), bf16
                ),
                scratch_shapes=[frame],
                compiler_params=PARAMS,
            )(masks, first, second, scale, *taken)
            pair = [(sections - 1 - step, sections - 2 - step)]
            sent.append(lax.ppermute(result, "section", pair))
        received.append(sent)
    taken = sum(received, [])
    input_grad, partial = pl.pallas_call(
        functools.partial(last_kernel, micros=micros, steps=sections - 1),
        name="last",
        in_specs=[SMEM] + [VMEM] * (6 + len(taken)),
        out_specs=[VMEM] * 2,
        out_shape=[
            jax.ShapeDtypeStruct(out_grad.shape, bf16),
            jax.ShapeDtypeStruct((2, 9, width, width), bf16),
        ],
        scratch_shapes=[pltpu.VMEM((sections - 1, high, wide, width), jnp.float32)],
        compiler_params=PARAMS,
    )(last, masks, first, second, scale, section_input[0], act, *taken)
    pixels = micros * rows_here * lax.axis_size(ROW) * cols_here * lax.axis_size(COL)
    factor = 1.0 / jnp.sqrt(jnp.float32(pixels))
    total = total_of(partial, factor).reshape(2, 3, 3, width, width)
    return (input_grad[None], total[None])


def solution(mesh):
    split = Mesh(
        mesh.devices.reshape(mesh.shape["section"], 8, 2, 2, 4),
        ("section", "row_0", "row_1", "col_0", "col_1"),
    )
    in_specs = (
        P("section", None, ROW, COL, None),
        P("section", None, ROW, COL, None),
        P("section", None, ROW, COL, None),
        P(None, ROW, COL, None),
        P("section", None, None, None, None, None),
        P("section", None, None),
        P("section", None, None),
    )
    out_specs = (P("section", None, ROW, COL, None), P("section", None, None, None, None, None))
    return jax.shard_map(
        on_device, mesh=split, in_specs=in_specs, out_specs=out_specs, check_vma=False
    )
```

time: 151 us -> 126 us (0.83)
  blocking collectives: 42 us -> 74.7 us
  waiting for transfers between devices: 42.7 us -> 15.8 us
  starting transfers between devices: 43.3 us -> 19.9 us
  Pallas kernels: 0 us -> 7.33 us
  matrix products: 6.13 us -> 0 us
  other arithmetic: 5.69 us -> 1.36 us
  local copies, waits for them, and re-layouts: 9.26 us -> 5.61 us
    all_to_all x2 -> x0, starting transfers between devices: 26.3 us -> none  [the longest x1 15.1 us: sum_of_blocks(): parts = lax.all_to_all(blocks, axes, 0, 0, tiled=True)]
    all_to_all x1 -> x2, blocking collectives: 23.5 us -> 49.3 us  [sum_of_blocks(): parts = lax.all_to_all(blocks, axes, 0, 0, tiled=True)]
    all_to_all x0 -> x2, blocking collectives: none -> 25.4 us  [copies(): lax.all_to_all(jnp.broadcast_to(block[None], (count, *block.shape)), axes...]
    all_to_all x2 -> x0, waiting for transfers between devices: 20.7 us -> none  [the longest x1 12 us: sum_of_blocks(): parts = lax.all_to_all(blocks, axes, 0, 0, tiled=True)]
    all_gather x1 -> x0, blocking collectives: 18.5 us -> none  [total_of(): part = lax.all_gather(own, 'row_0', axis=0, tiled=True)]
    pallas_call x0 -> x8, Pallas kernels: none -> 7.33 us  [the longest x6 5.53 us: on_device(): pl.pallas_call(functools.partial(stage_kernel, micro=micro, reach=reach,...]
    ppermute x7 -> x10, waiting for transfers between devices: 22.1 us -> 15.8 us  [the longest x6 9.63 us: on_device(): sent.append(lax.ppermute(result, 'section', pair))]
    conv_general_dilated x8 -> x0, matrix products: 5.53 us -> none  [correlate(): lax.conv_general_dilated(padded, kernel, (1, 1), 'VALID', dimension_numbe...]
  transfers between devices with their start and end apart: 9 -> 10, of which waited for: 6 -> 5; matrix products, arithmetic and copies ran while one was open for 1% -> 1% of each run, Pallas kernels for 0% -> 4%
where the time goes in v3:
time: 126 us
  blocking collectives  74.7 us (59%)
  starting transfers between devices  19.9 us (16%)
  waiting for transfers between devices  15.8 us (13%)
  Pallas kernels  7.33 us (6%)
  local copies, waits for them, and re-layouts  5.61 us (4%)
  other arithmetic  1.36 us (1%)
    all_to_all x2, blocking collectives, sum_of_blocks(): parts = lax.all_to_all(blocks, axes, 0, 0, tiled=True)  49.3 us
    all_to_all x2, blocking collectives, copies(): lax.all_to_all(jnp.broadcast_to(block[None], (count, *block.shape)), axes...  25.4 us
    ppermute x6, waiting for transfers between devices, on_device(): sent.append(lax.ppermute(result, 'section', pair))  9.63 us
    ppermute x2, starting transfers between devices, both_ways(): after = lax.ppermute(head, axis, [(i + 1, i) for i in range(count - 1)])  8.55 us
    ppermute x2, starting transfers between devices, both_ways(): before = lax.ppermute(tail, axis, [(i, i + 1) for i in range(count - 1)])  5.99 us
    pallas_call x6, Pallas kernels, on_device(): pl.pallas_call(functools.partial(stage_kernel, micro=micro, reach=reach,...  5.53 us
    ppermute x6, starting transfers between devices, on_device(): sent.append(lax.ppermute(result, 'section', pair))  5.39 us
    unnamed x22, local copies, waits for them, and re-layouts  4.85 us
  transfers between devices with their start and end apart: 10, of which 5 were waited for; matrix products, arithmetic and copies ran while one was open for 1% of the time, Pallas kernels for 4%

profile of v3, /device:TPU:1, one launch (start us, length us, event | category | flops | bytes accessed | tf_op | source)
XLA Modules:
  0.0 125.7 jit_solution(16271576229842278590)
XLA Ops:
  0.7 0.8 copy-done
  1.5 0.8 copy-done.2
  2.3 0.8 copy-done.3
  3.2 0.8 copy-done.4
  4.0 0.7 copy-done.5
  4.7 0.7 copy-done.7
  5.4 4.1 %collective-permute-start = (bf16[2,2,8,8,128]{4,3,2,1,0:T(8,128)(2,1)S(1)}, bf16[2,2,8,8,128]{4,3,2,1,0:T(8,128)(2,1)S(1)}, u32[]{:S(2)}, u32[]{:S(2)}) collective-permute-start(bf16[2,2,8,8,128]{4,3,2,1,0:T(8,128)(2,1)S(1)} %get-tuple-element.8), channel_id=1, source_target_pairs={{0,1},{1,2},{2,3},{3,4},{4,5},{5,6},{6,7},{8,9},{9,10},{10,11},{11... | collective-permute-start | bytes 196616 | tf_op jit(solution)/shard_map/ppermute | solution.py:136
  9.5 1.3 %collective-permute-start.1 = (bf16[2,2,8,8,128]{4,3,2,1,0:T(8,128)(2,1)S(1)}, bf16[2,2,8,8,128]{4,3,2,1,0:T(8,128)(2,1)S(1)}, u32[]{:S(2)}, u32[]{:S(2)}) collective-permute-start(bf16[2,2,8,8,128]{4,3,2,1,0:T(8,128)(2,1)S(1)} %get-tuple-element.10), channel_id=1, source_target_pairs={{1,0},{2,1},{3,2},{4,3},{5,4},{6,5},{7,6},{9,8},{10,9},{11,10},{12... | collective-permute-start | bytes 196616 | tf_op jit(solution)/shard_map/ppermute | solution.py:137
  10.9 3.7 %collective-permute-done.1 = bf16[2,2,8,8,128]{4,3,2,1,0:T(8,128)(2,1)S(1)} collective-permute-done((bf16[2,2,8,8,128]{4,3,2,1,0:T(8,128)(2,1)S(1)}, bf16[2,2,8,8,128]{4,3,2,1,0:T(8,128)(2,1)S(1)}, u32[]{:S(2)}, u32[]{:S(2)}) %collective-permute-start.1) | collective-permute-done | bytes 65568 | tf_op jit(solution)/shard_map/ppermute | solution.py:137
  14.6 7.3 %collective-permute-start.3 = (bf16[2,2,8,32,128]{4,3,2,1,0:T(8,128)(2,1)S(1)}, bf16[2,2,8,32,128]{4,3,2,1,0:T(8,128)(2,1)S(1)}, u32[]{:S(2)}, u32[]{:S(2)}) collective-permute-start(bf16[2,2,8,32,128]{4,3,2,1,0:T(8,128)(2,1)S(1)} %constant_dynamic-update-slice_fusion), channel_id=1, source_target_pairs={{8,0},{16,8},{24,16},{32,24},{40,32},{48,40},{56,48},{64,56},{72,6... | collective-permute-start | bytes 786440 | tf_op jit(solution)/shard_map/ppermute | solution.py:137
  21.8 1.9 %collective-permute-start.2 = (bf16[2,2,8,32,128]{4,3,2,1,0:T(8,128)(2,1)S(1)}, bf16[2,2,8,32,128]{4,3,2,1,0:T(8,128)(2,1)S(1)}, u32[]{:S(2)}, u32[]{:S(2)}) collective-permute-start(bf16[2,2,8,32,128]{4,3,2,1,0:T(8,128)(2,1)S(1)} %constant_dynamic-update-slice_fusion), channel_id=1, source_target_pairs={{0,8},{8,16},{16,24},{24,32},{32,40},{40,48},{48,56},{56,64},{64,7... | collective-permute-start | bytes 786440 | tf_op jit(solution)/shard_map/ppermute | solution.py:136
  24.6 2.4 %collective-permute-done.2 = bf16[2,2,8,32,128]{4,3,2,1,0:T(8,128)(2,1)S(1)} collective-permute-done((bf16[2,2,8,32,128]{4,3,2,1,0:T(8,128)(2,1)S(1)}, bf16[2,2,8,32,128]{4,3,2,1,0:T(8,128)(2,1)S(1)}, u32[]{:S(2)}, u32[]{:S(2)}) %collective-permute-start.2) | collective-permute-done | bytes 262176 | tf_op jit(solution)/shard_map/ppermute | solution.py:136
  27.1 1.0 stage_0_0.1
  28.2 0.7 collective-permute-start.4
  28.9 1.0 stage_0_1.1
  29.9 0.7 collective-permute-start.5
  30.6 0.9 stage_1_0.1
  31.5 0.7 collective-permute-start.6
  32.2 0.9 stage_1_1.1
  33.2 0.8 collective-permute-start.7
  34.0 0.8 stage_2_0.1
  34.8 1.3 %collective-permute-start.8 = (bf16[12,24,128]{2,1,0:T(8,128)(2,1)S(1)}, bf16[12,24,128]{2,1,0:T(8,128)(2,1)S(1)}, u32[]{:S(2)}, u32[]{:S(2)}) collective-permute-start(bf16[12,24,128]{2,1,0:T(8,128)(2,1)S(1)} %stage_2_0.1), channel_id=1, source_target_pairs={{128,0},{129,1},{130,2},{131,3},{132,4},{133,5},{134,6},{135,7},{1... | collective-permute-start | bytes 221192 | tf_op jit(solution)/shard_map/ppermute | solution.py:216
  36.1 0.8 stage_2_1.1
  36.9 1.3 %collective-permute-start.9 = (bf16[12,24,128]{2,1,0:T(8,128)(2,1)S(1)}, bf16[12,24,128]{2,1,0:T(8,128)(2,1)S(1)}, u32[]{:S(2)}, u32[]{:S(2)}) collective-permute-start(bf16[12,24,128]{2,1,0:T(8,128)(2,1)S(1)} %stage_2_1.1), channel_id=1, source_target_pairs={{128,0},{129,1},{130,2},{131,3},{132,4},{133,5},{134,6},{135,7},{1... | collective-permute-start | bytes 221192 | tf_op jit(solution)/shard_map/ppermute | solution.py:216
  38.2 7.5 %collective-permute-done.8.refs_11_ = bf16[12,24,128]{2,1,0:T(8,128)(2,1)S(1)} collective-permute-done((bf16[12,24,128]{2,1,0:T(8,128)(2,1)S(1)}, bf16[12,24,128]{2,1,0:T(8,128)(2,1)S(1)}, u32[]{:S(2)}, u32[]{:S(2)}) %collective-permute-start.8) | collective-permute-done | bytes 73760 | tf_op jit(solution)/shard_map/ppermute | solution.py:216
  45.7 2.1 %collective-permute-done.9.refs_12_ = bf16[12,24,128]{2,1,0:T(8,128)(2,1)S(1)} collective-permute-done((bf16[12,24,128]{2,1,0:T(8,128)(2,1)S(1)}, bf16[12,24,128]{2,1,0:T(8,128)(2,1)S(1)}, u32[]{:S(2)}, u32[]{:S(2)}) %collective-permute-start.9) | collective-permute-done | bytes 73760 | tf_op jit(solution)/shard_map/ppermute | solution.py:216
  47.8 1.7 %last.1 = (bf16[2,8,16,128]{3,2,1,0:T(8,128)(2,1)}, bf16[2,9,128,128]{3,2,1,0:T(8,128)(2,1)S(1)}) custom-call(s32[1]{0:T(128)} %bitcast.last.refs_0_, bf16[2,2,24,32,128]{4,3,2,1,0:T(8,128)(2,1)S(1)} %pad_maximum_fusion.refs_0_.refs_1_, bf16[384,384]{1,0:T(8,128)(2,1)S(1)} %bitcast.42, bf16[384,384]{1,0:T(8,128)(2,1)S(1)} %bitcast.35, ...), custom_call_target="tpu_custom_call" | custom-call | tf_op jit(solution)/shard_map/last/pallas_call | solution.py:219
  49.5 23.5 %all_to_all.20 = bf16[8,288,128]{2,1,0:T(8,128)(2,1)S(1)} all-to-all(bf16[8,288,128]{2,1,0:T(8,128)(2,1)S(1)} %bitcast.43), channel_id=1, replica_groups=mesh['section'=4,'row_0'=8,'row_1'=2,'col_0'=2,'col_1'=4] {'row_1','col_1'}, dimensions={0} | all-to-all | bytes 1179648 | tf_op jit(solution)/shard_map/all_to_all | solution.py:147
  73.1 25.9 %all_to_all.21 = bf16[16,36,128]{2,1,0:T(8,128)(2,1)S(1)} all-to-all(bf16[16,36,128]{2,1,0:T(8,128)(2,1)S(1)} %bitcast.60), channel_id=1, replica_groups=mesh['section'=4,'row_0'=8,'row_1'=2,'col_0'=2,'col_1'=4] {'row_0','col_0'}, dimensions={0} | all-to-all | bytes 294912 | tf_op jit(solution)/shard_map/all_to_all | solution.py:147
  99.1 9.8 %all_to_all.22 = bf16[8,36,128]{2,1,0:T(8,128)(2,1)S(1)} all-to-all(bf16[8,36,128]{2,1,0:T(8,128)(2,1)S(1)} %broadcast_in_dim.26), channel_id=1, replica_groups=mesh['section'=4,'row_0'=8,'row_1'=2,'col_0'=2,'col_1'=4] {'row_0'}, dimensions={0} | all-to-all | bytes 147456 | tf_op jit(solution)/shard_map/all_to_all | solution.py:153
  108.9 15.6 %all_to_all.23 = bf16[8,288,128]{2,1,0:T(8,128)(2,1)S(1)} all-to-all(bf16[8,288,128]{2,1,0:T(8,128)(2,1)S(1)} %broadcast_in_dim.28), channel_id=1, replica_groups=mesh['section'=4,'row_0'=8,'row_1'=2,'col_0'=2,'col_1'=4] {'row_1','col_1'}, dimensions={0} | all-to-all | bytes 1179648 | tf_op jit(solution)/shard_map/all_to_all | solution.py:153
  124.6 1.1 convert.3
  (37 shorter events, 1.3 us)
Async XLA Ops:
  0.6 0.8 copy-start
  1.5 0.8 copy-start.2
  2.3 0.8 copy-start.3
  3.2 0.8 copy-start.4
  4.0 0.7 copy-start.5
  4.7 0.7 copy-start.7
  5.4 18.4 %copy-start.8 = (bf16[1,2,3,3,128,128]{5,4,3,2,1,0:T(8,128)(2,1)S(1)}, bf16[1,2,3,3,128,128]{5,4,3,2,1,0:T(8,128)(2,1)}, u32[]{:S(2)}) copy-start(bf16[1,2,3,3,128,128]{5,4,3,2,1,0:T(8,128)(2,1)} %param.11) | copy-start | bytes 1769476
  5.4 5.4 %collective-permute-start = (bf16[2,2,8,8,128]{4,3,2,1,0:T(8,128)(2,1)S(1)}, bf16[2,2,8,8,128]{4,3,2,1,0:T(8,128)(2,1)S(1)}, u32[]{:S(2)}, u32[]{:S(2)}) collective-permute-start(bf16[2,2,8,8,128]{4,3,2,1,0:T(8,128)(2,1)S(1)} %get-tuple-element.8), channel_id=1, source_target_pairs={{0,1},{1,2},{2,3},{3,4},{4,5},{5,6},{6,7},{8,9},{9,10},{10,11},{11... | collective-permute-start | bytes 196616 | tf_op jit(solution)/shard_map/ppermute | solution.py:136
  9.5 5.0 %collective-permute-start.1 = (bf16[2,2,8,8,128]{4,3,2,1,0:T(8,128)(2,1)S(1)}, bf16[2,2,8,8,128]{4,3,2,1,0:T(8,128)(2,1)S(1)}, u32[]{:S(2)}, u32[]{:S(2)}) collective-permute-start(bf16[2,2,8,8,128]{4,3,2,1,0:T(8,128)(2,1)S(1)} %get-tuple-element.10), channel_id=1, source_target_pairs={{1,0},{2,1},{3,2},{4,3},{5,4},{6,5},{7,6},{9,8},{10,9},{11,10},{12... | collective-permute-start | bytes 196616 | tf_op jit(solution)/shard_map/ppermute | solution.py:137
  14.6 10.0 %collective-permute-start.3 = (bf16[2,2,8,32,128]{4,3,2,1,0:T(8,128)(2,1)S(1)}, bf16[2,2,8,32,128]{4,3,2,1,0:T(8,128)(2,1)S(1)}, u32[]{:S(2)}, u32[]{:S(2)}) collective-permute-start(bf16[2,2,8,32,128]{4,3,2,1,0:T(8,128)(2,1)S(1)} %constant_dynamic-update-slice_fusion), channel_id=1, source_target_pairs={{8,0},{16,8},{24,16},{32,24},{40,32},{48,40},{56,48},{64,56},{72,6... | collective-permute-start | bytes 786440 | tf_op jit(solution)/shard_map/ppermute | solution.py:137
  21.8 5.2 %collective-permute-start.2 = (bf16[2,2,8,32,128]{4,3,2,1,0:T(8,128)(2,1)S(1)}, bf16[2,2,8,32,128]{4,3,2,1,0:T(8,128)(2,1)S(1)}, u32[]{:S(2)}, u32[]{:S(2)}) collective-permute-start(bf16[2,2,8,32,128]{4,3,2,1,0:T(8,128)(2,1)S(1)} %constant_dynamic-update-slice_fusion), channel_id=1, source_target_pairs={{0,8},{8,16},{16,24},{24,32},{32,40},{40,48},{48,56},{56,64},{64,7... | collective-permute-start | bytes 786440 | tf_op jit(solution)/shard_map/ppermute | solution.py:136
  24.4 2.7 %copy-start.6 = (f32[1,2,128]{2,1,0:T(2,128)S(1)}, f32[1,2,128]{2,1,0:T(2,128)}, u32[]{:S(2)}) copy-start(f32[1,2,128]{2,1,0:T(2,128)} %param.12) | copy-start | bytes 3076
  28.2 2.4 %collective-permute-start.4 = (bf16[20,32,128]{2,1,0:T(8,128)(2,1)S(1)}, bf16[20,32,128]{2,1,0:T(8,128)(2,1)S(1)}, u32[]{:S(2)}, u32[]{:S(2)}) collective-permute-start(bf16[20,32,128]{2,1,0:T(8,128)(2,1)S(1)} %stage_0_0.1), channel_id=1, source_target_pairs={{384,256},{385,257},{386,258},{387,259},{388,260},{389,261},{390,2... | collective-permute-start | bytes 491528 | tf_op jit(solution)/shard_map/ppermute | solution.py:216
  29.9 2.3 %collective-permute-start.5 = (bf16[20,32,128]{2,1,0:T(8,128)(2,1)S(1)}, bf16[20,32,128]{2,1,0:T(8,128)(2,1)S(1)}, u32[]{:S(2)}, u32[]{:S(2)}) collective-permute-start(bf16[20,32,128]{2,1,0:T(8,128)(2,1)S(1)} %stage_0_1.1), channel_id=1, source_target_pairs={{384,256},{385,257},{386,258},{387,259},{388,260},{389,261},{390,2... | collective-permute-start | bytes 491528 | tf_op jit(solution)/shard_map/ppermute | solution.py:216
  31.5 2.4 %collective-permute-start.6 = (bf16[16,24,128]{2,1,0:T(8,128)(2,1)S(1)}, bf16[16,24,128]{2,1,0:T(8,128)(2,1)S(1)}, u32[]{:S(2)}, u32[]{:S(2)}) collective-permute-start(bf16[16,24,128]{2,1,0:T(8,128)(2,1)S(1)} %stage_1_0.1), channel_id=1, source_target_pairs={{256,128},{257,129},{258,130},{259,131},{260,132},{261,133},{262,1... | collective-permute-start | bytes 294920 | tf_op jit(solution)/shard_map/ppermute | solution.py:216
  33.1 14.7 %copy-start.1 = (bf16[1,2,8,16,128]{4,3,2,1,0:T(8,128)(2,1)S(1)}, bf16[1,2,8,16,128]{4,3,2,1,0:T(8,128)(2,1)}, u32[]{:S(2)}) copy-start(bf16[1,2,8,16,128]{4,3,2,1,0:T(8,128)(2,1)} %param.7) | copy-start | bytes 196612
  33.2 2.9 %collective-permute-start.7 = (bf16[16,24,128]{2,1,0:T(8,128)(2,1)S(1)}, bf16[16,24,128]{2,1,0:T(8,128)(2,1)S(1)}, u32[]{:S(2)}, u32[]{:S(2)}) collective-permute-start(bf16[16,24,128]{2,1,0:T(8,128)(2,1)S(1)} %stage_1_1.1), channel_id=1, source_target_pairs={{256,128},{257,129},{258,130},{259,131},{260,132},{261,133},{262,1... | collective-permute-start | bytes 294920 | tf_op jit(solution)/shard_map/ppermute | solution.py:216
  34.8 10.9 %collective-permute-start.8 = (bf16[12,24,128]{2,1,0:T(8,128)(2,1)S(1)}, bf16[12,24,128]{2,1,0:T(8,128)(2,1)S(1)}, u32[]{:S(2)}, u32[]{:S(2)}) collective-permute-start(bf16[12,24,128]{2,1,0:T(8,128)(2,1)S(1)} %stage_2_0.1), channel_id=1, source_target_pairs={{128,0},{129,1},{130,2},{131,3},{132,4},{133,5},{134,6},{135,7},{1... | collective-permute-start | bytes 221192 | tf_op jit(solution)/shard_map/ppermute | solution.py:216
  36.9 10.9 %collective-permute-start.9 = (bf16[12,24,128]{2,1,0:T(8,128)(2,1)S(1)}, bf16[12,24,128]{2,1,0:T(8,128)(2,1)S(1)}, u32[]{:S(2)}, u32[]{:S(2)}) collective-permute-start(bf16[12,24,128]{2,1,0:T(8,128)(2,1)S(1)} %stage_2_1.1), channel_id=1, source_target_pairs={{128,0},{129,1},{130,2},{131,3},{132,4},{133,5},{134,6},{135,7},{1... | collective-permute-start | bytes 221192 | tf_op jit(solution)/shard_map/ppermute | solution.py:216

commit v4 on v3

--- a/solution.py
+++ b/solution.py
@@ -21,19 +21,33 @@
 NARROW = 4
 
 
-def prepare_kernel(last, inputs, first_pre, second_pre, out_grad, scale, shift, masks, head, tail, act):
+def prepare_kernel(flags, *refs):
+    sources = refs[:6]
+    masks, inward, outward, act, fields, norms, done = refs[6:]
+    targets = [fields.at[k] for k in range(4)] + [norms.at[k] for k in range(2)]
+    moves = [
+        pltpu.make_async_copy(source, target, done.at[k])
+        for k, (source, target) in enumerate(zip(sources, targets))
+    ]
+    for move in moves:
+        move.start()
+    for move in moves:
+        move.wait()
+    inputs, first_pre, second_pre, out_grad = [fields[k].astype(jnp.float32) for k in range(4)]
+    scale, shift = (norms[0], norms[1])
     width = masks.shape[3]
-    first_norm = scale[0] * first_pre[...].astype(jnp.float32) + shift[0]
+    first_norm = scale[0] * first_pre + shift[0]
     act[...] = jnp.maximum(first_norm, 0.0).astype(jnp.bfloat16)
-    second_norm = scale[1] * second_pre[...].astype(jnp.float32) + shift[1]
-    alive = second_norm + inputs[...].astype(jnp.float32) > 0
-    passing = jnp.where(last[0] > 0, out_grad[...].astype(jnp.float32), 1.0)
-    passed = jnp.where(alive, passing, 0.0).astype(jnp.bfloat16)
-    on = jnp.where(first_norm > 0, 1.0, 0.0).astype(jnp.bfloat16)
+    alive = scale[1] * second_pre + shift[1] + inputs > 0
+    passing = jnp.where(flags[0] > 0, out_grad, 1.0)
+    passed = jnp.where(alive, passing, 0.0)
+    on = jnp.where(first_norm > 0, 1.0, 0.0)
     for kind, value in enumerate((passed, on)):
-        masks[kind] = value
-        head[kind] = value[:, :, :DEPTH]
-        tail[kind] = value[:, :, width - DEPTH :]
+        masks[kind] = value.astype(jnp.bfloat16)
+        head = value[:, :, :DEPTH]
+        tail = value[:, :, width - DEPTH :]
+        inward[kind] = jnp.where(flags[1] > 0, tail, head).astype(jnp.bfloat16)
+        outward[kind] = jnp.where(flags[1] > 0, head, tail).astype(jnp.bfloat16)
 
 
 def correlate(field, kernel):
@@ -105,37 +119,46 @@
     )
 
 
-def last_kernel(*refs, micros, steps):
-    last, masks, first, second, scale, inputs, act, *received = refs
-    out, partial, frame = received[-3:]
-    received = received[:-3]
-    firsts, seconds = ([], [])
-    for micro in range(micros):
-        incoming = jnp.where(last[0] > 0, 1.0, 0.0)
-        for step in range(steps):
-            incoming = incoming + widened(
-                received[step * micros + micro], frame.at[step], 2 * (steps - 1 - step)
-            )
-        result, first_grad, second_grad = unit(masks, micro, incoming, first, second, scale, 0)
-        out[micro] = result[:, DEPTH : result.shape[1] - DEPTH].astype(jnp.bfloat16)
-        firsts.append(first_grad)
-        seconds.append(second_grad[1:-1])
+def settle(last, masks, micro, received, first, second, scale, frame):
+    incoming = jnp.where(last[0] > 0, 1.0, 0.0)
+    steps = len(received)
+    for step, cells in enumerate(received):
+        incoming = incoming + widened(cells, frame.at[step], 2 * (steps - 1 - step))
+    result, first_grad, second_grad = unit(masks, micro, incoming, first, second, scale, 0)
+    tile = result[:, DEPTH : result.shape[1] - DEPTH].astype(jnp.bfloat16)
+    return (tile, first_grad, second_grad[1:-1])
+
+
+def early_kernel(*refs, micro):
+    last, masks, first, second, scale, *received, tile, first_grad, second_grad, frame = refs
+    values = settle(last, masks, micro, received, first, second, scale, frame)
+    for ref, value in zip((tile, first_grad, second_grad), values):
+        ref[...] = value
+
+
+def last_kernel(*refs, micros, early):
+    last, masks, first, second, scale, inputs, act, *rest = refs
+    out, partial, frame = rest[-3:]
+    ready = rest[: 3 * early]
+    received = rest[3 * early : -3]
+    units = [[ref[...] for ref in ready[3 * m : 3 * m + 3]] for m in range(early)]
+    units.append(settle(last, masks, micros - 1, received, first, second, scale, frame))
+    for micro, (tile, _, _) in enumerate(units):
+        out[micro] = tile
     width = scale.shape[1]
-    for which, (cells, windows) in enumerate(((inputs, firsts), (act, seconds))):
-        total = filter_grad(cells, windows).astype(jnp.bfloat16)
+    for which, cells in enumerate((inputs, act)):
+        total = filter_grad(cells, [u[1 + which] for u in units]).astype(jnp.bfloat16)
         for k in range(9):
             partial[which, k] = total[:, k * width : (k + 1) * width]
 
 
-def join_halo(before, cells, after, dim):
-    return jnp.concatenate([before, cells, after], axis=dim)
-
-
-def both_ways(head, tail, axis):
+def swaps(inward, outward, axis):
     count = lax.axis_size(axis)
-    before = lax.ppermute(tail, axis, [(i, i + 1) for i in range(count - 1)])
-    after = lax.ppermute(head, axis, [(i + 1, i) for i in range(count - 1)])
-    return (before, after)
+    crossing = [(i, i + 1) for i in range(1, count - 1, 2)]
+    apart = lax.ppermute(outward, axis, crossing + [(j, i) for i, j in crossing])
+    close = lax.ppermute(inward, axis, [(i, i ^ 1) for i in range(count)])
+    even = (lax.axis_index(axis) & 1) == 0
+    return (jnp.where(even, apart, close), jnp.where(even, close, apart))
 
 
 def matrix_of(kernel):
@@ -168,14 +191,15 @@
 def on_device(section_input, first_pre, second_pre, out_grad, kernels, bn_scale, bn_shift):
     sections = lax.axis_size("section")
     last = (lax.axis_index("section") == sections - 1).astype(jnp.int32).reshape(1)
+    even = ((lax.axis_index(COL) & 1) == 0).astype(jnp.int32).reshape(1)
     micros, rows_here, cols_here, width = out_grad.shape
     bf16 = jnp.bfloat16
     scale = bn_scale[0]
     two = (2, micros, rows_here)
-    masks, head, tail, act = pl.pallas_call(
+    masks, inward, outward, act = pl.pallas_call(
         prepare_kernel,
         name="prepare",
-        in_specs=[SMEM] + [VMEM] * 6,
+        in_specs=[SMEM] + [pl.BlockSpec(memory_space=pltpu.MemorySpace.HBM)] * 6,
         out_specs=[VMEM] * 4,
         out_shape=[
             jax.ShapeDtypeStruct((*two, cols_here, width), bf16),
@@ -183,14 +207,30 @@
             jax.ShapeDtypeStruct((*two, DEPTH, width), bf16),
             jax.ShapeDtypeStruct(out_grad.shape, bf16),
         ],
+        scratch_shapes=[
+            pltpu.VMEM((4, *out_grad.shape), bf16),
+            pltpu.VMEM((2, *scale.shape), jnp.float32),
+            pltpu.SemaphoreType.DMA((6,)),
+        ],
         compiler_params=PARAMS,
-    )(last, section_input[0], first_pre[0], second_pre[0], out_grad, scale, bn_shift[0])
-    before, after = both_ways(head, tail, COL)
+    )(
+        jnp.concatenate([last, even]),
+        *[
+            pltpu.with_memory_space_constraint(x, pltpu.MemorySpace.HBM)
+            for x in (section_input[0], first_pre[0], second_pre[0], out_grad, scale, bn_shift[0])
+        ],
+    )
+    left, right = swaps(inward, outward, COL)
+    above, below = swaps(masks, masks, ROW)
+    sides = jnp.concatenate([left, right], axis=3)
+    above_sides, below_sides = swaps(sides, sides, ROW)
     first = matrix_of(kernels[0, 0])
     second = matrix_of(kernels[0, 1])
-    masks = join_halo(before, masks, after, 3)
-    before, after = both_ways(masks, masks, ROW)
-    masks = join_halo(before, masks, after, 2)
+    bands = [
+        jnp.concatenate([side[:, :, :, :DEPTH], middle, side[:, :, :, DEPTH:]], axis=3)
+        for side, middle in ((above_sides, above), (sides, masks), (below_sides, below))
+    ]
+    masks = jnp.concatenate(bands, axis=2)
     high, wide = masks.shape[2:4]
     frame = pltpu.VMEM((high, wide, width), jnp.float32)
 
@@ -215,9 +255,24 @@
             pair = [(sections - 1 - step, sections - 2 - step)]
             sent.append(lax.ppermute(result, "section", pair))
         received.append(sent)
-    taken = sum(received, [])
+    frames = pltpu.VMEM((sections - 1, high, wide, width), jnp.float32)
+    common = (last, masks, first, second, scale)
+    arrived = [[step[micro] for step in received[1:]] for micro in range(micros)]
+    ready = []
+    for micro in range(micros - 1):
+        field = jax.ShapeDtypeStruct((rows_here + 2, wide, width), bf16)
+        ready += pl.pallas_call(
+            functools.partial(early_kernel, micro=micro),
+            name=f"early_{micro}",
+            in_specs=[SMEM] + [VMEM] * (4 + len(arrived[micro])),
+            out_specs=[VMEM] * 3,
+            out_shape=[jax.ShapeDtypeStruct(out_grad.shape[1:], bf16), field, field],
+            scratch_shapes=[frames],
+            compiler_params=PARAMS,
+        )(*common, *arrived[micro])
+    taken = ready + arrived[-1]
     input_grad, partial = pl.pallas_call(
-        functools.partial(last_kernel, micros=micros, steps=sections - 1),
+        functools.partial(last_kernel, micros=micros, early=micros - 1),
         name="last",
         in_specs=[SMEM] + [VMEM] * (6 + len(taken)),
         out_specs=[VMEM] * 2,
@@ -225,9 +280,9 @@
             jax.ShapeDtypeStruct(out_grad.shape, bf16),
             jax.ShapeDtypeStruct((2, 9, width, width), bf16),
         ],
-        scratch_shapes=[pltpu.VMEM((sections - 1, high, wide, width), jnp.float32)],
+        scratch_shapes=[frames],
         compiler_params=PARAMS,
-    )(last, masks, first, second, scale, section_input[0], act, *taken)
+    )(*common, section_input[0], act, *taken)
     pixels = micros * rows_here * lax.axis_size(ROW) * cols_here * lax.axis_size(COL)
     factor = 1.0 / jnp.sqrt(jnp.float32(pixels))
     total = total_of(partial, factor).reshape(2, 3, 3, width, width)

time: 126 us -> 123 us (0.976)
  starting transfers between devices: 19.9 us -> 25.6 us
  waiting for transfers between devices: 15.8 us -> 10.8 us
  local copies, waits for them, and re-layouts: 5.61 us -> 2.46 us
  blocking collectives: 74.7 us -> 71.8 us
  Pallas kernels: 7.33 us -> 9.07 us
    ppermute x4 -> x6, starting transfers between devices: 14.5 us -> 20.3 us  [the longest x3 12.9 us: swaps(): close = lax.ppermute(inward, axis, [(i, i ^ 1) for i in range(count)])]
    unnamed x22 -> x6, local copies, waits for them, and re-layouts: 4.85 us -> 0.61 us
    all_to_all x2, blocking collectives: 49.3 us -> 46.4 us  [sum_of_blocks(): parts = lax.all_to_all(blocks, axes, 0, 0, tiled=True)]
    ppermute x4 -> x6, waiting for transfers between devices: 6.21 us -> 3.58 us  [the longest x3 2.58 us: swaps(): lax.ppermute(outward, axis, crossing + [(j, i) for i, j in crossing])]
    ppermute x6, waiting for transfers between devices: 9.63 us -> 7.17 us  [on_device(): sent.append(lax.ppermute(result, 'section', pair))]
    pallas_call x2 -> x3, Pallas kernels: 1.79 us -> 3.57 us  [the longest x1 1.61 us: on_device(): pl.pallas_call(prepare_kernel, name='prepare', in_specs=[SMEM] + [pl.Bloc...]
  transfers between devices with their start and end apart: 10 -> 12, of which waited for: 5 -> 4; matrix products, arithmetic and copies ran while one was open for 1% -> 1% of each run, Pallas kernels for 4% -> 4%
where the time goes in v4:
time: 123 us; the launch traced here: 122 us
  blocking collectives  71.8 us (58%)
  starting transfers between devices  25.6 us (21%)
  waiting for transfers between devices  10.8 us (9%)
  Pallas kernels  9.07 us (7%)
  local copies, waits for them, and re-layouts  2.46 us (2%)
  other arithmetic  1.54 us (1%)
    all_to_all x2, blocking collectives, sum_of_blocks(): parts = lax.all_to_all(blocks, axes, 0, 0, tiled=True)  46.4 us
    all_to_all x2, blocking collectives, copies(): lax.all_to_all(jnp.broadcast_to(block[None], (count, *block.shape)), axes...  25.4 us
    ppermute x3, starting transfers between devices, swaps(): close = lax.ppermute(inward, axis, [(i, i ^ 1) for i in range(count)])  12.9 us
    ppermute x3, starting transfers between devices, swaps(): lax.ppermute(outward, axis, crossing + [(j, i) for i, j in crossing])  7.38 us
    ppermute x6, waiting for transfers between devices, on_device(): sent.append(lax.ppermute(result, 'section', pair))  7.17 us
    pallas_call x6, Pallas kernels, on_device(): pl.pallas_call(functools.partial(stage_kernel, micro=micro, reach=reach,...  5.5 us
    ppermute x6, starting transfers between devices, on_device(): sent.append(lax.ppermute(result, 'section', pair))  5.39 us
    ppermute x3, waiting for transfers between devices, swaps(): lax.ppermute(outward, axis, crossing + [(j, i) for i, j in crossing])  2.58 us
  transfers between devices with their start and end apart: 12, of which 4 were waited for; matrix products, arithmetic and copies ran while one was open for 1% of the time, Pallas kernels for 4%

profile of v4, /device:TPU:1, one launch (start us, length us, event | category | flops | bytes accessed | tf_op | source)
XLA Modules:
  0.0 122.2 jit_solution(2868508053464101050)
XLA Ops:
  0.7 1.6 %prepare.1 = (bf16[2,2,8,16,128]{4,3,2,1,0:T(8,128)(2,1)S(1)}, bf16[2,2,8,8,128]{4,3,2,1,0:T(8,128)(2,1)S(1)}, bf16[2,2,8,8,128]{4,3,2,1,0:T(8,128)(2,1)S(1)}, bf16[2,8,16,128]{3,2,1,0:T(8,128)(2,1)S(1)}) custom-call(s32[2]{0:T(128)S(1)} %pad_add_fusion.flags, bf16[2,8,16,128]{3,2,1,0:T(8,128)(2,1)} %bitcast.47, bf16[2,8,16,128]{3,2,1,0:T(8,128)(2,1)} %bitcast.62, ...), custom_call_target="tpu_custom_call" | custom-call | tf_op jit(solution)/shard_map/prepare/pallas_call | solution.py:199
  2.3 8.7 %collective-permute-start.5 = (bf16[2,2,8,16,128]{4,3,2,1,0:T(8,128)(2,1)S(1)}, bf16[2,2,8,16,128]{4,3,2,1,0:T(8,128)(2,1)S(1)}, u32[]{:S(2)}, u32[]{:S(2)}) collective-permute-start(bf16[2,2,8,16,128]{4,3,2,1,0:T(8,128)(2,1)S(1)} %get-tuple-element.13), channel_id=1, source_target_pairs={{0,8},{8,0},{16,24},{24,16},{32,40},{40,32},{48,56},{56,48},{64,72... | collective-permute-start | bytes 393224 | tf_op jit(solution)/shard_map/ppermute | solution.py:159
  11.1 1.9 %collective-permute-start.4 = (bf16[2,2,8,16,128]{4,3,2,1,0:T(8,128)(2,1)S(1)}, bf16[2,2,8,16,128]{4,3,2,1,0:T(8,128)(2,1)S(1)}, u32[]{:S(2)}, u32[]{:S(2)}) collective-permute-start(bf16[2,2,8,16,128]{4,3,2,1,0:T(8,128)(2,1)S(1)} %get-tuple-element.13), channel_id=1, source_target_pairs={{8,16},{24,32},{40,48},{56,64},{72,80},{88,96},{104,112},{16,8},{3... | collective-permute-start | bytes 393224 | tf_op jit(solution)/shard_map/ppermute | solution.py:158
  13.0 0.7 collective-permute-start
  13.7 2.2 %collective-permute-start.1 = (bf16[2,2,8,8,128]{4,3,2,1,0:T(8,128)(2,1)S(1)}, bf16[2,2,8,8,128]{4,3,2,1,0:T(8,128)(2,1)S(1)}, u32[]{:S(2)}, u32[]{:S(2)}) collective-permute-start(bf16[2,2,8,8,128]{4,3,2,1,0:T(8,128)(2,1)S(1)} %get-tuple-element.12), channel_id=1, source_target_pairs={{0,1},{1,0},{2,3},{3,2},{4,5},{5,4},{6,7},{7,6},{8,9},{9,8},{10,11... | collective-permute-start | bytes 196616 | tf_op jit(solution)/shard_map/ppermute | solution.py:159
  15.9 1.1 slice_bitcast_fusion
  17.7 1.0 collective-permute-done.1
  18.8 1.9 %collective-permute-start.3 = (bf16[2,2,8,16,128]{4,3,2,1,0:T(8,128)(2,1)S(1)}, bf16[2,2,8,16,128]{4,3,2,1,0:T(8,128)(2,1)S(1)}, u32[]{:S(2)}, u32[]{:S(2)}) collective-permute-start(bf16[2,2,8,16,128]{4,3,2,1,0:T(8,128)(2,1)S(1)} %pad_maximum_fusion), channel_id=1, source_target_pairs={{0,8},{8,0},{16,24},{24,16},{32,40},{40,32},{48,56},{56,48},{64,72... | collective-permute-start | bytes 393224 | tf_op jit(solution)/shard_map/ppermute | solution.py:159
  20.7 4.8 %collective-permute-start.2 = (bf16[2,2,8,16,128]{4,3,2,1,0:T(8,128)(2,1)S(1)}, bf16[2,2,8,16,128]{4,3,2,1,0:T(8,128)(2,1)S(1)}, u32[]{:S(2)}, u32[]{:S(2)}) collective-permute-start(bf16[2,2,8,16,128]{4,3,2,1,0:T(8,128)(2,1)S(1)} %pad_maximum_fusion), channel_id=1, source_target_pairs={{8,16},{24,32},{40,48},{56,64},{72,80},{88,96},{104,112},{16,8},{3... | collective-permute-start | bytes 393224 | tf_op jit(solution)/shard_map/ppermute | solution.py:158
  25.5 2.6 %collective-permute-done.2 = bf16[2,2,8,16,128]{4,3,2,1,0:T(8,128)(2,1)S(1)} collective-permute-done((bf16[2,2,8,16,128]{4,3,2,1,0:T(8,128)(2,1)S(1)}, bf16[2,2,8,16,128]{4,3,2,1,0:T(8,128)(2,1)S(1)}, u32[]{:S(2)}, u32[]{:S(2)}) %collective-permute-start.2) | collective-permute-done | bytes 131104 | tf_op jit(solution)/shard_map/ppermute | solution.py:158
  28.3 0.5 copy-done.1
  28.8 1.0 stage_0_0.1
  29.9 0.7 collective-permute-start.6
  30.5 1.0 stage_0_1.1
  31.6 0.7 collective-permute-start.9
  32.3 0.9 stage_1_0.1
  33.2 0.7 collective-permute-start.7
  33.9 0.9 stage_1_1.1
  34.8 0.7 collective-permute-start.10
  35.5 0.8 stage_2_0.1
  36.3 1.3 %collective-permute-start.8 = (bf16[12,24,128]{2,1,0:T(8,128)(2,1)S(1)}, bf16[12,24,128]{2,1,0:T(8,128)(2,1)S(1)}, u32[]{:S(2)}, u32[]{:S(2)}) collective-permute-start(bf16[12,24,128]{2,1,0:T(8,128)(2,1)S(1)} %stage_2_0.1), channel_id=1, source_target_pairs={{128,0},{129,1},{130,2},{131,3},{132,4},{133,5},{134,6},{135,7},{1... | collective-permute-start | bytes 221192 | tf_op jit(solution)/shard_map/ppermute | solution.py:256
  37.6 0.8 stage_2_1.1
  38.4 1.4 %collective-permute-start.11 = (bf16[12,24,128]{2,1,0:T(8,128)(2,1)S(1)}, bf16[12,24,128]{2,1,0:T(8,128)(2,1)S(1)}, u32[]{:S(2)}, u32[]{:S(2)}) collective-permute-start(bf16[12,24,128]{2,1,0:T(8,128)(2,1)S(1)} %stage_2_1.1), channel_id=1, source_target_pairs={{128,0},{129,1},{130,2},{131,3},{132,4},{133,5},{134,6},{135,7},{1... | collective-permute-start | bytes 221192 | tf_op jit(solution)/shard_map/ppermute | solution.py:256
  39.8 5.3 %collective-permute-done.8.refs_7_ = bf16[12,24,128]{2,1,0:T(8,128)(2,1)S(1)} collective-permute-done((bf16[12,24,128]{2,1,0:T(8,128)(2,1)S(1)}, bf16[12,24,128]{2,1,0:T(8,128)(2,1)S(1)}, u32[]{:S(2)}, u32[]{:S(2)}) %collective-permute-start.8) | collective-permute-done | bytes 73760 | tf_op jit(solution)/shard_map/ppermute | solution.py:256
  45.2 0.6 early_0.1
  45.8 1.9 %collective-permute-done.11.refs_12_ = bf16[12,24,128]{2,1,0:T(8,128)(2,1)S(1)} collective-permute-done((bf16[12,24,128]{2,1,0:T(8,128)(2,1)S(1)}, bf16[12,24,128]{2,1,0:T(8,128)(2,1)S(1)}, u32[]{:S(2)}, u32[]{:S(2)}) %collective-permute-start.11) | collective-permute-done | bytes 73760 | tf_op jit(solution)/shard_map/ppermute | solution.py:256
  47.6 1.3 %last.1 = (bf16[2,8,16,128]{3,2,1,0:T(8,128)(2,1)}, bf16[2,9,128,128]{3,2,1,0:T(8,128)(2,1)S(1)}) custom-call(s32[1]{0:T(128)} %bitcast.refs_0_, bf16[2,2,24,32,128]{4,3,2,1,0:T(8,128)(2,1)S(1)} %maximum_maximum_fusion.refs_0_.refs_1_, bf16[384,384]{1,0:T(8,128)(2,1)S(1)} %bitcast.45, bf16[384,384]{1,0:T(8,128)(2,1)S(1)} %bitcast.37, f32[2,128]{1,0:T(2,128)S(1)} %bitcast.57, ...), custom_call_target="tpu_custom_call" | custom-call | tf_op jit(solution)/shard_map/last/pallas_call | solution.py:274
  49.0 17.7 %all_to_all.20 = bf16[8,288,128]{2,1,0:T(8,128)(2,1)S(1)} all-to-all(bf16[8,288,128]{2,1,0:T(8,128)(2,1)S(1)} %bitcast.46), channel_id=1, replica_groups=mesh['section'=4,'row_0'=8,'row_1'=2,'col_0'=2,'col_1'=4] {'row_1','col_1'}, dimensions={0} | all-to-all | bytes 1179648 | tf_op jit(solution)/shard_map/all_to_all | solution.py:170
  66.8 28.7 %all_to_all.21 = bf16[16,36,128]{2,1,0:T(8,128)(2,1)S(1)} all-to-all(bf16[16,36,128]{2,1,0:T(8,128)(2,1)S(1)} %bitcast.61), channel_id=1, replica_groups=mesh['section'=4,'row_0'=8,'row_1'=2,'col_0'=2,'col_1'=4] {'row_0','col_0'}, dimensions={0} | all-to-all | bytes 294912 | tf_op jit(solution)/shard_map/all_to_all | solution.py:170
  95.6 9.8 %all_to_all.22 = bf16[8,36,128]{2,1,0:T(8,128)(2,1)S(1)} all-to-all(bf16[8,36,128]{2,1,0:T(8,128)(2,1)S(1)} %broadcast_in_dim.26), channel_id=1, replica_groups=mesh['section'=4,'row_0'=8,'row_1'=2,'col_0'=2,'col_1'=4] {'row_0'}, dimensions={0} | all-to-all | bytes 147456 | tf_op jit(solution)/shard_map/all_to_all | solution.py:176
  105.5 15.6 %all_to_all.23 = bf16[8,288,128]{2,1,0:T(8,128)(2,1)S(1)} all-to-all(bf16[8,288,128]{2,1,0:T(8,128)(2,1)S(1)} %broadcast_in_dim.28), channel_id=1, replica_groups=mesh['section'=4,'row_0'=8,'row_1'=2,'col_0'=2,'col_1'=4] {'row_1','col_1'}, dimensions={0} | all-to-all | bytes 1179648 | tf_op jit(solution)/shard_map/all_to_all | solution.py:176
  121.1 1.1 convert.4
  (31 shorter events, 1.3 us)
Async XLA Ops:
  2.3 23.1 %collective-permute-start.5 = (bf16[2,2,8,16,128]{4,3,2,1,0:T(8,128)(2,1)S(1)}, bf16[2,2,8,16,128]{4,3,2,1,0:T(8,128)(2,1)S(1)}, u32[]{:S(2)}, u32[]{:S(2)}) collective-permute-start(bf16[2,2,8,16,128]{4,3,2,1,0:T(8,128)(2,1)S(1)} %get-tuple-element.13), channel_id=1, source_target_pairs={{0,8},{8,0},{16,24},{24,16},{32,40},{40,32},{48,56},{56,48},{64,72... | collective-permute-start | bytes 393224 | tf_op jit(solution)/shard_map/ppermute | solution.py:159
  11.1 14.4 %collective-permute-start.4 = (bf16[2,2,8,16,128]{4,3,2,1,0:T(8,128)(2,1)S(1)}, bf16[2,2,8,16,128]{4,3,2,1,0:T(8,128)(2,1)S(1)}, u32[]{:S(2)}, u32[]{:S(2)}) collective-permute-start(bf16[2,2,8,16,128]{4,3,2,1,0:T(8,128)(2,1)S(1)} %get-tuple-element.13), channel_id=1, source_target_pairs={{8,16},{24,32},{40,48},{56,64},{72,80},{88,96},{104,112},{16,8},{3... | collective-permute-start | bytes 393224 | tf_op jit(solution)/shard_map/ppermute | solution.py:158
  13.0 4.7 %collective-permute-start = (bf16[2,2,8,8,128]{4,3,2,1,0:T(8,128)(2,1)S(1)}, bf16[2,2,8,8,128]{4,3,2,1,0:T(8,128)(2,1)S(1)}, u32[]{:S(2)}, u32[]{:S(2)}) collective-permute-start(bf16[2,2,8,8,128]{4,3,2,1,0:T(8,128)(2,1)S(1)} %get-tuple-element.11), channel_id=1, source_target_pairs={{1,2},{3,4},{5,6},{2,1},{4,3},{6,5},{9,10},{11,12},{13,14},{10,9},... | collective-permute-start | bytes 196616 | tf_op jit(solution)/shard_map/ppermute | solution.py:158
  13.7 5.0 %collective-permute-start.1 = (bf16[2,2,8,8,128]{4,3,2,1,0:T(8,128)(2,1)S(1)}, bf16[2,2,8,8,128]{4,3,2,1,0:T(8,128)(2,1)S(1)}, u32[]{:S(2)}, u32[]{:S(2)}) collective-permute-start(bf16[2,2,8,8,128]{4,3,2,1,0:T(8,128)(2,1)S(1)} %get-tuple-element.12), channel_id=1, source_target_pairs={{0,1},{1,0},{2,3},{3,2},{4,5},{5,4},{6,7},{7,6},{8,9},{9,8},{10,11... | collective-permute-start | bytes 196616 | tf_op jit(solution)/shard_map/ppermute | solution.py:159
  18.8 6.8 %collective-permute-start.3 = (bf16[2,2,8,16,128]{4,3,2,1,0:T(8,128)(2,1)S(1)}, bf16[2,2,8,16,128]{4,3,2,1,0:T(8,128)(2,1)S(1)}, u32[]{:S(2)}, u32[]{:S(2)}) collective-permute-start(bf16[2,2,8,16,128]{4,3,2,1,0:T(8,128)(2,1)S(1)} %pad_maximum_fusion), channel_id=1, source_target_pairs={{0,8},{8,0},{16,24},{24,16},{32,40},{40,32},{48,56},{56,48},{64,72... | collective-permute-start | bytes 393224 | tf_op jit(solution)/shard_map/ppermute | solution.py:159
  20.7 7.4 %collective-permute-start.2 = (bf16[2,2,8,16,128]{4,3,2,1,0:T(8,128)(2,1)S(1)}, bf16[2,2,8,16,128]{4,3,2,1,0:T(8,128)(2,1)S(1)}, u32[]{:S(2)}, u32[]{:S(2)}) collective-permute-start(bf16[2,2,8,16,128]{4,3,2,1,0:T(8,128)(2,1)S(1)} %pad_maximum_fusion), channel_id=1, source_target_pairs={{8,16},{24,32},{40,48},{56,64},{72,80},{88,96},{104,112},{16,8},{3... | collective-permute-start | bytes 393224 | tf_op jit(solution)/shard_map/ppermute | solution.py:158
  28.1 0.7 copy-start.1
  29.9 2.4 %collective-permute-start.6 = (bf16[20,32,128]{2,1,0:T(8,128)(2,1)S(1)}, bf16[20,32,128]{2,1,0:T(8,128)(2,1)S(1)}, u32[]{:S(2)}, u32[]{:S(2)}) collective-permute-start(bf16[20,32,128]{2,1,0:T(8,128)(2,1)S(1)} %stage_0_0.1), channel_id=1, source_target_pairs={{384,256},{385,257},{386,258},{387,259},{388,260},{389,261},{390,2... | collective-permute-start | bytes 491528 | tf_op jit(solution)/shard_map/ppermute | solution.py:256
  31.6 2.3 %collective-permute-start.9 = (bf16[20,32,128]{2,1,0:T(8,128)(2,1)S(1)}, bf16[20,32,128]{2,1,0:T(8,128)(2,1)S(1)}, u32[]{:S(2)}, u32[]{:S(2)}) collective-permute-start(bf16[20,32,128]{2,1,0:T(8,128)(2,1)S(1)} %stage_0_1.1), channel_id=1, source_target_pairs={{384,256},{385,257},{386,258},{387,259},{388,260},{389,261},{390,2... | collective-permute-start | bytes 491528 | tf_op jit(solution)/shard_map/ppermute | solution.py:256
  33.2 2.3 %collective-permute-start.7 = (bf16[16,24,128]{2,1,0:T(8,128)(2,1)S(1)}, bf16[16,24,128]{2,1,0:T(8,128)(2,1)S(1)}, u32[]{:S(2)}, u32[]{:S(2)}) collective-permute-start(bf16[16,24,128]{2,1,0:T(8,128)(2,1)S(1)} %stage_1_0.1), channel_id=1, source_target_pairs={{256,128},{257,129},{258,130},{259,131},{260,132},{261,133},{262,1... | collective-permute-start | bytes 294920 | tf_op jit(solution)/shard_map/ppermute | solution.py:256
  34.8 2.8 %collective-permute-start.10 = (bf16[16,24,128]{2,1,0:T(8,128)(2,1)S(1)}, bf16[16,24,128]{2,1,0:T(8,128)(2,1)S(1)}, u32[]{:S(2)}, u32[]{:S(2)}) collective-permute-start(bf16[16,24,128]{2,1,0:T(8,128)(2,1)S(1)} %stage_1_1.1), channel_id=1, source_target_pairs={{256,128},{257,129},{258,130},{259,131},{260,132},{261,133},{262,1... | collective-permute-start | bytes 294920 | tf_op jit(solution)/shard_map/ppermute | solution.py:256
  36.3 8.9 %collective-permute-start.8 = (bf16[12,24,128]{2,1,0:T(8,128)(2,1)S(1)}, bf16[12,24,128]{2,1,0:T(8,128)(2,1)S(1)}, u32[]{:S(2)}, u32[]{:S(2)}) collective-permute-start(bf16[12,24,128]{2,1,0:T(8,128)(2,1)S(1)} %stage_2_0.1), channel_id=1, source_target_pairs={{128,0},{129,1},{130,2},{131,3},{132,4},{133,5},{134,6},{135,7},{1... | collective-permute-start | bytes 221192 | tf_op jit(solution)/shard_map/ppermute | solution.py:256
  38.4 9.2 %copy-start = (bf16[1,2,8,16,128]{4,3,2,1,0:T(8,128)(2,1)S(1)}, bf16[1,2,8,16,128]{4,3,2,1,0:T(8,128)(2,1)}, u32[]{:S(2)}) copy-start(bf16[1,2,8,16,128]{4,3,2,1,0:T(8,128)(2,1)} %param.7) | copy-start | bytes 196612
  38.4 9.2 %collective-permute-start.11 = (bf16[12,24,128]{2,1,0:T(8,128)(2,1)S(1)}, bf16[12,24,128]{2,1,0:T(8,128)(2,1)S(1)}, u32[]{:S(2)}, u32[]{:S(2)}) collective-permute-start(bf16[12,24,128]{2,1,0:T(8,128)(2,1)S(1)} %stage_2_1.1), channel_id=1, source_target_pairs={{128,0},{129,1},{130,2},{131,3},{132,4},{133,5},{134,6},{135,7},{1... | collective-permute-start | bytes 221192 | tf_op jit(solution)/shard_map/ppermute | solution.py:256

commit v5 on v4

--- a/solution.py
+++ b/solution.py
@@ -23,7 +23,7 @@
 
 def prepare_kernel(flags, *refs):
     sources = refs[:6]
-    masks, inward, outward, act, fields, norms, done = refs[6:]
+    masks, inward, outward, act, kept, fields, norms, done = refs[6:]
     targets = [fields.at[k] for k in range(4)] + [norms.at[k] for k in range(2)]
     moves = [
         pltpu.make_async_copy(source, target, done.at[k])
@@ -35,6 +35,7 @@
         move.wait()
     inputs, first_pre, second_pre, out_grad = [fields[k].astype(jnp.float32) for k in range(4)]
     scale, shift = (norms[0], norms[1])
+    kept[...] = scale
     width = masks.shape[3]
     first_norm = scale[0] * first_pre + shift[0]
     act[...] = jnp.maximum(first_norm, 0.0).astype(jnp.bfloat16)
@@ -188,7 +189,7 @@
     return copies(part, NEAR).reshape(x.shape).astype(jnp.float32)
 
 
-def on_device(section_input, first_pre, second_pre, out_grad, kernels, bn_scale, bn_shift):
+def section_backward(section_input, first_pre, second_pre, out_grad, kernels, bn_scale, bn_shift):
     sections = lax.axis_size("section")
     last = (lax.axis_index("section") == sections - 1).astype(jnp.int32).reshape(1)
     even = ((lax.axis_index(COL) & 1) == 0).astype(jnp.int32).reshape(1)
@@ -196,16 +197,17 @@
     bf16 = jnp.bfloat16
     scale = bn_scale[0]
     two = (2, micros, rows_here)
-    masks, inward, outward, act = pl.pallas_call(
+    masks, inward, outward, act, scale = pl.pallas_call(
         prepare_kernel,
         name="prepare",
         in_specs=[SMEM] + [pl.BlockSpec(memory_space=pltpu.MemorySpace.HBM)] * 6,
-        out_specs=[VMEM] * 4,
+        out_specs=[VMEM] * 5,
         out_shape=[
             jax.ShapeDtypeStruct((*two, cols_here, width), bf16),
             jax.ShapeDtypeStruct((*two, DEPTH, width), bf16),
             jax.ShapeDtypeStruct((*two, DEPTH, width), bf16),
             jax.ShapeDtypeStruct(out_grad.shape, bf16),
+            jax.ShapeDtypeStruct(scale.shape, jnp.float32),
         ],
         scratch_shapes=[
             pltpu.VMEM((4, *out_grad.shape), bf16),
@@ -223,6 +225,7 @@
     left, right = swaps(inward, outward, COL)
     above, below = swaps(masks, masks, ROW)
     sides = jnp.concatenate([left, right], axis=3)
+    sides, kernels = lax.optimization_barrier((sides, kernels))
     above_sides, below_sides = swaps(sides, sides, ROW)
     first = matrix_of(kernels[0, 0])
     second = matrix_of(kernels[0, 1])
@@ -243,7 +246,6 @@
             taken = [received[-1][micro]] if step else []
             result = pl.pallas_call(
                 functools.partial(stage_kernel, micro=micro, reach=reach, narrow=bool(step)),
-                name=f"stage_{step}_{micro}",
                 in_specs=[VMEM] * (4 + len(taken)),
                 out_specs=VMEM,
                 out_shape=jax.ShapeDtypeStruct(
@@ -263,7 +265,6 @@
         field = jax.ShapeDtypeStruct((rows_here + 2, wide, width), bf16)
         ready += pl.pallas_call(
             functools.partial(early_kernel, micro=micro),
-            name=f"early_{micro}",
             in_specs=[SMEM] + [VMEM] * (4 + len(arrived[micro])),
             out_specs=[VMEM] * 3,
             out_shape=[jax.ShapeDtypeStruct(out_grad.shape[1:], bf16), field, field],
@@ -305,5 +306,5 @@
     )
     out_specs = (P("section", None, ROW, COL, None), P("section", None, None, None, None, None))
     return jax.shard_map(
-        on_device, mesh=split, in_specs=in_specs, out_specs=out_specs, check_vma=False
-    )
+        section_backward, mesh=split, in_specs=in_specs, out_specs=out_specs, check_vma=False
+    )

time: 123 us -> 120 us (0.976)
  blocking collectives: 71.8 us -> 70.2 us
  local copies, waits for them, and re-layouts: 2.46 us -> 0.91 us
    all_to_all x2, blocking collectives: 46.4 us -> 44.8 us  [sum_of_blocks(): parts = lax.all_to_all(blocks, axes, 0, 0, tiled=True)]
    ppermute x6, waiting for transfers between devices: 7.17 us -> 8.57 us  [section_backward(): sent.append(lax.ppermute(result, 'section', pair))]
  transfers between devices with their start and end apart: 12 -> 12, of which waited for: 4 -> 3; matrix products, arithmetic and copies ran while one was open for 1% -> 1% of each run, Pallas kernels for 4% -> 4%
where the time goes in v5:
time: 120 us; the launch traced here: 119 us
  blocking collectives  70.2 us (58%)
  starting transfers between devices  25.8 us (22%)
  waiting for transfers between devices  10.4 us (9%)
  Pallas kernels  9.08 us (8%)
  other arithmetic  1.53 us (1%)
    all_to_all x2, blocking collectives, sum_of_blocks(): parts = lax.all_to_all(blocks, axes, 0, 0, tiled=True)  44.8 us
    all_to_all x2, blocking collectives, copies(): lax.all_to_all(jnp.broadcast_to(block[None], (count, *block.shape)), axes...  25.4 us
    ppermute x3, starting transfers between devices, swaps(): close = lax.ppermute(inward, axis, [(i, i ^ 1) for i in range(count)])  12.6 us
    ppermute x6, waiting for transfers between devices, section_backward(): sent.append(lax.ppermute(result, 'section', pair))  8.57 us
    ppermute x3, starting transfers between devices, swaps(): lax.ppermute(outward, axis, crossing + [(j, i) for i, j in crossing])  7.81 us
    pallas_call x6, Pallas kernels, section_backward(): pl.pallas_call(functools.partial(stage_kernel, micro=micro, reach=reach,...  5.51 us
    ppermute x6, starting transfers between devices, section_backward(): sent.append(lax.ppermute(result, 'section', pair))  5.39 us
  transfers between devices with their start and end apart: 12, of which 3 were waited for; matrix products, arithmetic and copies ran while one was open for 1% of the time, Pallas kernels for 4%

profile of v5, /device:TPU:1, one launch (start us, length us, event | category | flops | bytes accessed | tf_op | source)
XLA Modules:
  0.0 119.0 jit_solution(11384379617831723739)
XLA Ops:
  0.7 1.6 %prepare.1 = (bf16[2,2,8,16,128]{4,3,2,1,0:T(8,128)(2,1)S(1)}, bf16[2,2,8,8,128]{4,3,2,1,0:T(8,128)(2,1)S(1)}, bf16[2,2,8,8,128]{4,3,2,1,0:T(8,128)(2,1)S(1)}, b...) custom-call(s32[2]{0:T(128)S(1)} %pad_add_fusion.flags, bf16[2,8,16,128]{3,2,1,0:T(8,128)(2,1)} %bitcast.47, ...), custom_call_target="tpu_custom_call" | custom-call | tf_op jit(solution)/shard_map/prepare/pallas_call | solution.py:200
  2.4 0.7 collective-permute-start
  3.0 6.4 %collective-permute-start.1 = (bf16[2,2,8,8,128]{4,3,2,1,0:T(8,128)(2,1)S(1)}, bf16[2,2,8,8,128]{4,3,2,1,0:T(8,128)(2,1)S(1)}, u32[]{:S(2)}, u32[]{:S(2)}) collective-permute-start(bf16[2,2,8,8,128]{4,3,2,1,0:T(8,128)(2,1)S(1)} %get-tuple-element.15), channel_id=1, source_target_pairs={{0,1},{1,0},{2,3},{3,2},{4,5},{5,4},{6,7},{7,6},{8,9},{9,8},{10,11... | collective-permute-start | bytes 196616 | tf_op jit(solution)/shard_map/ppermute | solution.py:160
  9.4 4.3 %collective-permute-start.5 = (bf16[2,2,8,16,128]{4,3,2,1,0:T(8,128)(2,1)S(1)}, bf16[2,2,8,16,128]{4,3,2,1,0:T(8,128)(2,1)S(1)}, u32[]{:S(2)}, u32[]{:S(2)}) collective-permute-start(bf16[2,2,8,16,128]{4,3,2,1,0:T(8,128)(2,1)S(1)} %get-tuple-element.17), channel_id=1, source_target_pairs={{0,8},{8,0},{16,24},{24,16},{32,40},{40,32},{48,56},{56,48},{64,72... | collective-permute-start | bytes 393224 | tf_op jit(solution)/shard_map/ppermute | solution.py:160
  13.7 2.8 %collective-permute-start.4 = (bf16[2,2,8,16,128]{4,3,2,1,0:T(8,128)(2,1)S(1)}, bf16[2,2,8,16,128]{4,3,2,1,0:T(8,128)(2,1)S(1)}, u32[]{:S(2)}, u32[]{:S(2)}) collective-permute-start(bf16[2,2,8,16,128]{4,3,2,1,0:T(8,128)(2,1)S(1)} %get-tuple-element.17), channel_id=1, source_target_pairs={{8,16},{24,32},{40,48},{56,64},{72,80},{88,96},{104,112},{16,8},{3... | collective-permute-start | bytes 393224 | tf_op jit(solution)/shard_map/ppermute | solution.py:159
  16.6 1.9 %collective-permute-start.3 = (bf16[2,2,8,16,128]{4,3,2,1,0:T(8,128)(2,1)S(1)}, bf16[2,2,8,16,128]{4,3,2,1,0:T(8,128)(2,1)S(1)}, u32[]{:S(2)}, u32[]{:S(2)}) collective-permute-start(bf16[2,2,8,16,128]{4,3,2,1,0:T(8,128)(2,1)S(1)} %pad_maximum_fusion), channel_id=1, source_target_pairs={{0,8},{8,0},{16,24},{24,16},{32,40},{40,32},{48,56},{56,48},{64,72... | collective-permute-start | bytes 393224 | tf_op jit(solution)/shard_map/ppermute | solution.py:160
  18.5 4.4 %collective-permute-start.2 = (bf16[2,2,8,16,128]{4,3,2,1,0:T(8,128)(2,1)S(1)}, bf16[2,2,8,16,128]{4,3,2,1,0:T(8,128)(2,1)S(1)}, u32[]{:S(2)}, u32[]{:S(2)}) collective-permute-start(bf16[2,2,8,16,128]{4,3,2,1,0:T(8,128)(2,1)S(1)} %pad_maximum_fusion), channel_id=1, source_target_pairs={{8,16},{24,32},{40,48},{56,64},{72,80},{88,96},{104,112},{16,8},{3... | collective-permute-start | bytes 393224 | tf_op jit(solution)/shard_map/ppermute | solution.py:159
  23.0 0.2 copy.20
  23.3 0.2 copy.19
  23.7 1.8 %collective-permute-done.2 = bf16[2,2,8,16,128]{4,3,2,1,0:T(8,128)(2,1)S(1)} collective-permute-done((bf16[2,2,8,16,128]{4,3,2,1,0:T(8,128)(2,1)S(1)}, bf16[2,2,8,16,128]{4,3,2,1,0:T(8,128)(2,1)S(1)}, u32[]{:S(2)}, u32[]{:S(2)}) %collective-permute-start.2) | collective-permute-done | bytes 131104 | tf_op jit(solution)/shard_map/ppermute | solution.py:159
  25.6 0.1 maximum_maximum_fusion.refs_0_.refs_1_
  25.7 1.0 shard_map.86
  26.8 0.7 collective-permute-start.6
  27.5 1.0 shard_map.90
  28.5 0.7 collective-permute-start.9
  29.2 0.9 shard_map.87
  30.1 0.7 collective-permute-start.7
  30.8 0.9 shard_map.91
  31.7 0.7 collective-permute-start.10
  32.4 0.8 shard_map.88
  33.2 1.3 %collective-permute-start.8 = (bf16[12,24,128]{2,1,0:T(8,128)(2,1)S(1)}, bf16[12,24,128]{2,1,0:T(8,128)(2,1)S(1)}, u32[]{:S(2)}, u32[]{:S(2)}) collective-permute-start(bf16[12,24,128]{2,1,0:T(8,128)(2,1)S(1)} %shard_map.88), channel_id=1, source_target_pairs={{128,0},{129,1},{130,2},{131,3},{132,4},{133,5},{134,6},{135,7},{1... | collective-permute-start | bytes 221192 | tf_op jit(solution)/shard_map/ppermute | solution.py:258
  34.5 0.8 shard_map.92
  35.3 1.4 %collective-permute-start.11 = (bf16[12,24,128]{2,1,0:T(8,128)(2,1)S(1)}, bf16[12,24,128]{2,1,0:T(8,128)(2,1)S(1)}, u32[]{:S(2)}, u32[]{:S(2)}) collective-permute-start(bf16[12,24,128]{2,1,0:T(8,128)(2,1)S(1)} %shard_map.92), channel_id=1, source_target_pairs={{128,0},{129,1},{130,2},{131,3},{132,4},{133,5},{134,6},{135,7},{1... | collective-permute-start | bytes 221192 | tf_op jit(solution)/shard_map/ppermute | solution.py:258
  36.8 7.1 %collective-permute-done.8.refs_7_ = bf16[12,24,128]{2,1,0:T(8,128)(2,1)S(1)} collective-permute-done((bf16[12,24,128]{2,1,0:T(8,128)(2,1)S(1)}, bf16[12,24,128]{2,1,0:T(8,128)(2,1)S(1)}, u32[]{:S(2)}, u32[]{:S(2)}) %collective-permute-start.8) | collective-permute-done | bytes 73760 | tf_op jit(solution)/shard_map/ppermute | solution.py:258
  43.9 0.6 shard_map.89
  44.5 1.4 %collective-permute-done.11.refs_12_ = bf16[12,24,128]{2,1,0:T(8,128)(2,1)S(1)} collective-permute-done((bf16[12,24,128]{2,1,0:T(8,128)(2,1)S(1)}, bf16[12,24,128]{2,1,0:T(8,128)(2,1)S(1)}, u32[]{:S(2)}, u32[]{:S(2)}) %collective-permute-start.11) | collective-permute-done | bytes 73760 | tf_op jit(solution)/shard_map/ppermute | solution.py:258
  46.0 1.3 %last.1 = (bf16[2,8,16,128]{3,2,1,0:T(8,128)(2,1)}, bf16[2,9,128,128]{3,2,1,0:T(8,128)(2,1)S(1)}) custom-call(s32[1]{0:T(128)} %bitcast.refs_0_, bf16[2,2,24,32,128]{4,3,2,1,0:T(8,128)(2,1)S(1)} %maximum_maximum_fusion.refs_0_.refs_1_, bf16[384,384]{1,0:T(8,128)(2,1)S(1)} %bitcast.45, bf16[384,384]{1,0:T(8,128)(2,1)S(1)} %bitcast.37, ...), custom_call_target="tpu_custom_call" | custom-call | tf_op jit(solution)/shard_map/last/pallas_call | solution.py:275
  47.3 16.7 %all_to_all.20 = bf16[8,288,128]{2,1,0:T(8,128)(2,1)S(1)} all-to-all(bf16[8,288,128]{2,1,0:T(8,128)(2,1)S(1)} %bitcast.46), channel_id=1, replica_groups=mesh['section'=4,'row_0'=8,'row_1'=2,'col_0'=2,'col_1'=4] {'row_1','col_1'}, dimensions={0} | all-to-all | bytes 1179648 | tf_op jit(solution)/shard_map/all_to_all | solution.py:171
  64.1 28.1 %all_to_all.21 = bf16[16,36,128]{2,1,0:T(8,128)(2,1)S(1)} all-to-all(bf16[16,36,128]{2,1,0:T(8,128)(2,1)S(1)} %bitcast.52), channel_id=1, replica_groups=mesh['section'=4,'row_0'=8,'row_1'=2,'col_0'=2,'col_1'=4] {'row_0','col_0'}, dimensions={0} | all-to-all | bytes 294912 | tf_op jit(solution)/shard_map/all_to_all | solution.py:171
  92.3 9.8 %all_to_all.22 = bf16[8,36,128]{2,1,0:T(8,128)(2,1)S(1)} all-to-all(bf16[8,36,128]{2,1,0:T(8,128)(2,1)S(1)} %broadcast_in_dim.26), channel_id=1, replica_groups=mesh['section'=4,'row_0'=8,'row_1'=2,'col_0'=2,'col_1'=4] {'row_0'}, dimensions={0} | all-to-all | bytes 147456 | tf_op jit(solution)/shard_map/all_to_all | solution.py:177
  102.2 15.6 %all_to_all.23 = bf16[8,288,128]{2,1,0:T(8,128)(2,1)S(1)} all-to-all(bf16[8,288,128]{2,1,0:T(8,128)(2,1)S(1)} %broadcast_in_dim.28), channel_id=1, replica_groups=mesh['section'=4,'row_0'=8,'row_1'=2,'col_0'=2,'col_1'=4] {'row_1','col_1'}, dimensions={0} | all-to-all | bytes 1179648 | tf_op jit(solution)/shard_map/all_to_all | solution.py:177
  117.8 1.1 convert.4
  (32 shorter events, 0.7 us)
Async XLA Ops:
  0.6 22.3 %copy-start.1 = (bf16[1,2,3,3,128,128]{5,4,3,2,1,0:T(8,128)(2,1)S(1)}, bf16[1,2,3,3,128,128]{5,4,3,2,1,0:T(8,128)(2,1)}, u32[]{:S(2)}) copy-start(bf16[1,2,3,3,128,128]{5,4,3,2,1,0:T(8,128)(2,1)} %param.11) | copy-start | bytes 1769476
  2.4 14.1 %collective-permute-start = (bf16[2,2,8,8,128]{4,3,2,1,0:T(8,128)(2,1)S(1)}, bf16[2,2,8,8,128]{4,3,2,1,0:T(8,128)(2,1)S(1)}, u32[]{:S(2)}, u32[]{:S(2)}) collective-permute-start(bf16[2,2,8,8,128]{4,3,2,1,0:T(8,128)(2,1)S(1)} %get-tuple-element.14), channel_id=1, source_target_pairs={{1,2},{3,4},{5,6},{2,1},{4,3},{6,5},{9,10},{11,12},{13,14},{10,9},... | collective-permute-start | bytes 196616 | tf_op jit(solution)/shard_map/ppermute | solution.py:159
  3.0 13.5 %collective-permute-start.1 = (bf16[2,2,8,8,128]{4,3,2,1,0:T(8,128)(2,1)S(1)}, bf16[2,2,8,8,128]{4,3,2,1,0:T(8,128)(2,1)S(1)}, u32[]{:S(2)}, u32[]{:S(2)}) collective-permute-start(bf16[2,2,8,8,128]{4,3,2,1,0:T(8,128)(2,1)S(1)} %get-tuple-element.15), channel_id=1, source_target_pairs={{0,1},{1,0},{2,3},{3,2},{4,5},{5,4},{6,7},{7,6},{8,9},{9,8},{10,11... | collective-permute-start | bytes 196616 | tf_op jit(solution)/shard_map/ppermute | solution.py:160
  9.4 14.2 %collective-permute-start.5 = (bf16[2,2,8,16,128]{4,3,2,1,0:T(8,128)(2,1)S(1)}, bf16[2,2,8,16,128]{4,3,2,1,0:T(8,128)(2,1)S(1)}, u32[]{:S(2)}, u32[]{:S(2)}) collective-permute-start(bf16[2,2,8,16,128]{4,3,2,1,0:T(8,128)(2,1)S(1)} %get-tuple-element.17), channel_id=1, source_target_pairs={{0,8},{8,0},{16,24},{24,16},{32,40},{40,32},{48,56},{56,48},{64,72... | collective-permute-start | bytes 393224 | tf_op jit(solution)/shard_map/ppermute | solution.py:160
  13.7 10.0 %collective-permute-start.4 = (bf16[2,2,8,16,128]{4,3,2,1,0:T(8,128)(2,1)S(1)}, bf16[2,2,8,16,128]{4,3,2,1,0:T(8,128)(2,1)S(1)}, u32[]{:S(2)}, u32[]{:S(2)}) collective-permute-start(bf16[2,2,8,16,128]{4,3,2,1,0:T(8,128)(2,1)S(1)} %get-tuple-element.17), channel_id=1, source_target_pairs={{8,16},{24,32},{40,48},{56,64},{72,80},{88,96},{104,112},{16,8},{3... | collective-permute-start | bytes 393224 | tf_op jit(solution)/shard_map/ppermute | solution.py:159
  16.6 7.1 %collective-permute-start.3 = (bf16[2,2,8,16,128]{4,3,2,1,0:T(8,128)(2,1)S(1)}, bf16[2,2,8,16,128]{4,3,2,1,0:T(8,128)(2,1)S(1)}, u32[]{:S(2)}, u32[]{:S(2)}) collective-permute-start(bf16[2,2,8,16,128]{4,3,2,1,0:T(8,128)(2,1)S(1)} %pad_maximum_fusion), channel_id=1, source_target_pairs={{0,8},{8,0},{16,24},{24,16},{32,40},{40,32},{48,56},{56,48},{64,72... | collective-permute-start | bytes 393224 | tf_op jit(solution)/shard_map/ppermute | solution.py:160
  18.5 7.0 %collective-permute-start.2 = (bf16[2,2,8,16,128]{4,3,2,1,0:T(8,128)(2,1)S(1)}, bf16[2,2,8,16,128]{4,3,2,1,0:T(8,128)(2,1)S(1)}, u32[]{:S(2)}, u32[]{:S(2)}) collective-permute-start(bf16[2,2,8,16,128]{4,3,2,1,0:T(8,128)(2,1)S(1)} %pad_maximum_fusion), channel_id=1, source_target_pairs={{8,16},{24,32},{40,48},{56,64},{72,80},{88,96},{104,112},{16,8},{3... | collective-permute-start | bytes 393224 | tf_op jit(solution)/shard_map/ppermute | solution.py:159
  26.8 2.4 %collective-permute-start.6 = (bf16[20,32,128]{2,1,0:T(8,128)(2,1)S(1)}, bf16[20,32,128]{2,1,0:T(8,128)(2,1)S(1)}, u32[]{:S(2)}, u32[]{:S(2)}) collective-permute-start(bf16[20,32,128]{2,1,0:T(8,128)(2,1)S(1)} %shard_map.86), channel_id=1, source_target_pairs={{384,256},{385,257},{386,258},{387,259},{388,260},{389,261},{390,2... | collective-permute-start | bytes 491528 | tf_op jit(solution)/shard_map/ppermute | solution.py:258
  28.5 2.3 %collective-permute-start.9 = (bf16[20,32,128]{2,1,0:T(8,128)(2,1)S(1)}, bf16[20,32,128]{2,1,0:T(8,128)(2,1)S(1)}, u32[]{:S(2)}, u32[]{:S(2)}) collective-permute-start(bf16[20,32,128]{2,1,0:T(8,128)(2,1)S(1)} %shard_map.90), channel_id=1, source_target_pairs={{384,256},{385,257},{386,258},{387,259},{388,260},{389,261},{390,2... | collective-permute-start | bytes 491528 | tf_op jit(solution)/shard_map/ppermute | solution.py:258
  30.1 2.3 %collective-permute-start.7 = (bf16[16,24,128]{2,1,0:T(8,128)(2,1)S(1)}, bf16[16,24,128]{2,1,0:T(8,128)(2,1)S(1)}, u32[]{:S(2)}, u32[]{:S(2)}) collective-permute-start(bf16[16,24,128]{2,1,0:T(8,128)(2,1)S(1)} %shard_map.87), channel_id=1, source_target_pairs={{256,128},{257,129},{258,130},{259,131},{260,132},{261,133},{262,1... | collective-permute-start | bytes 294920 | tf_op jit(solution)/shard_map/ppermute | solution.py:258
  31.7 2.8 %collective-permute-start.10 = (bf16[16,24,128]{2,1,0:T(8,128)(2,1)S(1)}, bf16[16,24,128]{2,1,0:T(8,128)(2,1)S(1)}, u32[]{:S(2)}, u32[]{:S(2)}) collective-permute-start(bf16[16,24,128]{2,1,0:T(8,128)(2,1)S(1)} %shard_map.91), channel_id=1, source_target_pairs={{256,128},{257,129},{258,130},{259,131},{260,132},{261,133},{262,1... | collective-permute-start | bytes 294920 | tf_op jit(solution)/shard_map/ppermute | solution.py:258
  33.2 10.7 %collective-permute-start.8 = (bf16[12,24,128]{2,1,0:T(8,128)(2,1)S(1)}, bf16[12,24,128]{2,1,0:T(8,128)(2,1)S(1)}, u32[]{:S(2)}, u32[]{:S(2)}) collective-permute-start(bf16[12,24,128]{2,1,0:T(8,128)(2,1)S(1)} %shard_map.88), channel_id=1, source_target_pairs={{128,0},{129,1},{130,2},{131,3},{132,4},{133,5},{134,6},{135,7},{1... | collective-permute-start | bytes 221192 | tf_op jit(solution)/shard_map/ppermute | solution.py:258
  35.3 10.6 %copy-start = (bf16[1,2,8,16,128]{4,3,2,1,0:T(8,128)(2,1)S(1)}, bf16[1,2,8,16,128]{4,3,2,1,0:T(8,128)(2,1)}, u32[]{:S(2)}) copy-start(bf16[1,2,8,16,128]{4,3,2,1,0:T(8,128)(2,1)} %param.7) | copy-start | bytes 196612
  35.3 10.6 %collective-permute-start.11 = (bf16[12,24,128]{2,1,0:T(8,128)(2,1)S(1)}, bf16[12,24,128]{2,1,0:T(8,128)(2,1)S(1)}, u32[]{:S(2)}, u32[]{:S(2)}) collective-permute-start(bf16[12,24,128]{2,1,0:T(8,128)(2,1)S(1)} %shard_map.92), channel_id=1, source_target_pairs={{128,0},{129,1},{130,2},{131,3},{132,4},{133,5},{134,6},{135,7},{1... | collective-permute-start | bytes 221192 | tf_op jit(solution)/shard_map/ppermute | solution.py:258

commit v6 on v5

--- a/solution.py
+++ b/solution.py
@@ -223,17 +223,11 @@
         ],
     )
     left, right = swaps(inward, outward, COL)
-    above, below = swaps(masks, masks, ROW)
-    sides = jnp.concatenate([left, right], axis=3)
-    sides, kernels = lax.optimization_barrier((sides, kernels))
-    above_sides, below_sides = swaps(sides, sides, ROW)
+    band = jnp.concatenate([left, masks, right], axis=3)
+    above, below = swaps(band, band, ROW)
     first = matrix_of(kernels[0, 0])
     second = matrix_of(kernels[0, 1])
-    bands = [
-        jnp.concatenate([side[:, :, :, :DEPTH], middle, side[:, :, :, DEPTH:]], axis=3)
-        for side, middle in ((above_sides, above), (sides, masks), (below_sides, below))
-    ]
-    masks = jnp.concatenate(bands, axis=2)
+    masks = jnp.concatenate([above, band, below], axis=2)
     high, wide = masks.shape[2:4]
     frame = pltpu.VMEM((high, wide, width), jnp.float32)
 

time: 120 us -> 120 us (level)
  starting transfers between devices: 25.8 us -> 21.2 us
  blocking collectives: 70.2 us -> 72.9 us
  waiting for transfers between devices: 10.4 us -> 12.6 us
    ppermute x3 -> x2, starting transfers between devices: 7.81 us -> 2.59 us  [swaps(): lax.ppermute(outward, axis, crossing + [(j, i) for i, j in crossing])]
    ppermute x3 -> x2, waiting for transfers between devices: 1.85 us -> 5.03 us  [swaps(): lax.ppermute(outward, axis, crossing + [(j, i) for i, j in crossing])]
    all_to_all x2, blocking collectives: 44.8 us -> 47.5 us  [sum_of_blocks(): parts = lax.all_to_all(blocks, axes, 0, 0, tiled=True)]
    ppermute x6, waiting for transfers between devices: 8.57 us -> 5.97 us  [section_backward(): sent.append(lax.ppermute(result, 'section', pair))]
    ppermute x3 -> x2, waiting for transfers between devices: 0.01 us -> 1.62 us  [swaps(): close = lax.ppermute(inward, axis, [(i, i ^ 1) for i in range(count)])]
    ppermute x3 -> x2, starting transfers between devices: 12.6 us -> 13.3 us  [swaps(): close = lax.ppermute(inward, axis, [(i, i ^ 1) for i in range(count)])]
  transfers between devices with their start and end apart: 12 -> 10, of which waited for: 3 -> 4; matrix products, arithmetic and copies ran while one was open for 1% -> 1% of each run, Pallas kernels for 4% -> 4%
where the time goes in v6:
time: 120 us; the launch traced here: 119 us
  blocking collectives  72.9 us (61%)
  starting transfers between devices  21.2 us (18%)
  waiting for transfers between devices  12.6 us (10%)
  Pallas kernels  9.08 us (8%)
  other arithmetic  1.51 us (1%)
    all_to_all x2, blocking collectives, sum_of_blocks(): parts = lax.all_to_all(blocks, axes, 0, 0, tiled=True)  47.5 us
    all_to_all x2, blocking collectives, copies(): lax.all_to_all(jnp.broadcast_to(block[None], (count, *block.shape)), axes...  25.4 us
    ppermute x2, starting transfers between devices, swaps(): close = lax.ppermute(inward, axis, [(i, i ^ 1) for i in range(count)])  13.3 us
    ppermute x6, waiting for transfers between devices, section_backward(): sent.append(lax.ppermute(result, 'section', pair))  5.97 us
    pallas_call x6, Pallas kernels, section_backward(): pl.pallas_call(functools.partial(stage_kernel, micro=micro, reach=reach,...  5.51 us
    ppermute x6, starting transfers between devices, section_backward(): sent.append(lax.ppermute(result, 'section', pair))  5.39 us
    ppermute x2, waiting for transfers between devices, swaps(): lax.ppermute(outward, axis, crossing + [(j, i) for i, j in crossing])  5.03 us
    ppermute x2, starting transfers between devices, swaps(): lax.ppermute(outward, axis, crossing + [(j, i) for i, j in crossing])  2.59 us
  transfers between devices with their start and end apart: 10, of which 4 were waited for; matrix products, arithmetic and copies ran while one was open for 1% of the time, Pallas kernels for 4%

profile of v6, /device:TPU:1, one launch (start us, length us, event | category | flops | bytes accessed | tf_op | source)
XLA Modules:
  0.0 119.1 jit_solution(17191707482367822134)
XLA Ops:
  0.7 1.6 %prepare.1 = (bf16[2,2,8,16,128]{4,3,2,1,0:T(8,128)(2,1)S(1)}, bf16[2,2,8,8,128]{4,3,2,1,0:T(8,128)(2,1)S(1)}, bf16[2,2,8,8,128]{4,3,2,1,0:T(8,128)(2,1)S(1)}, b...) custom-call(s32[2]{0:T(128)S(1)} %pad_add_fusion.flags, bf16[2,8,16,128]{3,2,1,0:T(8,128)(2,1)} %bitcast.47, ...), custom_call_target="tpu_custom_call" | custom-call | tf_op jit(solution)/shard_map/prepare/pallas_call | solution.py:200
  2.4 0.7 collective-permute-start
  3.0 6.4 %collective-permute-start.1 = (bf16[2,2,8,8,128]{4,3,2,1,0:T(8,128)(2,1)S(1)}, bf16[2,2,8,8,128]{4,3,2,1,0:T(8,128)(2,1)S(1)}, u32[]{:S(2)}, u32[]{:S(2)}) collective-permute-start(bf16[2,2,8,8,128]{4,3,2,1,0:T(8,128)(2,1)S(1)} %get-tuple-element.13), channel_id=1, source_target_pairs={{0,1},{1,0},{2,3},{3,2},{4,5},{5,4},{6,7},{7,6},{8,9},{9,8},{10,11... | collective-permute-start | bytes 196616 | tf_op jit(solution)/shard_map/ppermute | solution.py:160
  9.4 1.6 %collective-permute-done.1 = bf16[2,2,8,8,128]{4,3,2,1,0:T(8,128)(2,1)S(1)} collective-permute-done((bf16[2,2,8,8,128]{4,3,2,1,0:T(8,128)(2,1)S(1)}, bf16[2,2,8,8,128]{4,3,2,1,0:T(8,128)(2,1)S(1)}, u32[]{:S(2)}, u32[]{:S(2)}) %collective-permute-start.1) | collective-permute-done | bytes 65568 | tf_op jit(solution)/shard_map/ppermute | solution.py:160
  11.1 6.9 %collective-permute-start.3 = (bf16[2,2,8,32,128]{4,3,2,1,0:T(8,128)(2,1)S(1)}, bf16[2,2,8,32,128]{4,3,2,1,0:T(8,128)(2,1)S(1)}, u32[]{:S(2)}, u32[]{:S(2)}) collective-permute-start(bf16[2,2,8,32,128]{4,3,2,1,0:T(8,128)(2,1)S(1)} %pad_maximum_fusion.1), channel_id=1, source_target_pairs={{0,8},{8,0},{16,24},{24,16},{32,40},{40,32},{48,56},{56,48},{64,72... | collective-permute-start | bytes 786440 | tf_op jit(solution)/shard_map/ppermute | solution.py:160
  18.0 1.9 %collective-permute-start.2 = (bf16[2,2,8,32,128]{4,3,2,1,0:T(8,128)(2,1)S(1)}, bf16[2,2,8,32,128]{4,3,2,1,0:T(8,128)(2,1)S(1)}, u32[]{:S(2)}, u32[]{:S(2)}) collective-permute-start(bf16[2,2,8,32,128]{4,3,2,1,0:T(8,128)(2,1)S(1)} %pad_maximum_fusion.1), channel_id=1, source_target_pairs={{8,16},{24,32},{40,48},{56,64},{72,80},{88,96},{104,112},{16,8},{3... | collective-permute-start | bytes 786440 | tf_op jit(solution)/shard_map/ppermute | solution.py:159
  20.0 0.2 copy.20
  20.3 0.2 copy.19
  20.7 5.0 %collective-permute-done.2 = bf16[2,2,8,32,128]{4,3,2,1,0:T(8,128)(2,1)S(1)} collective-permute-done((bf16[2,2,8,32,128]{4,3,2,1,0:T(8,128)(2,1)S(1)}, bf16[2,2,8,32,128]{4,3,2,1,0:T(8,128)(2,1)S(1)}, u32[]{:S(2)}, u32[]{:S(2)}) %collective-permute-start.2) | collective-permute-done | bytes 262176 | tf_op jit(solution)/shard_map/ppermute | solution.py:159
  25.8 1.0 shard_map.86
  26.8 0.7 collective-permute-start.4
  27.5 1.0 shard_map.90
  28.6 0.7 collective-permute-start.7
  29.2 0.9 shard_map.87
  30.2 0.7 collective-permute-start.5
  30.9 0.9 shard_map.91
  31.8 0.7 collective-permute-start.8
  32.5 0.8 shard_map.88
  33.3 1.3 %collective-permute-start.6 = (bf16[12,24,128]{2,1,0:T(8,128)(2,1)S(1)}, bf16[12,24,128]{2,1,0:T(8,128)(2,1)S(1)}, u32[]{:S(2)}, u32[]{:S(2)}) collective-permute-start(bf16[12,24,128]{2,1,0:T(8,128)(2,1)S(1)} %shard_map.88), channel_id=1, source_target_pairs={{128,0},{129,1},{130,2},{131,3},{132,4},{133,5},{134,6},{135,7},{1... | collective-permute-start | bytes 221192 | tf_op jit(solution)/shard_map/ppermute | solution.py:252
  34.6 0.8 shard_map.92
  35.4 1.4 %collective-permute-start.9 = (bf16[12,24,128]{2,1,0:T(8,128)(2,1)S(1)}, bf16[12,24,128]{2,1,0:T(8,128)(2,1)S(1)}, u32[]{:S(2)}, u32[]{:S(2)}) collective-permute-start(bf16[12,24,128]{2,1,0:T(8,128)(2,1)S(1)} %shard_map.92), channel_id=1, source_target_pairs={{128,0},{129,1},{130,2},{131,3},{132,4},{133,5},{134,6},{135,7},{1... | collective-permute-start | bytes 221192 | tf_op jit(solution)/shard_map/ppermute | solution.py:252
  36.8 4.1 %collective-permute-done.6.refs_7_ = bf16[12,24,128]{2,1,0:T(8,128)(2,1)S(1)} collective-permute-done((bf16[12,24,128]{2,1,0:T(8,128)(2,1)S(1)}, bf16[12,24,128]{2,1,0:T(8,128)(2,1)S(1)}, u32[]{:S(2)}, u32[]{:S(2)}) %collective-permute-start.6) | collective-permute-done | bytes 73760 | tf_op jit(solution)/shard_map/ppermute | solution.py:252
  40.9 0.6 shard_map.89
  41.6 1.9 %collective-permute-done.9.refs_12_ = bf16[12,24,128]{2,1,0:T(8,128)(2,1)S(1)} collective-permute-done((bf16[12,24,128]{2,1,0:T(8,128)(2,1)S(1)}, bf16[12,24,128]{2,1,0:T(8,128)(2,1)S(1)}, u32[]{:S(2)}, u32[]{:S(2)}) %collective-permute-start.9) | collective-permute-done | bytes 73760 | tf_op jit(solution)/shard_map/ppermute | solution.py:252
  43.4 1.3 %last.1 = (bf16[2,8,16,128]{3,2,1,0:T(8,128)(2,1)}, bf16[2,9,128,128]{3,2,1,0:T(8,128)(2,1)S(1)}) custom-call(s32[1]{0:T(128)} %bitcast.refs_0_, bf16[2,2,24,32,128]{4,3,2,1,0:T(8,128)(2,1)S(1)} %pad_maximum_fusion.refs_0_.refs_1_, bf16[384,384]{1,0:T(8,128)(2,1)S(1)} %bitcast.45, bf16[384,384]{1,0:T(8,128)(2,1)S(1)} %bitcast.37, ...), custom_call_target="tpu_custom_call" | custom-call | tf_op jit(solution)/shard_map/last/pallas_call | solution.py:269
  44.8 18.2 %all_to_all.20 = bf16[8,288,128]{2,1,0:T(8,128)(2,1)S(1)} all-to-all(bf16[8,288,128]{2,1,0:T(8,128)(2,1)S(1)} %bitcast.46), channel_id=1, replica_groups=mesh['section'=4,'row_0'=8,'row_1'=2,'col_0'=2,'col_1'=4] {'row_1','col_1'}, dimensions={0} | all-to-all | bytes 1179648 | tf_op jit(solution)/shard_map/all_to_all | solution.py:171
  62.9 0.1 reduce_sum.21
  63.1 29.3 %all_to_all.21 = bf16[16,36,128]{2,1,0:T(8,128)(2,1)S(1)} all-to-all(bf16[16,36,128]{2,1,0:T(8,128)(2,1)S(1)} %bitcast.52), channel_id=1, replica_groups=mesh['section'=4,'row_0'=8,'row_1'=2,'col_0'=2,'col_1'=4] {'row_0','col_0'}, dimensions={0} | all-to-all | bytes 294912 | tf_op jit(solution)/shard_map/all_to_all | solution.py:171
  92.5 9.8 %all_to_all.22 = bf16[8,36,128]{2,1,0:T(8,128)(2,1)S(1)} all-to-all(bf16[8,36,128]{2,1,0:T(8,128)(2,1)S(1)} %broadcast_in_dim.26), channel_id=1, replica_groups=mesh['section'=4,'row_0'=8,'row_1'=2,'col_0'=2,'col_1'=4] {'row_0'}, dimensions={0} | all-to-all | bytes 147456 | tf_op jit(solution)/shard_map/all_to_all | solution.py:177
  102.3 0.1 broadcast_in_dim.28
  102.4 15.6 %all_to_all.23 = bf16[8,288,128]{2,1,0:T(8,128)(2,1)S(1)} all-to-all(bf16[8,288,128]{2,1,0:T(8,128)(2,1)S(1)} %broadcast_in_dim.28), channel_id=1, replica_groups=mesh['section'=4,'row_0'=8,'row_1'=2,'col_0'=2,'col_1'=4] {'row_1','col_1'}, dimensions={0} | all-to-all | bytes 1179648 | tf_op jit(solution)/shard_map/all_to_all | solution.py:177
  118.0 1.1 convert.4
  (25 shorter events, 0.6 us)
Async XLA Ops:
  0.6 19.3 %copy-start.1 = (bf16[1,2,3,3,128,128]{5,4,3,2,1,0:T(8,128)(2,1)S(1)}, bf16[1,2,3,3,128,128]{5,4,3,2,1,0:T(8,128)(2,1)}, u32[]{:S(2)}) copy-start(bf16[1,2,3,3,128,128]{5,4,3,2,1,0:T(8,128)(2,1)} %param.11) | copy-start | bytes 1769476
  2.4 7.1 %collective-permute-start = (bf16[2,2,8,8,128]{4,3,2,1,0:T(8,128)(2,1)S(1)}, bf16[2,2,8,8,128]{4,3,2,1,0:T(8,128)(2,1)S(1)}, u32[]{:S(2)}, u32[]{:S(2)}) collective-permute-start(bf16[2,2,8,8,128]{4,3,2,1,0:T(8,128)(2,1)S(1)} %get-tuple-element.12), channel_id=1, source_target_pairs={{1,2},{3,4},{5,6},{2,1},{4,3},{6,5},{9,10},{11,12},{13,14},{10,9},... | collective-permute-start | bytes 196616 | tf_op jit(solution)/shard_map/ppermute | solution.py:159
  3.0 8.0 %collective-permute-start.1 = (bf16[2,2,8,8,128]{4,3,2,1,0:T(8,128)(2,1)S(1)}, bf16[2,2,8,8,128]{4,3,2,1,0:T(8,128)(2,1)S(1)}, u32[]{:S(2)}, u32[]{:S(2)}) collective-permute-start(bf16[2,2,8,8,128]{4,3,2,1,0:T(8,128)(2,1)S(1)} %get-tuple-element.13), channel_id=1, source_target_pairs={{0,1},{1,0},{2,3},{3,2},{4,5},{5,4},{6,7},{7,6},{8,9},{9,8},{10,11... | collective-permute-start | bytes 196616 | tf_op jit(solution)/shard_map/ppermute | solution.py:160
  11.1 9.5 %collective-permute-start.3 = (bf16[2,2,8,32,128]{4,3,2,1,0:T(8,128)(2,1)S(1)}, bf16[2,2,8,32,128]{4,3,2,1,0:T(8,128)(2,1)S(1)}, u32[]{:S(2)}, u32[]{:S(2)}) collective-permute-start(bf16[2,2,8,32,128]{4,3,2,1,0:T(8,128)(2,1)S(1)} %pad_maximum_fusion.1), channel_id=1, source_target_pairs={{0,8},{8,0},{16,24},{24,16},{32,40},{40,32},{48,56},{56,48},{64,72... | collective-permute-start | bytes 786440 | tf_op jit(solution)/shard_map/ppermute | solution.py:160
  18.0 7.7 %collective-permute-start.2 = (bf16[2,2,8,32,128]{4,3,2,1,0:T(8,128)(2,1)S(1)}, bf16[2,2,8,32,128]{4,3,2,1,0:T(8,128)(2,1)S(1)}, u32[]{:S(2)}, u32[]{:S(2)}) collective-permute-start(bf16[2,2,8,32,128]{4,3,2,1,0:T(8,128)(2,1)S(1)} %pad_maximum_fusion.1), channel_id=1, source_target_pairs={{8,16},{24,32},{40,48},{56,64},{72,80},{88,96},{104,112},{16,8},{3... | collective-permute-start | bytes 786440 | tf_op jit(solution)/shard_map/ppermute | solution.py:159
  26.8 2.4 %collective-permute-start.4 = (bf16[20,32,128]{2,1,0:T(8,128)(2,1)S(1)}, bf16[20,32,128]{2,1,0:T(8,128)(2,1)S(1)}, u32[]{:S(2)}, u32[]{:S(2)}) collective-permute-start(bf16[20,32,128]{2,1,0:T(8,128)(2,1)S(1)} %shard_map.86), channel_id=1, source_target_pairs={{384,256},{385,257},{386,258},{387,259},{388,260},{389,261},{390,2... | collective-permute-start | bytes 491528 | tf_op jit(solution)/shard_map/ppermute | solution.py:252
  28.6 2.3 %collective-permute-start.7 = (bf16[20,32,128]{2,1,0:T(8,128)(2,1)S(1)}, bf16[20,32,128]{2,1,0:T(8,128)(2,1)S(1)}, u32[]{:S(2)}, u32[]{:S(2)}) collective-permute-start(bf16[20,32,128]{2,1,0:T(8,128)(2,1)S(1)} %shard_map.90), channel_id=1, source_target_pairs={{384,256},{385,257},{386,258},{387,259},{388,260},{389,261},{390,2... | collective-permute-start | bytes 491528 | tf_op jit(solution)/shard_map/ppermute | solution.py:252
  30.2 2.3 %collective-permute-start.5 = (bf16[16,24,128]{2,1,0:T(8,128)(2,1)S(1)}, bf16[16,24,128]{2,1,0:T(8,128)(2,1)S(1)}, u32[]{:S(2)}, u32[]{:S(2)}) collective-permute-start(bf16[16,24,128]{2,1,0:T(8,128)(2,1)S(1)} %shard_map.87), channel_id=1, source_target_pairs={{256,128},{257,129},{258,130},{259,131},{260,132},{261,133},{262,1... | collective-permute-start | bytes 294920 | tf_op jit(solution)/shard_map/ppermute | solution.py:252
  31.8 2.8 %collective-permute-start.8 = (bf16[16,24,128]{2,1,0:T(8,128)(2,1)S(1)}, bf16[16,24,128]{2,1,0:T(8,128)(2,1)S(1)}, u32[]{:S(2)}, u32[]{:S(2)}) collective-permute-start(bf16[16,24,128]{2,1,0:T(8,128)(2,1)S(1)} %shard_map.91), channel_id=1, source_target_pairs={{256,128},{257,129},{258,130},{259,131},{260,132},{261,133},{262,1... | collective-permute-start | bytes 294920 | tf_op jit(solution)/shard_map/ppermute | solution.py:252
  33.3 7.7 %collective-permute-start.6 = (bf16[12,24,128]{2,1,0:T(8,128)(2,1)S(1)}, bf16[12,24,128]{2,1,0:T(8,128)(2,1)S(1)}, u32[]{:S(2)}, u32[]{:S(2)}) collective-permute-start(bf16[12,24,128]{2,1,0:T(8,128)(2,1)S(1)} %shard_map.88), channel_id=1, source_target_pairs={{128,0},{129,1},{130,2},{131,3},{132,4},{133,5},{134,6},{135,7},{1... | collective-permute-start | bytes 221192 | tf_op jit(solution)/shard_map/ppermute | solution.py:252
  35.4 8.0 %copy-start = (bf16[1,2,8,16,128]{4,3,2,1,0:T(8,128)(2,1)S(1)}, bf16[1,2,8,16,128]{4,3,2,1,0:T(8,128)(2,1)}, u32[]{:S(2)}) copy-start(bf16[1,2,8,16,128]{4,3,2,1,0:T(8,128)(2,1)} %param.7) | copy-start | bytes 196612
  35.4 8.0 %collective-permute-start.9 = (bf16[12,24,128]{2,1,0:T(8,128)(2,1)S(1)}, bf16[12,24,128]{2,1,0:T(8,128)(2,1)S(1)}, u32[]{:S(2)}, u32[]{:S(2)}) collective-permute-start(bf16[12,24,128]{2,1,0:T(8,128)(2,1)S(1)} %shard_map.92), channel_id=1, source_target_pairs={{128,0},{129,1},{130,2},{131,3},{132,4},{133,5},{134,6},{135,7},{1... | collective-permute-start | bytes 221192 | tf_op jit(solution)/shard_map/ppermute | solution.py:252

commit v7 on v5

--- a/solution.py
+++ b/solution.py
@@ -19,6 +19,7 @@
 
 DEPTH = 8
 NARROW = 4
+PACKED = 2
 
 
 def prepare_kernel(flags, *refs):
@@ -74,24 +75,53 @@
     return (result, first_grad, second_grad)
 
 
+def packed(cells, pairs, pack, cut):
+    rows, cols, width = cells.shape
+    half = rows // 2
+    kept = cols - 2 * cut
+    pairs[:half] = cells.reshape(half, 2, cols, width)
+    for k in range(2):
+        pack[:half, k * kept : (k + 1) * kept] = pairs[:half, k, cut : cut + kept]
+    return pack[:half]
+
+
+def unpacked(cells, pairs, pack, skip):
+    half = cells.shape[0] - skip
+    kept = cells.shape[1] // 2
+    cols = pairs.shape[2]
+    cut = (cols - kept) // 2
+    pack[:half] = cells[skip // 2 : skip // 2 + half].astype(jnp.float32)
+    pairs[:half] = jnp.zeros((half, *pairs.shape[1:]), jnp.float32)
+    for k in range(2):
+        pairs[:half, k, cut : cut + kept] = pack[:half, k * kept : (k + 1) * kept]
+    return pairs[:half].reshape(2 * half, cols, pairs.shape[3])
+
+
 def widened(cells, frame, skip):
     rows = cells.shape[0] - 2 * skip
     value = cells[skip : skip + rows].astype(jnp.float32)
-    if cells.shape[1] == frame.shape[1]:
-        return value
     frame[:rows] = jnp.zeros((rows, *frame.shape[1:]), jnp.float32)
     frame[:rows, NARROW : frame.shape[1] - NARROW] = value
     return frame[:rows]
 
 
-def stage_kernel(*refs, micro, reach, narrow):
-    masks, first, second, scale, *received, out, frame = refs
-    incoming = widened(received[0], frame, 0) if received else None
-    result, _, _ = unit(masks, micro, incoming, first, second, scale, reach)
-    if narrow:
-        frame[: result.shape[0]] = result
-        result = frame[: result.shape[0], NARROW : result.shape[1] - NARROW]
-    out[...] = result.astype(jnp.bfloat16)
+def stage_kernel(*refs, micro, step, reach):
+    active, masks, first, second, scale, *received, out, frame, pairs, pack = refs
+
+    @pl.when(active[0] > 0)
+    def _():
+        incoming = None
+        if step == 1:
+            incoming = unpacked(received[0], pairs, pack, 0)
+        elif step > 1:
+            incoming = widened(received[0], frame, 0)
+        result, _, _ = unit(masks, micro, incoming, first, second, scale, reach)
+        if step:
+            frame[: result.shape[0]] = result
+            result = frame[: result.shape[0], NARROW : result.shape[1] - NARROW]
+        else:
+            result = packed(result, pairs, pack, PACKED)
+        out[...] = result.astype(jnp.bfloat16)
 
 
 def filter_grad(cells, windows):
@@ -120,30 +150,37 @@
     )
 
 
-def settle(last, masks, micro, received, first, second, scale, frame):
+def settle(last, masks, micro, received, first, second, scale, frame, pairs, pack):
     incoming = jnp.where(last[0] > 0, 1.0, 0.0)
     steps = len(received)
     for step, cells in enumerate(received):
-        incoming = incoming + widened(cells, frame.at[step], 2 * (steps - 1 - step))
+        skip = 2 * (steps - 1 - step)
+        if step:
+            incoming = incoming + widened(cells, frame.at[step], skip)
+        else:
+            incoming = incoming + unpacked(cells, pairs, pack, skip)
     result, first_grad, second_grad = unit(masks, micro, incoming, first, second, scale, 0)
     tile = result[:, DEPTH : result.shape[1] - DEPTH].astype(jnp.bfloat16)
     return (tile, first_grad, second_grad[1:-1])
 
 
 def early_kernel(*refs, micro):
-    last, masks, first, second, scale, *received, tile, first_grad, second_grad, frame = refs
-    values = settle(last, masks, micro, received, first, second, scale, frame)
-    for ref, value in zip((tile, first_grad, second_grad), values):
+    last, masks, first, second, scale, *received = refs
+    *outs, frame, pairs, pack = received[-6:]
+    received = received[:-6]
+    values = settle(last, masks, micro, received, first, second, scale, frame, pairs, pack)
+    for ref, value in zip(outs, values):
         ref[...] = value
 
 
 def last_kernel(*refs, micros, early):
     last, masks, first, second, scale, inputs, act, *rest = refs
-    out, partial, frame = rest[-3:]
+    out, partial, frame, pairs, pack = rest[-5:]
     ready = rest[: 3 * early]
-    received = rest[3 * early : -3]
+    received = rest[3 * early : -5]
     units = [[ref[...] for ref in ready[3 * m : 3 * m + 3]] for m in range(early)]
-    units.append(settle(last, masks, micros - 1, received, first, second, scale, frame))
+    scratch = (frame, pairs, pack)
+    units.append(settle(last, masks, micros - 1, received, first, second, scale, *scratch))
     for micro, (tile, _, _) in enumerate(units):
         out[micro] = tile
     width = scale.shape[1]
@@ -235,29 +272,34 @@
     ]
     masks = jnp.concatenate(bands, axis=2)
     high, wide = masks.shape[2:4]
-    frame = pltpu.VMEM((high, wide, width), jnp.float32)
+    pairs = [
+        pltpu.VMEM((high // 2, 2, wide, width), jnp.float32),
+        pltpu.VMEM((high // 2, 2 * (wide - 2 * PACKED), width), jnp.float32),
+    ]
 
     received = [[]]
     for step in range(sections - 1):
         reach = 2 * (sections - 1 - step)
-        narrow = NARROW if step else 0
+        rows = rows_here + 2 * reach
+        shape = (rows, wide - 2 * NARROW, width)
+        if step == 0:
+            shape = (rows // 2, 2 * (wide - 2 * PACKED), width)
+        active = (lax.axis_index("section") == sections - 1 - step).astype(jnp.int32).reshape(1)
         sent = []
         for micro in range(micros):
             taken = [received[-1][micro]] if step else []
             result = pl.pallas_call(
-                functools.partial(stage_kernel, micro=micro, reach=reach, narrow=bool(step)),
-                in_specs=[VMEM] * (4 + len(taken)),
+                functools.partial(stage_kernel, micro=micro, step=step, reach=reach),
+                in_specs=[SMEM] + [VMEM] * (4 + len(taken)),
                 out_specs=VMEM,
-                out_shape=jax.ShapeDtypeStruct(
-                    (rows_here + 2 * reach, wide - 2 * narrow, width), bf16
-                ),
-                scratch_shapes=[frame],
+                out_shape=jax.ShapeDtypeStruct(shape, bf16),
+                scratch_shapes=[pltpu.VMEM((high, wide, width), jnp.float32)] + pairs,
                 compiler_params=PARAMS,
-            )(masks, first, second, scale, *taken)
+            )(active, masks, first, second, scale, *taken)
             pair = [(sections - 1 - step, sections - 2 - step)]
             sent.append(lax.ppermute(result, "section", pair))
         received.append(sent)
-    frames = pltpu.VMEM((sections - 1, high, wide, width), jnp.float32)
+    scratch = [pltpu.VMEM((sections - 1, high, wide, width), jnp.float32)] + pairs
     common = (last, masks, first, second, scale)
     arrived = [[step[micro] for step in received[1:]] for micro in range(micros)]
     ready = []
@@ -268,7 +310,7 @@
             in_specs=[SMEM] + [VMEM] * (4 + len(arrived[micro])),
             out_specs=[VMEM] * 3,
             out_shape=[jax.ShapeDtypeStruct(out_grad.shape[1:], bf16), field, field],
-            scratch_shapes=[frames],
+            scratch_shapes=scratch,
             compiler_params=PARAMS,
         )(*common, *arrived[micro])
     taken = ready + arrived[-1]
@@ -281,7 +323,7 @@
             jax.ShapeDtypeStruct(out_grad.shape, bf16),
             jax.ShapeDtypeStruct((2, 9, width, width), bf16),
         ],
-        scratch_shapes=[frames],
+        scratch_shapes=scratch,
         compiler_params=PARAMS,
     )(*common, section_input[0], act, *taken)
     pixels = micros * rows_here * lax.axis_size(ROW) * cols_here * lax.axis_size(COL)

time: 120 us -> 117 us (0.975)
  Pallas kernels: 9.08 us -> 3.69 us
  waiting for transfers between devices: 10.4 us -> 15 us
  blocking collectives: 70.2 us -> 68.9 us
    pallas_call x6, Pallas kernels: 5.51 us -> 0.06 us  [section_backward(): pl.pallas_call(functools.partial(stage_kernel, micro=micro, step=step, re...]
    ppermute x6, waiting for transfers between devices: 8.57 us -> 13.1 us  [section_backward(): sent.append(lax.ppermute(result, 'section', pair))]
    all_to_all x2, blocking collectives: 44.8 us -> 43.5 us  [sum_of_blocks(): parts = lax.all_to_all(blocks, axes, 0, 0, tiled=True)]
  transfers between devices with their start and end apart: 12 -> 12, of which waited for: 3 -> 3; matrix products, arithmetic and copies ran while one was open for 1% -> 1% of each run, Pallas kernels for 4% -> 1%
where the time goes in v7:
time: 117 us
  blocking collectives  68.9 us (59%)
  starting transfers between devices  25.8 us (22%)
  waiting for transfers between devices  15 us (13%)
  Pallas kernels  3.69 us (3%)
  other arithmetic  1.53 us (1%)
    all_to_all x2, blocking collectives, sum_of_blocks(): parts = lax.all_to_all(blocks, axes, 0, 0, tiled=True)  43.5 us
    all_to_all x2, blocking collectives, copies(): lax.all_to_all(jnp.broadcast_to(block[None], (count, *block.shape)), axes...  25.4 us
    ppermute x6, waiting for transfers between devices, section_backward(): sent.append(lax.ppermute(result, 'section', pair))  13.1 us
    ppermute x3, starting transfers between devices, swaps(): close = lax.ppermute(inward, axis, [(i, i ^ 1) for i in range(count)])  12.6 us
    ppermute x3, starting transfers between devices, swaps(): lax.ppermute(outward, axis, crossing + [(j, i) for i, j in crossing])  7.81 us
    ppermute x6, starting transfers between devices, section_backward(): sent.append(lax.ppermute(result, 'section', pair))  5.39 us
  transfers between devices with their start and end apart: 12, of which 3 were waited for; matrix products, arithmetic and copies ran while one was open for 1% of the time, Pallas kernels for 1%

profile of v7, /device:TPU:1, one launch (start us, length us, event | category | flops | bytes accessed | tf_op | source)
XLA Modules:
  0.0 116.8 jit_solution(13846086608733233913)
XLA Ops:
  0.7 0.1 pad_add_fusion.flags
  0.7 1.6 %prepare.1 = (bf16[2,2,8,16,128]{4,3,2,1,0:T(8,128)(2,1)S(1)}, bf16[2,2,8,8,128]{4,3,2,1,0:T(8,128)(2,1)S(1)}, bf16[2,2,8,8,128]{4,3,2,1,0:T(8,128)(2,1)S(1)}, b...) custom-call(s32[2]{0:T(128)S(1)} %pad_add_fusion.flags, bf16[2,8,16,128]{3,2,1,0:T(8,128)(2,1)} %bitcast.49, ...), custom_call_target="tpu_custom_call" | custom-call | tf_op jit(solution)/shard_map/prepare/pallas_call | solution.py:237
  2.4 0.7 collective-permute-start
  3.0 6.4 %collective-permute-start.1 = (bf16[2,2,8,8,128]{4,3,2,1,0:T(8,128)(2,1)S(1)}, bf16[2,2,8,8,128]{4,3,2,1,0:T(8,128)(2,1)S(1)}, u32[]{:S(2)}, u32[]{:S(2)}) collective-permute-start(bf16[2,2,8,8,128]{4,3,2,1,0:T(8,128)(2,1)S(1)} %get-tuple-element.15), channel_id=1, source_target_pairs={{0,1},{1,0},{2,3},{3,2},{4,5},{5,4},{6,7},{7,6},{8,9},{9,8},{10,11... | collective-permute-start | bytes 196616 | tf_op jit(solution)/shard_map/ppermute | solution.py:197
  9.4 4.3 %collective-permute-start.5 = (bf16[2,2,8,16,128]{4,3,2,1,0:T(8,128)(2,1)S(1)}, bf16[2,2,8,16,128]{4,3,2,1,0:T(8,128)(2,1)S(1)}, u32[]{:S(2)}, u32[]{:S(2)}) collective-permute-start(bf16[2,2,8,16,128]{4,3,2,1,0:T(8,128)(2,1)S(1)} %get-tuple-element.17), channel_id=1, source_target_pairs={{0,8},{8,0},{16,24},{24,16},{32,40},{40,32},{48,56},{56,48},{64,72... | collective-permute-start | bytes 393224 | tf_op jit(solution)/shard_map/ppermute | solution.py:197
  13.7 2.8 %collective-permute-start.4 = (bf16[2,2,8,16,128]{4,3,2,1,0:T(8,128)(2,1)S(1)}, bf16[2,2,8,16,128]{4,3,2,1,0:T(8,128)(2,1)S(1)}, u32[]{:S(2)}, u32[]{:S(2)}) collective-permute-start(bf16[2,2,8,16,128]{4,3,2,1,0:T(8,128)(2,1)S(1)} %get-tuple-element.17), channel_id=1, source_target_pairs={{8,16},{24,32},{40,48},{56,64},{72,80},{88,96},{104,112},{16,8},{3... | collective-permute-start | bytes 393224 | tf_op jit(solution)/shard_map/ppermute | solution.py:196
  16.6 1.9 %collective-permute-start.3 = (bf16[2,2,8,16,128]{4,3,2,1,0:T(8,128)(2,1)S(1)}, bf16[2,2,8,16,128]{4,3,2,1,0:T(8,128)(2,1)S(1)}, u32[]{:S(2)}, u32[]{:S(2)}) collective-permute-start(bf16[2,2,8,16,128]{4,3,2,1,0:T(8,128)(2,1)S(1)} %pad_maximum_fusion), channel_id=1, source_target_pairs={{0,8},{8,0},{16,24},{24,16},{32,40},{40,32},{48,56},{56,48},{64,72... | collective-permute-start | bytes 393224 | tf_op jit(solution)/shard_map/ppermute | solution.py:197
  18.5 4.4 %collective-permute-start.2 = (bf16[2,2,8,16,128]{4,3,2,1,0:T(8,128)(2,1)S(1)}, bf16[2,2,8,16,128]{4,3,2,1,0:T(8,128)(2,1)S(1)}, u32[]{:S(2)}, u32[]{:S(2)}) collective-permute-start(bf16[2,2,8,16,128]{4,3,2,1,0:T(8,128)(2,1)S(1)} %pad_maximum_fusion), channel_id=1, source_target_pairs={{8,16},{24,32},{40,48},{56,64},{72,80},{88,96},{104,112},{16,8},{3... | collective-permute-start | bytes 393224 | tf_op jit(solution)/shard_map/ppermute | solution.py:196
  23.0 0.2 copy.20
  23.3 0.2 copy.19
  23.7 0.0 collective-permute-done.4
  23.7 0.0 collective-permute-done.3
  23.7 1.8 %collective-permute-done.2 = bf16[2,2,8,16,128]{4,3,2,1,0:T(8,128)(2,1)S(1)} collective-permute-done((bf16[2,2,8,16,128]{4,3,2,1,0:T(8,128)(2,1)S(1)}, bf16[2,2,8,16,128]{4,3,2,1,0:T(8,128)(2,1)S(1)}, u32[]{:S(2)}, u32[]{:S(2)}) %collective-permute-start.2) | collective-permute-done | bytes 131104 | tf_op jit(solution)/shard_map/ppermute | solution.py:196
  25.6 0.1 maximum_maximum_fusion.refs_1_
  25.8 0.7 collective-permute-start.6
  26.5 0.7 collective-permute-start.9
  27.2 0.7 collective-permute-start.7
  27.9 0.7 collective-permute-start.10
  28.6 1.3 %collective-permute-start.8 = (bf16[12,24,128]{2,1,0:T(8,128)(2,1)S(1)}, bf16[12,24,128]{2,1,0:T(8,128)(2,1)S(1)}, u32[]{:S(2)}, u32[]{:S(2)}) collective-permute-start(bf16[12,24,128]{2,1,0:T(8,128)(2,1)S(1)} %shard_map.88), channel_id=1, source_target_pairs={{128,0},{129,1},{130,2},{131,3},{132,4},{133,5},{134,6},{135,7},{1... | collective-permute-start | bytes 221192 | tf_op jit(solution)/shard_map/ppermute | solution.py:300
  29.9 0.0 copy-start
  29.9 1.4 %collective-permute-start.11 = (bf16[12,24,128]{2,1,0:T(8,128)(2,1)S(1)}, bf16[12,24,128]{2,1,0:T(8,128)(2,1)S(1)}, u32[]{:S(2)}, u32[]{:S(2)}) collective-permute-start(bf16[12,24,128]{2,1,0:T(8,128)(2,1)S(1)} %shard_map.92), channel_id=1, source_target_pairs={{128,0},{129,1},{130,2},{131,3},{132,4},{133,5},{134,6},{135,7},{1... | collective-permute-start | bytes 221192 | tf_op jit(solution)/shard_map/ppermute | solution.py:300
  31.3 11.4 %collective-permute-done.8.refs_7_ = bf16[12,24,128]{2,1,0:T(8,128)(2,1)S(1)} collective-permute-done((bf16[12,24,128]{2,1,0:T(8,128)(2,1)S(1)}, bf16[12,24,128]{2,1,0:T(8,128)(2,1)S(1)}, u32[]{:S(2)}, u32[]{:S(2)}) %collective-permute-start.8) | collective-permute-done | bytes 73760 | tf_op jit(solution)/shard_map/ppermute | solution.py:300
  42.8 0.6 shard_map.89
  43.4 1.7 %collective-permute-done.11.refs_12_ = bf16[12,24,128]{2,1,0:T(8,128)(2,1)S(1)} collective-permute-done((bf16[12,24,128]{2,1,0:T(8,128)(2,1)S(1)}, bf16[12,24,128]{2,1,0:T(8,128)(2,1)S(1)}, u32[]{:S(2)}, u32[]{:S(2)}) %collective-permute-start.11) | collective-permute-done | bytes 73760 | tf_op jit(solution)/shard_map/ppermute | solution.py:300
  45.1 1.4 %last.1 = (bf16[2,8,16,128]{3,2,1,0:T(8,128)(2,1)}, bf16[2,9,128,128]{3,2,1,0:T(8,128)(2,1)S(1)}) custom-call(s32[1]{0:T(128)} %bitcast.refs_0_, bf16[2,2,24,32,128]{4,3,2,1,0:T(8,128)(2,1)S(1)} %maximum_maximum_fusion.refs_1_, bf16[384,384]{1,0:T(8,128)(2,1)S(1)} %bitcast.47, bf16[384,384]{1,0:T(8,128)(2,1)S(1)} %bitcast.39, ...), custom_call_target="tpu_custom_call" | custom-call | tf_op jit(solution)/shard_map/last/pallas_call | solution.py:317
  46.5 16.7 %all_to_all.20 = bf16[8,288,128]{2,1,0:T(8,128)(2,1)S(1)} all-to-all(bf16[8,288,128]{2,1,0:T(8,128)(2,1)S(1)} %bitcast.48), channel_id=1, replica_groups=mesh['section'=4,'row_0'=8,'row_1'=2,'col_0'=2,'col_1'=4] {'row_1','col_1'}, dimensions={0} | all-to-all | bytes 1179648 | tf_op jit(solution)/shard_map/all_to_all | solution.py:208
  63.1 0.1 reduce_sum.21
  63.3 26.8 %all_to_all.21 = bf16[16,36,128]{2,1,0:T(8,128)(2,1)S(1)} all-to-all(bf16[16,36,128]{2,1,0:T(8,128)(2,1)S(1)} %bitcast.54), channel_id=1, replica_groups=mesh['section'=4,'row_0'=8,'row_1'=2,'col_0'=2,'col_1'=4] {'row_0','col_0'}, dimensions={0} | all-to-all | bytes 294912 | tf_op jit(solution)/shard_map/all_to_all | solution.py:208
  90.2 9.8 %all_to_all.22 = bf16[8,36,128]{2,1,0:T(8,128)(2,1)S(1)} all-to-all(bf16[8,36,128]{2,1,0:T(8,128)(2,1)S(1)} %broadcast_in_dim.26), channel_id=1, replica_groups=mesh['section'=4,'row_0'=8,'row_1'=2,'col_0'=2,'col_1'=4] {'row_0'}, dimensions={0} | all-to-all | bytes 147456 | tf_op jit(solution)/shard_map/all_to_all | solution.py:214
  100.0 0.1 broadcast_in_dim.28
  100.1 15.6 %all_to_all.23 = bf16[8,288,128]{2,1,0:T(8,128)(2,1)S(1)} all-to-all(bf16[8,288,128]{2,1,0:T(8,128)(2,1)S(1)} %broadcast_in_dim.28), channel_id=1, replica_groups=mesh['section'=4,'row_0'=8,'row_1'=2,'col_0'=2,'col_1'=4] {'row_1','col_1'}, dimensions={0} | all-to-all | bytes 1179648 | tf_op jit(solution)/shard_map/all_to_all | solution.py:214
  115.7 1.1 convert.6
  (32 shorter events, 0.6 us)
Async XLA Ops:
  0.6 22.3 %copy-start.1 = (bf16[1,2,3,3,128,128]{5,4,3,2,1,0:T(8,128)(2,1)S(1)}, bf16[1,2,3,3,128,128]{5,4,3,2,1,0:T(8,128)(2,1)}, u32[]{:S(2)}) copy-start(bf16[1,2,3,3,128,128]{5,4,3,2,1,0:T(8,128)(2,1)} %param.11) | copy-start | bytes 1769476
  2.4 14.1 %collective-permute-start = (bf16[2,2,8,8,128]{4,3,2,1,0:T(8,128)(2,1)S(1)}, bf16[2,2,8,8,128]{4,3,2,1,0:T(8,128)(2,1)S(1)}, u32[]{:S(2)}, u32[]{:S(2)}) collective-permute-start(bf16[2,2,8,8,128]{4,3,2,1,0:T(8,128)(2,1)S(1)} %get-tuple-element.14), channel_id=1, source_target_pairs={{1,2},{3,4},{5,6},{2,1},{4,3},{6,5},{9,10},{11,12},{13,14},{10,9},... | collective-permute-start | bytes 196616 | tf_op jit(solution)/shard_map/ppermute | solution.py:196
  3.0 13.5 %collective-permute-start.1 = (bf16[2,2,8,8,128]{4,3,2,1,0:T(8,128)(2,1)S(1)}, bf16[2,2,8,8,128]{4,3,2,1,0:T(8,128)(2,1)S(1)}, u32[]{:S(2)}, u32[]{:S(2)}) collective-permute-start(bf16[2,2,8,8,128]{4,3,2,1,0:T(8,128)(2,1)S(1)} %get-tuple-element.15), channel_id=1, source_target_pairs={{0,1},{1,0},{2,3},{3,2},{4,5},{5,4},{6,7},{7,6},{8,9},{9,8},{10,11... | collective-permute-start | bytes 196616 | tf_op jit(solution)/shard_map/ppermute | solution.py:197
  9.4 14.2 %collective-permute-start.5 = (bf16[2,2,8,16,128]{4,3,2,1,0:T(8,128)(2,1)S(1)}, bf16[2,2,8,16,128]{4,3,2,1,0:T(8,128)(2,1)S(1)}, u32[]{:S(2)}, u32[]{:S(2)}) collective-permute-start(bf16[2,2,8,16,128]{4,3,2,1,0:T(8,128)(2,1)S(1)} %get-tuple-element.17), channel_id=1, source_target_pairs={{0,8},{8,0},{16,24},{24,16},{32,40},{40,32},{48,56},{56,48},{64,72... | collective-permute-start | bytes 393224 | tf_op jit(solution)/shard_map/ppermute | solution.py:197
  13.7 10.0 %collective-permute-start.4 = (bf16[2,2,8,16,128]{4,3,2,1,0:T(8,128)(2,1)S(1)}, bf16[2,2,8,16,128]{4,3,2,1,0:T(8,128)(2,1)S(1)}, u32[]{:S(2)}, u32[]{:S(2)}) collective-permute-start(bf16[2,2,8,16,128]{4,3,2,1,0:T(8,128)(2,1)S(1)} %get-tuple-element.17), channel_id=1, source_target_pairs={{8,16},{24,32},{40,48},{56,64},{72,80},{88,96},{104,112},{16,8},{3... | collective-permute-start | bytes 393224 | tf_op jit(solution)/shard_map/ppermute | solution.py:196
  16.6 7.1 %collective-permute-start.3 = (bf16[2,2,8,16,128]{4,3,2,1,0:T(8,128)(2,1)S(1)}, bf16[2,2,8,16,128]{4,3,2,1,0:T(8,128)(2,1)S(1)}, u32[]{:S(2)}, u32[]{:S(2)}) collective-permute-start(bf16[2,2,8,16,128]{4,3,2,1,0:T(8,128)(2,1)S(1)} %pad_maximum_fusion), channel_id=1, source_target_pairs={{0,8},{8,0},{16,24},{24,16},{32,40},{40,32},{48,56},{56,48},{64,72... | collective-permute-start | bytes 393224 | tf_op jit(solution)/shard_map/ppermute | solution.py:197
  18.5 7.0 %collective-permute-start.2 = (bf16[2,2,8,16,128]{4,3,2,1,0:T(8,128)(2,1)S(1)}, bf16[2,2,8,16,128]{4,3,2,1,0:T(8,128)(2,1)S(1)}, u32[]{:S(2)}, u32[]{:S(2)}) collective-permute-start(bf16[2,2,8,16,128]{4,3,2,1,0:T(8,128)(2,1)S(1)} %pad_maximum_fusion), channel_id=1, source_target_pairs={{8,16},{24,32},{40,48},{56,64},{72,80},{88,96},{104,112},{16,8},{3... | collective-permute-start | bytes 393224 | tf_op jit(solution)/shard_map/ppermute | solution.py:196
  25.8 1.4 %collective-permute-start.6 = (bf16[10,56,128]{2,1,0:T(8,128)(2,1)S(1)}, bf16[10,56,128]{2,1,0:T(8,128)(2,1)S(1)}, u32[]{:S(2)}, u32[]{:S(2)}) collective-permute-start(bf16[10,56,128]{2,1,0:T(8,128)(2,1)S(1)} %shard_map.86), channel_id=1, source_target_pairs={{384,256},{385,257},{386,258},{387,259},{388,260},{389,261},{390,2... | collective-permute-start | bytes 430088 | tf_op jit(solution)/shard_map/ppermute | solution.py:300
  26.5 1.4 %collective-permute-start.9 = (bf16[10,56,128]{2,1,0:T(8,128)(2,1)S(1)}, bf16[10,56,128]{2,1,0:T(8,128)(2,1)S(1)}, u32[]{:S(2)}, u32[]{:S(2)}) collective-permute-start(bf16[10,56,128]{2,1,0:T(8,128)(2,1)S(1)} %shard_map.90), channel_id=1, source_target_pairs={{384,256},{385,257},{386,258},{387,259},{388,260},{389,261},{390,2... | collective-permute-start | bytes 430088 | tf_op jit(solution)/shard_map/ppermute | solution.py:300
  27.2 1.4 %collective-permute-start.7 = (bf16[16,24,128]{2,1,0:T(8,128)(2,1)S(1)}, bf16[16,24,128]{2,1,0:T(8,128)(2,1)S(1)}, u32[]{:S(2)}, u32[]{:S(2)}) collective-permute-start(bf16[16,24,128]{2,1,0:T(8,128)(2,1)S(1)} %shard_map.87), channel_id=1, source_target_pairs={{256,128},{257,129},{258,130},{259,131},{260,132},{261,133},{262,1... | collective-permute-start | bytes 294920 | tf_op jit(solution)/shard_map/ppermute | solution.py:300
  27.9 2.0 %collective-permute-start.10 = (bf16[16,24,128]{2,1,0:T(8,128)(2,1)S(1)}, bf16[16,24,128]{2,1,0:T(8,128)(2,1)S(1)}, u32[]{:S(2)}, u32[]{:S(2)}) collective-permute-start(bf16[16,24,128]{2,1,0:T(8,128)(2,1)S(1)} %shard_map.91), channel_id=1, source_target_pairs={{256,128},{257,129},{258,130},{259,131},{260,132},{261,133},{262,1... | collective-permute-start | bytes 294920 | tf_op jit(solution)/shard_map/ppermute | solution.py:300
  28.6 14.2 %collective-permute-start.8 = (bf16[12,24,128]{2,1,0:T(8,128)(2,1)S(1)}, bf16[12,24,128]{2,1,0:T(8,128)(2,1)S(1)}, u32[]{:S(2)}, u32[]{:S(2)}) collective-permute-start(bf16[12,24,128]{2,1,0:T(8,128)(2,1)S(1)} %shard_map.88), channel_id=1, source_target_pairs={{128,0},{129,1},{130,2},{131,3},{132,4},{133,5},{134,6},{135,7},{1... | collective-permute-start | bytes 221192 | tf_op jit(solution)/shard_map/ppermute | solution.py:300
  29.9 15.2 %copy-start = (bf16[1,2,8,16,128]{4,3,2,1,0:T(8,128)(2,1)S(1)}, bf16[1,2,8,16,128]{4,3,2,1,0:T(8,128)(2,1)}, u32[]{:S(2)}) copy-start(bf16[1,2,8,16,128]{4,3,2,1,0:T(8,128)(2,1)} %param.7) | copy-start | bytes 196612
  29.9 15.2 %collective-permute-start.11 = (bf16[12,24,128]{2,1,0:T(8,128)(2,1)S(1)}, bf16[12,24,128]{2,1,0:T(8,128)(2,1)S(1)}, u32[]{:S(2)}, u32[]{:S(2)}) collective-permute-start(bf16[12,24,128]{2,1,0:T(8,128)(2,1)S(1)} %shard_map.92), channel_id=1, source_target_pairs={{128,0},{129,1},{130,2},{131,3},{132,4},{133,5},{134,6},{135,7},{1... | collective-permute-start | bytes 221192 | tf_op jit(solution)/shard_map/ppermute | solution.py:300

commit v8 on v7

--- a/solution.py
+++ b/solution.py
@@ -190,11 +190,17 @@
             partial[which, k] = total[:, k * width : (k + 1) * width]
 
 
-def swaps(inward, outward, axis):
+def cross(cells, axis):
     count = lax.axis_size(axis)
-    crossing = [(i, i + 1) for i in range(1, count - 1, 2)]
-    apart = lax.ppermute(outward, axis, crossing + [(j, i) for i, j in crossing])
-    close = lax.ppermute(inward, axis, [(i, i ^ 1) for i in range(count)])
+    pairs = [(i, i + 1) for i in range(1, count - 1, 2)]
+    return lax.ppermute(cells, axis, pairs + [(j, i) for i, j in pairs])
+
+
+def swap(cells, axis):
+    return lax.ppermute(cells, axis, [(i, i ^ 1) for i in range(lax.axis_size(axis))])
+
+
+def in_place(apart, close, axis):
     even = (lax.axis_index(axis) & 1) == 0
     return (jnp.where(even, apart, close), jnp.where(even, close, apart))
 
@@ -259,18 +265,18 @@
             for x in (section_input[0], first_pre[0], second_pre[0], out_grad, scale, bn_shift[0])
         ],
     )
-    left, right = swaps(inward, outward, COL)
-    above, below = swaps(masks, masks, ROW)
+    left, right = in_place(cross(outward, COL), swap(inward, COL), COL)
+    middle = cross(masks, ROW)
     sides = jnp.concatenate([left, right], axis=3)
     sides, kernels = lax.optimization_barrier((sides, kernels))
-    above_sides, below_sides = swaps(sides, sides, ROW)
+    band = jnp.concatenate([sides[:, :, :, :DEPTH], masks, sides[:, :, :, DEPTH:]], axis=3)
+    corners = cross(sides, ROW)
+    close = swap(band, ROW)
     first = matrix_of(kernels[0, 0])
     second = matrix_of(kernels[0, 1])
-    bands = [
-        jnp.concatenate([side[:, :, :, :DEPTH], middle, side[:, :, :, DEPTH:]], axis=3)
-        for side, middle in ((above_sides, above), (sides, masks), (below_sides, below))
-    ]
-    masks = jnp.concatenate(bands, axis=2)
+    apart = jnp.concatenate([corners[:, :, :, :DEPTH], middle, corners[:, :, :, DEPTH:]], axis=3)
+    above, below = in_place(apart, close, ROW)
+    masks = jnp.concatenate([above, band, below], axis=2)
     high, wide = masks.shape[2:4]
     pairs = [
         pltpu.VMEM((high // 2, 2, wide, width), jnp.float32),

time: 117 us -> 114 us (0.974)
  starting transfers between devices: 25.8 us -> 21.7 us
  waiting for transfers between devices: 15 us -> 17.2 us
  blocking collectives: 68.9 us -> 67.6 us
    ppermute x6 -> x5, starting transfers between devices: 20.4 us -> 16.3 us  [the longest x2 8.31 us: swap(): lax.ppermute(cells, axis, [(i, i ^ 1) for i in range(lax.axis_size(axis))])]
    ppermute x6, waiting for transfers between devices: 13.1 us -> 15.8 us  [section_backward(): sent.append(lax.ppermute(result, 'section', pair))]
    all_to_all x2, blocking collectives: 43.5 us -> 42.2 us  [sum_of_blocks(): parts = lax.all_to_all(blocks, axes, 0, 0, tiled=True)]
  transfers between devices with their start and end apart: 12 -> 11, of which waited for: 3 -> 3; matrix products, arithmetic and copies ran while one was open for 1% -> 1% of each run, Pallas kernels for 1% -> 1%
where the time goes in v8:
time: 114 us
  blocking collectives  67.6 us (59%)
  starting transfers between devices  21.7 us (19%)
  waiting for transfers between devices  17.2 us (15%)
  Pallas kernels  3.69 us (3%)
  other arithmetic  1.62 us (1%)
    all_to_all x2, blocking collectives, sum_of_blocks(): parts = lax.all_to_all(blocks, axes, 0, 0, tiled=True)  42.2 us
    all_to_all x2, blocking collectives, copies(): lax.all_to_all(jnp.broadcast_to(block[None], (count, *block.shape)), axes...  25.4 us
    ppermute x6, waiting for transfers between devices, section_backward(): sent.append(lax.ppermute(result, 'section', pair))  15.8 us
    ppermute x2, starting transfers between devices, swap(): lax.ppermute(cells, axis, [(i, i ^ 1) for i in range(lax.axis_size(axis))])  8.31 us
    ppermute x3, starting transfers between devices, cross(): return lax.ppermute(cells, axis, pairs + [(j, i) for i, j in pairs])  7.97 us
    ppermute x6, starting transfers between devices, section_backward(): sent.append(lax.ppermute(result, 'section', pair))  5.39 us
  transfers between devices with their start and end apart: 11, of which 3 were waited for; matrix products, arithmetic and copies ran while one was open for 1% of the time, Pallas kernels for 1%

profile of v8, /device:TPU:1, one launch (start us, length us, event | category | flops | bytes accessed | tf_op | source)
XLA Modules:
  0.0 113.7 jit_solution(7796092444888359968)
XLA Ops:
  0.7 0.1 pad_add_fusion.flags
  0.7 1.6 %prepare.1 = (bf16[2,2,8,16,128]{4,3,2,1,0:T(8,128)(2,1)S(1)}, bf16[2,2,8,8,128]{4,3,2,1,0:T(8,128)(2,1)S(1)}, bf16[2,2,8,8,128]{4,3,2,1,0:T(8,128)(2,1)S(1)}, b...) custom-call(s32[2]{0:T(128)S(1)} %pad_add_fusion.flags, bf16[2,8,16,128]{3,2,1,0:T(8,128)(2,1)} %bitcast.49, ...), custom_call_target="tpu_custom_call" | custom-call | tf_op jit(solution)/shard_map/prepare/pallas_call | solution.py:243
  2.4 0.7 collective-permute-start
  3.0 6.4 %collective-permute-start.1 = (bf16[2,2,8,8,128]{4,3,2,1,0:T(8,128)(2,1)S(1)}, bf16[2,2,8,8,128]{4,3,2,1,0:T(8,128)(2,1)S(1)}, u32[]{:S(2)}, u32[]{:S(2)}) collective-permute-start(bf16[2,2,8,8,128]{4,3,2,1,0:T(8,128)(2,1)S(1)} %get-tuple-element.15), channel_id=1, source_target_pairs={{0,1},{1,0},{2,3},{3,2},{4,5},{5,4},{6,7},{7,6},{8,9},{9,8},{10,11... | collective-permute-start | bytes 196616 | tf_op jit(solution)/shard_map/ppermute | solution.py:200
  9.4 5.1 %collective-permute-start.3 = (bf16[2,2,8,16,128]{4,3,2,1,0:T(8,128)(2,1)S(1)}, bf16[2,2,8,16,128]{4,3,2,1,0:T(8,128)(2,1)S(1)}, u32[]{:S(2)}, u32[]{:S(2)}) collective-permute-start(bf16[2,2,8,16,128]{4,3,2,1,0:T(8,128)(2,1)S(1)} %get-tuple-element.17), channel_id=1, source_target_pairs={{8,16},{24,32},{40,48},{56,64},{72,80},{88,96},{104,112},{16,8},{3... | collective-permute-start | bytes 393224 | tf_op jit(solution)/shard_map/ppermute | solution.py:196
  14.6 0.0 collective-permute-done
  14.7 2.2 %collective-permute-start.2 = (bf16[2,2,8,16,128]{4,3,2,1,0:T(8,128)(2,1)S(1)}, bf16[2,2,8,16,128]{4,3,2,1,0:T(8,128)(2,1)S(1)}, u32[]{:S(2)}, u32[]{:S(2)}) collective-permute-start(bf16[2,2,8,16,128]{4,3,2,1,0:T(8,128)(2,1)S(1)} %pad_maximum_fusion.3), channel_id=1, source_target_pairs={{8,16},{24,32},{40,48},{56,64},{72,80},{88,96},{104,112},{16,8},{3... | collective-permute-start | bytes 393224 | tf_op jit(solution)/shard_map/ppermute | solution.py:196
  16.9 1.9 %collective-permute-start.4 = (bf16[2,2,8,32,128]{4,3,2,1,0:T(8,128)(2,1)S(1)}, bf16[2,2,8,32,128]{4,3,2,1,0:T(8,128)(2,1)S(1)}, u32[]{:S(2)}, u32[]{:S(2)}) collective-permute-start(bf16[2,2,8,32,128]{4,3,2,1,0:T(8,128)(2,1)S(1)} %pad_maximum_fusion.2), channel_id=1, source_target_pairs={{0,8},{8,0},{16,24},{24,16},{32,40},{40,32},{48,56},{56,48},{64,72... | collective-permute-start | bytes 786440 | tf_op jit(solution)/shard_map/ppermute | solution.py:200
  19.0 0.2 copy.20
  19.3 0.2 copy.19
  19.6 1.4 %collective-permute-done.2 = bf16[2,2,8,16,128]{4,3,2,1,0:T(8,128)(2,1)S(1)} collective-permute-done((bf16[2,2,8,16,128]{4,3,2,1,0:T(8,128)(2,1)S(1)}, bf16[2,2,8,16,128]{4,3,2,1,0:T(8,128)(2,1)S(1)}, u32[]{:S(2)}, u32[]{:S(2)}) %collective-permute-start.2) | collective-permute-done | bytes 131104 | tf_op jit(solution)/shard_map/ppermute | solution.py:196
  21.0 0.0 collective-permute-done.4
  21.0 0.1 broadcast_select_fusion.1
  21.1 0.1 pad_maximum_fusion.refs_1_
  21.2 0.7 collective-permute-start.5
  21.9 0.7 collective-permute-start.8
  22.6 0.7 collective-permute-start.6
  23.3 0.7 collective-permute-start.9
  24.1 1.3 %collective-permute-start.7 = (bf16[12,24,128]{2,1,0:T(8,128)(2,1)S(1)}, bf16[12,24,128]{2,1,0:T(8,128)(2,1)S(1)}, u32[]{:S(2)}, u32[]{:S(2)}) collective-permute-start(bf16[12,24,128]{2,1,0:T(8,128)(2,1)S(1)} %shard_map.88), channel_id=1, source_target_pairs={{128,0},{129,1},{130,2},{131,3},{132,4},{133,5},{134,6},{135,7},{1... | collective-permute-start | bytes 221192 | tf_op jit(solution)/shard_map/ppermute | solution.py:306
  25.4 0.0 copy-start
  25.4 1.4 %collective-permute-start.10 = (bf16[12,24,128]{2,1,0:T(8,128)(2,1)S(1)}, bf16[12,24,128]{2,1,0:T(8,128)(2,1)S(1)}, u32[]{:S(2)}, u32[]{:S(2)}) collective-permute-start(bf16[12,24,128]{2,1,0:T(8,128)(2,1)S(1)} %shard_map.92), channel_id=1, source_target_pairs={{128,0},{129,1},{130,2},{131,3},{132,4},{133,5},{134,6},{135,7},{1... | collective-permute-start | bytes 221192 | tf_op jit(solution)/shard_map/ppermute | solution.py:306
  26.8 14.6 %collective-permute-done.7.refs_7_ = bf16[12,24,128]{2,1,0:T(8,128)(2,1)S(1)} collective-permute-done((bf16[12,24,128]{2,1,0:T(8,128)(2,1)S(1)}, bf16[12,24,128]{2,1,0:T(8,128)(2,1)S(1)}, u32[]{:S(2)}, u32[]{:S(2)}) %collective-permute-start.7) | collective-permute-done | bytes 73760 | tf_op jit(solution)/shard_map/ppermute | solution.py:306
  41.4 0.6 shard_map.89
  42.1 1.2 %collective-permute-done.10.refs_12_ = bf16[12,24,128]{2,1,0:T(8,128)(2,1)S(1)} collective-permute-done((bf16[12,24,128]{2,1,0:T(8,128)(2,1)S(1)}, bf16[12,24,128]{2,1,0:T(8,128)(2,1)S(1)}, u32[]{:S(2)}, u32[]{:S(2)}) %collective-permute-start.10) | collective-permute-done | bytes 73760 | tf_op jit(solution)/shard_map/ppermute | solution.py:306
  43.3 1.4 %last.1 = (bf16[2,8,16,128]{3,2,1,0:T(8,128)(2,1)}, bf16[2,9,128,128]{3,2,1,0:T(8,128)(2,1)S(1)}) custom-call(s32[1]{0:T(128)} %bitcast.refs_0_, bf16[2,2,24,32,128]{4,3,2,1,0:T(8,128)(2,1)S(1)} %pad_maximum_fusion.refs_1_, bf16[384,384]{1,0:T(8,128)(2,1)S(1)} %bitcast.47, bf16[384,384]{1,0:T(8,128)(2,1)S(1)} %bitcast.39, ...), custom_call_target="tpu_custom_call" | custom-call | tf_op jit(solution)/shard_map/last/pallas_call | solution.py:323
  44.6 19.0 %all_to_all.20 = bf16[8,288,128]{2,1,0:T(8,128)(2,1)S(1)} all-to-all(bf16[8,288,128]{2,1,0:T(8,128)(2,1)S(1)} %bitcast.48), channel_id=1, replica_groups=mesh['section'=4,'row_0'=8,'row_1'=2,'col_0'=2,'col_1'=4] {'row_1','col_1'}, dimensions={0} | all-to-all | bytes 1179648 | tf_op jit(solution)/shard_map/all_to_all | solution.py:214
  63.6 0.1 reduce_sum.21
  63.8 23.2 %all_to_all.21 = bf16[16,36,128]{2,1,0:T(8,128)(2,1)S(1)} all-to-all(bf16[16,36,128]{2,1,0:T(8,128)(2,1)S(1)} %bitcast.54), channel_id=1, replica_groups=mesh['section'=4,'row_0'=8,'row_1'=2,'col_0'=2,'col_1'=4] {'row_0','col_0'}, dimensions={0} | all-to-all | bytes 294912 | tf_op jit(solution)/shard_map/all_to_all | solution.py:214
  87.1 9.8 %all_to_all.22 = bf16[8,36,128]{2,1,0:T(8,128)(2,1)S(1)} all-to-all(bf16[8,36,128]{2,1,0:T(8,128)(2,1)S(1)} %broadcast_in_dim.26), channel_id=1, replica_groups=mesh['section'=4,'row_0'=8,'row_1'=2,'col_0'=2,'col_1'=4] {'row_0'}, dimensions={0} | all-to-all | bytes 147456 | tf_op jit(solution)/shard_map/all_to_all | solution.py:220
  96.9 0.1 broadcast_in_dim.28
  97.0 15.6 %all_to_all.23 = bf16[8,288,128]{2,1,0:T(8,128)(2,1)S(1)} all-to-all(bf16[8,288,128]{2,1,0:T(8,128)(2,1)S(1)} %broadcast_in_dim.28), channel_id=1, replica_groups=mesh['section'=4,'row_0'=8,'row_1'=2,'col_0'=2,'col_1'=4] {'row_1','col_1'}, dimensions={0} | all-to-all | bytes 1179648 | tf_op jit(solution)/shard_map/all_to_all | solution.py:220
  112.6 1.1 %convert.6 = f32[1,2,3,3,128,128]{5,4,3,2,1,0:T(8,128)} convert(bf16[1,2,3,3,128,128]{5,4,3,2,1,0:T(8,128)(2,1)S(1)} %bitcast.51) | non-fusion elementwise | flops 294912 | bytes 1769472 | tf_op jit(solution)/shard_map/convert_element_type | solution.py:232
  (30 shorter events, 0.5 us)
Async XLA Ops:
  0.6 18.2 %copy-start.1 = (bf16[1,2,3,3,128,128]{5,4,3,2,1,0:T(8,128)(2,1)S(1)}, bf16[1,2,3,3,128,128]{5,4,3,2,1,0:T(8,128)(2,1)}, u32[]{:S(2)}) copy-start(bf16[1,2,3,3,128,128]{5,4,3,2,1,0:T(8,128)(2,1)} %param.11) | copy-start | bytes 1769476
  2.4 12.2 %collective-permute-start = (bf16[2,2,8,8,128]{4,3,2,1,0:T(8,128)(2,1)S(1)}, bf16[2,2,8,8,128]{4,3,2,1,0:T(8,128)(2,1)S(1)}, u32[]{:S(2)}, u32[]{:S(2)}) collective-permute-start(bf16[2,2,8,8,128]{4,3,2,1,0:T(8,128)(2,1)S(1)} %get-tuple-element.14), channel_id=1, source_target_pairs={{1,2},{3,4},{5,6},{2,1},{4,3},{6,5},{9,10},{11,12},{13,14},{10,9},... | collective-permute-start | bytes 196616 | tf_op jit(solution)/shard_map/ppermute | solution.py:196
  3.0 11.6 %collective-permute-start.1 = (bf16[2,2,8,8,128]{4,3,2,1,0:T(8,128)(2,1)S(1)}, bf16[2,2,8,8,128]{4,3,2,1,0:T(8,128)(2,1)S(1)}, u32[]{:S(2)}, u32[]{:S(2)}) collective-permute-start(bf16[2,2,8,8,128]{4,3,2,1,0:T(8,128)(2,1)S(1)} %get-tuple-element.15), channel_id=1, source_target_pairs={{0,1},{1,0},{2,3},{3,2},{4,5},{5,4},{6,7},{7,6},{8,9},{9,8},{10,11... | collective-permute-start | bytes 196616 | tf_op jit(solution)/shard_map/ppermute | solution.py:200
  9.4 11.6 %collective-permute-start.3 = (bf16[2,2,8,16,128]{4,3,2,1,0:T(8,128)(2,1)S(1)}, bf16[2,2,8,16,128]{4,3,2,1,0:T(8,128)(2,1)S(1)}, u32[]{:S(2)}, u32[]{:S(2)}) collective-permute-start(bf16[2,2,8,16,128]{4,3,2,1,0:T(8,128)(2,1)S(1)} %get-tuple-element.17), channel_id=1, source_target_pairs={{8,16},{24,32},{40,48},{56,64},{72,80},{88,96},{104,112},{16,8},{3... | collective-permute-start | bytes 393224 | tf_op jit(solution)/shard_map/ppermute | solution.py:196
  14.7 6.3 %collective-permute-start.2 = (bf16[2,2,8,16,128]{4,3,2,1,0:T(8,128)(2,1)S(1)}, bf16[2,2,8,16,128]{4,3,2,1,0:T(8,128)(2,1)S(1)}, u32[]{:S(2)}, u32[]{:S(2)}) collective-permute-start(bf16[2,2,8,16,128]{4,3,2,1,0:T(8,128)(2,1)S(1)} %pad_maximum_fusion.3), channel_id=1, source_target_pairs={{8,16},{24,32},{40,48},{56,64},{72,80},{88,96},{104,112},{16,8},{3... | collective-permute-start | bytes 393224 | tf_op jit(solution)/shard_map/ppermute | solution.py:196
  16.9 4.1 %collective-permute-start.4 = (bf16[2,2,8,32,128]{4,3,2,1,0:T(8,128)(2,1)S(1)}, bf16[2,2,8,32,128]{4,3,2,1,0:T(8,128)(2,1)S(1)}, u32[]{:S(2)}, u32[]{:S(2)}) collective-permute-start(bf16[2,2,8,32,128]{4,3,2,1,0:T(8,128)(2,1)S(1)} %pad_maximum_fusion.2), channel_id=1, source_target_pairs={{0,8},{8,0},{16,24},{24,16},{32,40},{40,32},{48,56},{56,48},{64,72... | collective-permute-start | bytes 786440 | tf_op jit(solution)/shard_map/ppermute | solution.py:200
  21.2 1.4 %collective-permute-start.5 = (bf16[10,56,128]{2,1,0:T(8,128)(2,1)S(1)}, bf16[10,56,128]{2,1,0:T(8,128)(2,1)S(1)}, u32[]{:S(2)}, u32[]{:S(2)}) collective-permute-start(bf16[10,56,128]{2,1,0:T(8,128)(2,1)S(1)} %shard_map.86), channel_id=1, source_target_pairs={{384,256},{385,257},{386,258},{387,259},{388,260},{389,261},{390,2... | collective-permute-start | bytes 430088 | tf_op jit(solution)/shard_map/ppermute | solution.py:306
  21.9 1.4 %collective-permute-start.8 = (bf16[10,56,128]{2,1,0:T(8,128)(2,1)S(1)}, bf16[10,56,128]{2,1,0:T(8,128)(2,1)S(1)}, u32[]{:S(2)}, u32[]{:S(2)}) collective-permute-start(bf16[10,56,128]{2,1,0:T(8,128)(2,1)S(1)} %shard_map.90), channel_id=1, source_target_pairs={{384,256},{385,257},{386,258},{387,259},{388,260},{389,261},{390,2... | collective-permute-start | bytes 430088 | tf_op jit(solution)/shard_map/ppermute | solution.py:306
  22.6 1.4 %collective-permute-start.6 = (bf16[16,24,128]{2,1,0:T(8,128)(2,1)S(1)}, bf16[16,24,128]{2,1,0:T(8,128)(2,1)S(1)}, u32[]{:S(2)}, u32[]{:S(2)}) collective-permute-start(bf16[16,24,128]{2,1,0:T(8,128)(2,1)S(1)} %shard_map.87), channel_id=1, source_target_pairs={{256,128},{257,129},{258,130},{259,131},{260,132},{261,133},{262,1... | collective-permute-start | bytes 294920 | tf_op jit(solution)/shard_map/ppermute | solution.py:306
  23.3 2.0 %collective-permute-start.9 = (bf16[16,24,128]{2,1,0:T(8,128)(2,1)S(1)}, bf16[16,24,128]{2,1,0:T(8,128)(2,1)S(1)}, u32[]{:S(2)}, u32[]{:S(2)}) collective-permute-start(bf16[16,24,128]{2,1,0:T(8,128)(2,1)S(1)} %shard_map.91), channel_id=1, source_target_pairs={{256,128},{257,129},{258,130},{259,131},{260,132},{261,133},{262,1... | collective-permute-start | bytes 294920 | tf_op jit(solution)/shard_map/ppermute | solution.py:306
  24.1 17.3 %collective-permute-start.7 = (bf16[12,24,128]{2,1,0:T(8,128)(2,1)S(1)}, bf16[12,24,128]{2,1,0:T(8,128)(2,1)S(1)}, u32[]{:S(2)}, u32[]{:S(2)}) collective-permute-start(bf16[12,24,128]{2,1,0:T(8,128)(2,1)S(1)} %shard_map.88), channel_id=1, source_target_pairs={{128,0},{129,1},{130,2},{131,3},{132,4},{133,5},{134,6},{135,7},{1... | collective-permute-start | bytes 221192 | tf_op jit(solution)/shard_map/ppermute | solution.py:306
  25.4 17.9 %copy-start = (bf16[1,2,8,16,128]{4,3,2,1,0:T(8,128)(2,1)S(1)}, bf16[1,2,8,16,128]{4,3,2,1,0:T(8,128)(2,1)}, u32[]{:S(2)}) copy-start(bf16[1,2,8,16,128]{4,3,2,1,0:T(8,128)(2,1)} %param.7) | copy-start | bytes 196612
  25.4 17.9 %collective-permute-start.10 = (bf16[12,24,128]{2,1,0:T(8,128)(2,1)S(1)}, bf16[12,24,128]{2,1,0:T(8,128)(2,1)S(1)}, u32[]{:S(2)}, u32[]{:S(2)}) collective-permute-start(bf16[12,24,128]{2,1,0:T(8,128)(2,1)S(1)} %shard_map.92), channel_id=1, source_target_pairs={{128,0},{129,1},{130,2},{131,3},{132,4},{133,5},{134,6},{135,7},{1... | collective-permute-start | bytes 221192 | tf_op jit(solution)/shard_map/ppermute | solution.py:306

commit v9 on v8

--- a/solution.py
+++ b/solution.py
@@ -220,16 +220,49 @@
     return lax.all_to_all(jnp.broadcast_to(block[None], (count, *block.shape)), axes, 0, 0, tiled=True)
 
 
+def write_kernel(first_core, half, other, out, lines, done):
+    stack, ring, rows, _ = half.shape
+    chunk = stack * rows
+    moves = []
+    for core in range(2):
+        mine = first_core[0] > 0 if core == 0 else first_core[0] == 0
+        for x in range(ring):
+            start = (core * ring + x) * chunk
+            for z in range(stack):
+                value = jnp.where(mine, half[z, x].astype(jnp.float32), other[z, x].astype(jnp.float32))
+                lines[start + z * rows : start + (z + 1) * rows] = value
+            part = pl.ds(start, chunk)
+            move = pltpu.make_async_copy(lines.at[part], out.at[part], done.at[len(moves)])
+            move.start()
+            moves.append(move)
+    for move in moves:
+        move.wait()
+
+
 def total_of(x, factor):
-    near, stack = (lax.axis_size(NEAR), lax.axis_size("row_0"))
+    near, stack, ring = (lax.axis_size(NEAR), lax.axis_size("row_0"), lax.axis_size("col_1"))
     width = x.shape[-1]
     part = sum_of_blocks(x.reshape(near, -1, width), NEAR).astype(jnp.bfloat16)
     part = part.reshape(stack, 1, -1, width)
     twice = jnp.broadcast_to(part, (stack, lax.axis_size("col_0"), *part.shape[2:]))
     own = sum_of_blocks(twice.reshape(-1, *part.shape[2:]), FAR)
     own = (own * factor).astype(jnp.bfloat16)
-    part = copies(own, "row_0").reshape(-1, width)
-    return copies(part, NEAR).reshape(x.shape).astype(jnp.float32)
+    half = copies(own[None], ("row_0", "col_1"))
+    other = lax.ppermute(half, "row_1", [(0, 1), (1, 0)])
+    first_core = (lax.axis_index("row_1") == 0).astype(jnp.int32).reshape(1)
+    shape = (stack, ring, *own.shape)
+    return pl.pallas_call(
+        write_kernel,
+        name="write",
+        in_specs=[SMEM, VMEM, VMEM],
+        out_specs=pl.BlockSpec(memory_space=pltpu.MemorySpace.HBM),
+        out_shape=jax.ShapeDtypeStruct((x.size // width, width), jnp.float32),
+        scratch_shapes=[
+            pltpu.VMEM((x.size // width, width), jnp.float32),
+            pltpu.SemaphoreType.DMA((2 * ring,)),
+        ],
+        compiler_params=PARAMS,
+    )(first_core, half.reshape(shape), other.reshape(shape))
 
 
 def section_backward(section_input, first_pre, second_pre, out_grad, kernels, bn_scale, bn_shift):

time: 114 us -> 110 us (0.965)
  blocking collectives: 67.6 us -> 56.3 us
  starting transfers between devices: 21.7 us -> 27.9 us
  waiting for transfers between devices: 17.2 us -> 18.4 us
  other arithmetic: 1.62 us -> 0.48 us
    all_to_all x2 -> x1, blocking collectives: 25.4 us -> 14.1 us  [copies(): lax.all_to_all(jnp.broadcast_to(block[None], (count, *block.shape)), axes...]
    ppermute x0 -> x1, starting transfers between devices: none -> 6.18 us  [total_of(): other = lax.ppermute(half, 'row_1', [(0, 1), (1, 0)])]
    ppermute x0 -> x1, waiting for transfers between devices: none -> 1.23 us  [total_of(): other = lax.ppermute(half, 'row_1', [(0, 1), (1, 0)])]
  transfers between devices with their start and end apart: 11 -> 12, of which waited for: 3 -> 4; matrix products, arithmetic and copies ran while one was open for 1% -> 1% of each run, Pallas kernels for 1% -> 1%
where the time goes in v9:
time: 110 us
  blocking collectives  56.3 us (51%)
  starting transfers between devices  27.9 us (25%)
  waiting for transfers between devices  18.4 us (17%)
  Pallas kernels  4.76 us (4%)
    all_to_all x2, blocking collectives, sum_of_blocks(): parts = lax.all_to_all(blocks, axes, 0, 0, tiled=True)  42.3 us
    ppermute x6, waiting for transfers between devices, section_backward(): sent.append(lax.ppermute(result, 'section', pair))  15.8 us
    all_to_all x1, blocking collectives, copies(): lax.all_to_all(jnp.broadcast_to(block[None], (count, *block.shape)), axes...  14.1 us
    ppermute x2, starting transfers between devices, swap(): lax.ppermute(cells, axis, [(i, i ^ 1) for i in range(lax.axis_size(axis))])  8.31 us
    ppermute x3, starting transfers between devices, cross(): return lax.ppermute(cells, axis, pairs + [(j, i) for i, j in pairs])  7.97 us
    ppermute x1, starting transfers between devices, total_of(): other = lax.ppermute(half, 'row_1', [(0, 1), (1, 0)])  6.18 us
    ppermute x6, starting transfers between devices, section_backward(): sent.append(lax.ppermute(result, 'section', pair))  5.39 us
  transfers between devices with their start and end apart: 12, of which 4 were waited for; matrix products, arithmetic and copies ran while one was open for 1% of the time, Pallas kernels for 1%

profile of v9, /device:TPU:1, one launch (start us, length us, event | category | flops | bytes accessed | tf_op | source)
XLA Modules:
  0.0 109.7 jit_solution(5309339903091604640)
XLA Ops:
  0.7 0.1 pad_add_fusion.flags
  0.7 1.6 %prepare.1 = (bf16[2,2,8,16,128]{4,3,2,1,0:T(8,128)(2,1)S(1)}, bf16[2,2,8,8,128]{4,3,2,1,0:T(8,128)(2,1)S(1)}, bf16[2,2,8,8,128]{4,3,2,1,0:T(8,128)(2,1)S(1)}, b...) custom-call(s32[2]{0:T(128)S(1)} %pad_add_fusion.flags, bf16[2,8,16,128]{3,2,1,0:T(8,128)(2,1)} %bitcast.53, ...), custom_call_target="tpu_custom_call" | custom-call | tf_op jit(solution)/shard_map/prepare/pallas_call | solution.py:276
  2.4 0.7 collective-permute-start
  3.0 6.4 %collective-permute-start.1 = (bf16[2,2,8,8,128]{4,3,2,1,0:T(8,128)(2,1)S(1)}, bf16[2,2,8,8,128]{4,3,2,1,0:T(8,128)(2,1)S(1)}, u32[]{:S(2)}, u32[]{:S(2)}) collective-permute-start(bf16[2,2,8,8,128]{4,3,2,1,0:T(8,128)(2,1)S(1)} %get-tuple-element.15), channel_id=1, source_target_pairs={{0,1},{1,0},{2,3},{3,2},{4,5},{5,4},{6,7},{7,6},{8,9},{9,8},{10,11... | collective-permute-start | bytes 196616 | tf_op jit(solution)/shard_map/ppermute | solution.py:200
  9.4 5.1 %collective-permute-start.3 = (bf16[2,2,8,16,128]{4,3,2,1,0:T(8,128)(2,1)S(1)}, bf16[2,2,8,16,128]{4,3,2,1,0:T(8,128)(2,1)S(1)}, u32[]{:S(2)}, u32[]{:S(2)}) collective-permute-start(bf16[2,2,8,16,128]{4,3,2,1,0:T(8,128)(2,1)S(1)} %get-tuple-element.17), channel_id=1, source_target_pairs={{8,16},{24,32},{40,48},{56,64},{72,80},{88,96},{104,112},{16,8},{3... | collective-permute-start | bytes 393224 | tf_op jit(solution)/shard_map/ppermute | solution.py:196
  14.6 0.0 collective-permute-done
  14.6 0.0 collective-permute-done.1
  14.7 2.2 %collective-permute-start.2 = (bf16[2,2,8,16,128]{4,3,2,1,0:T(8,128)(2,1)S(1)}, bf16[2,2,8,16,128]{4,3,2,1,0:T(8,128)(2,1)S(1)}, u32[]{:S(2)}, u32[]{:S(2)}) collective-permute-start(bf16[2,2,8,16,128]{4,3,2,1,0:T(8,128)(2,1)S(1)} %pad_maximum_fusion.3), channel_id=1, source_target_pairs={{8,16},{24,32},{40,48},{56,64},{72,80},{88,96},{104,112},{16,8},{3... | collective-permute-start | bytes 393224 | tf_op jit(solution)/shard_map/ppermute | solution.py:196
  16.9 1.9 %collective-permute-start.4 = (bf16[2,2,8,32,128]{4,3,2,1,0:T(8,128)(2,1)S(1)}, bf16[2,2,8,32,128]{4,3,2,1,0:T(8,128)(2,1)S(1)}, u32[]{:S(2)}, u32[]{:S(2)}) collective-permute-start(bf16[2,2,8,32,128]{4,3,2,1,0:T(8,128)(2,1)S(1)} %pad_maximum_fusion.2), channel_id=1, source_target_pairs={{0,8},{8,0},{16,24},{24,16},{32,40},{40,32},{48,56},{56,48},{64,72... | collective-permute-start | bytes 786440 | tf_op jit(solution)/shard_map/ppermute | solution.py:200
  19.0 0.2 copy.22
  19.3 0.2 copy.21
  19.6 1.4 %collective-permute-done.2 = bf16[2,2,8,16,128]{4,3,2,1,0:T(8,128)(2,1)S(1)} collective-permute-done((bf16[2,2,8,16,128]{4,3,2,1,0:T(8,128)(2,1)S(1)}, bf16[2,2,8,16,128]{4,3,2,1,0:T(8,128)(2,1)S(1)}, u32[]{:S(2)}, u32[]{:S(2)}) %collective-permute-start.2) | collective-permute-done | bytes 131104 | tf_op jit(solution)/shard_map/ppermute | solution.py:196
  21.0 0.1 broadcast_select_fusion.1
  21.1 0.1 pad_maximum_fusion.refs_1_
  21.2 0.7 collective-permute-start.5
  21.9 0.7 collective-permute-start.8
  22.6 0.7 collective-permute-start.6
  23.3 0.7 collective-permute-start.9
  24.1 1.3 %collective-permute-start.7 = (bf16[12,24,128]{2,1,0:T(8,128)(2,1)S(1)}, bf16[12,24,128]{2,1,0:T(8,128)(2,1)S(1)}, u32[]{:S(2)}, u32[]{:S(2)}) collective-permute-start(bf16[12,24,128]{2,1,0:T(8,128)(2,1)S(1)} %shard_map.88), channel_id=1, source_target_pairs={{128,0},{129,1},{130,2},{131,3},{132,4},{133,5},{134,6},{135,7},{1... | collective-permute-start | bytes 221192 | tf_op jit(solution)/shard_map/ppermute | solution.py:339
  25.4 0.0 copy-start
  25.4 1.4 %collective-permute-start.10 = (bf16[12,24,128]{2,1,0:T(8,128)(2,1)S(1)}, bf16[12,24,128]{2,1,0:T(8,128)(2,1)S(1)}, u32[]{:S(2)}, u32[]{:S(2)}) collective-permute-start(bf16[12,24,128]{2,1,0:T(8,128)(2,1)S(1)} %shard_map.92), channel_id=1, source_target_pairs={{128,0},{129,1},{130,2},{131,3},{132,4},{133,5},{134,6},{135,7},{1... | collective-permute-start | bytes 221192 | tf_op jit(solution)/shard_map/ppermute | solution.py:339
  26.8 14.6 %collective-permute-done.7.refs_7_ = bf16[12,24,128]{2,1,0:T(8,128)(2,1)S(1)} collective-permute-done((bf16[12,24,128]{2,1,0:T(8,128)(2,1)S(1)}, bf16[12,24,128]{2,1,0:T(8,128)(2,1)S(1)}, u32[]{:S(2)}, u32[]{:S(2)}) %collective-permute-start.7) | collective-permute-done | bytes 73760 | tf_op jit(solution)/shard_map/ppermute | solution.py:339
  41.4 0.6 shard_map.89
  42.0 1.2 %collective-permute-done.10.refs_12_ = bf16[12,24,128]{2,1,0:T(8,128)(2,1)S(1)} collective-permute-done((bf16[12,24,128]{2,1,0:T(8,128)(2,1)S(1)}, bf16[12,24,128]{2,1,0:T(8,128)(2,1)S(1)}, u32[]{:S(2)}, u32[]{:S(2)}) %collective-permute-start.10) | collective-permute-done | bytes 73760 | tf_op jit(solution)/shard_map/ppermute | solution.py:339
  43.3 1.3 %last.1 = (bf16[2,8,16,128]{3,2,1,0:T(8,128)(2,1)}, bf16[2,9,128,128]{3,2,1,0:T(8,128)(2,1)S(1)}) custom-call(s32[1]{0:T(128)} %bitcast.refs_0_, bf16[2,2,24,32,128]{4,3,2,1,0:T(8,128)(2,1)S(1)} %pad_maximum_fusion.refs_1_, bf16[384,384]{1,0:T(8,128)(2,1)S(1)} %bitcast.49, bf16[384,384]{1,0:T(8,128)(2,1)S(1)} %bitcast.41, ...), custom_call_target="tpu_custom_call" | custom-call | tf_op jit(solution)/shard_map/last/pallas_call | solution.py:356
  44.6 19.0 %all_to_all.15 = bf16[8,288,128]{2,1,0:T(8,128)(2,1)S(1)} all-to-all(bf16[8,288,128]{2,1,0:T(8,128)(2,1)S(1)} %bitcast.51), channel_id=1, replica_groups=mesh['section'=4,'row_0'=8,'row_1'=2,'col_0'=2,'col_1'=4] {'row_1','col_1'}, dimensions={0} | all-to-all | bytes 1179648 | tf_op jit(solution)/shard_map/all_to_all | solution.py:214
  63.6 0.1 reduce_sum.21
  63.8 23.2 %all_to_all.16 = bf16[16,36,128]{2,1,0:T(8,128)(2,1)S(1)} all-to-all(bf16[16,36,128]{2,1,0:T(8,128)(2,1)S(1)} %bitcast.58), channel_id=1, replica_groups=mesh['section'=4,'row_0'=8,'row_1'=2,'col_0'=2,'col_1'=4] {'row_0','col_0'}, dimensions={0} | all-to-all | bytes 294912 | tf_op jit(solution)/shard_map/all_to_all | solution.py:214
  87.1 14.1 %all_to_all.17 = bf16[32,1,36,128]{3,2,1,0:T(8,128)(2,1)S(1)} all-to-all(bf16[32,1,36,128]{3,2,1,0:T(8,128)(2,1)S(1)} %broadcast_in_dim.18), channel_id=1, replica_groups=mesh['section'=4,'row_0'=8,'row_1'=2,'col_0'=2,'col_1'=4] {'row_0','col_1'}, dimensions={0} | all-to-all | bytes 589824 | tf_op jit(solution)/shard_map/all_to_all | solution.py:220
  101.2 6.2 %collective-permute-start.11 = (bf16[32,1,36,128]{3,2,1,0:T(8,128)(2,1)S(1)}, bf16[32,1,36,128]{3,2,1,0:T(8,128)(2,1)S(1)}, u32[]{:S(2)}, u32[]{:S(2)}) collective-permute-start(bf16[32,1,36,128]{3,2,1,0:T(8,128)(2,1)S(1)} %all_to_all.17), channel_id=1, source_target_pairs={{0,8},{8,0},{1,9},{9,1},{2,10},{10,2},{3,11},{11,3},{4,12},{12,4},... | collective-permute-start | bytes 884744 | tf_op jit(solution)/shard_map/ppermute | solution.py:251
  107.4 1.2 %collective-permute-done.11 = bf16[32,1,36,128]{3,2,1,0:T(8,128)(2,1)S(1)} collective-permute-done((bf16[32,1,36,128]{3,2,1,0:T(8,128)(2,1)S(1)}, bf16[32,1,36,128]{3,2,1,0:T(8,128)(2,1)S(1)}, u32[]{:S(2)}, u32[]{:S(2)}) %collective-permute-start.11) | collective-permute-done | bytes 294944 | tf_op jit(solution)/shard_map/ppermute | solution.py:251
  108.6 1.1 write.1
  (29 shorter events, 0.5 us)
Async XLA Ops:
  0.6 18.2 %copy-start.1 = (bf16[1,2,3,3,128,128]{5,4,3,2,1,0:T(8,128)(2,1)S(1)}, bf16[1,2,3,3,128,128]{5,4,3,2,1,0:T(8,128)(2,1)}, u32[]{:S(2)}) copy-start(bf16[1,2,3,3,128,128]{5,4,3,2,1,0:T(8,128)(2,1)} %param.11) | copy-start | bytes 1769476
  2.4 12.2 %collective-permute-start = (bf16[2,2,8,8,128]{4,3,2,1,0:T(8,128)(2,1)S(1)}, bf16[2,2,8,8,128]{4,3,2,1,0:T(8,128)(2,1)S(1)}, u32[]{:S(2)}, u32[]{:S(2)}) collective-permute-start(bf16[2,2,8,8,128]{4,3,2,1,0:T(8,128)(2,1)S(1)} %get-tuple-element.14), channel_id=1, source_target_pairs={{1,2},{3,4},{5,6},{2,1},{4,3},{6,5},{9,10},{11,12},{13,14},{10,9},... | collective-permute-start | bytes 196616 | tf_op jit(solution)/shard_map/ppermute | solution.py:196
  3.0 11.6 %collective-permute-start.1 = (bf16[2,2,8,8,128]{4,3,2,1,0:T(8,128)(2,1)S(1)}, bf16[2,2,8,8,128]{4,3,2,1,0:T(8,128)(2,1)S(1)}, u32[]{:S(2)}, u32[]{:S(2)}) collective-permute-start(bf16[2,2,8,8,128]{4,3,2,1,0:T(8,128)(2,1)S(1)} %get-tuple-element.15), channel_id=1, source_target_pairs={{0,1},{1,0},{2,3},{3,2},{4,5},{5,4},{6,7},{7,6},{8,9},{9,8},{10,11... | collective-permute-start | bytes 196616 | tf_op jit(solution)/shard_map/ppermute | solution.py:200
  9.4 11.6 %collective-permute-start.3 = (bf16[2,2,8,16,128]{4,3,2,1,0:T(8,128)(2,1)S(1)}, bf16[2,2,8,16,128]{4,3,2,1,0:T(8,128)(2,1)S(1)}, u32[]{:S(2)}, u32[]{:S(2)}) collective-permute-start(bf16[2,2,8,16,128]{4,3,2,1,0:T(8,128)(2,1)S(1)} %get-tuple-element.17), channel_id=1, source_target_pairs={{8,16},{24,32},{40,48},{56,64},{72,80},{88,96},{104,112},{16,8},{3... | collective-permute-start | bytes 393224 | tf_op jit(solution)/shard_map/ppermute | solution.py:196
  14.7 6.3 %collective-permute-start.2 = (bf16[2,2,8,16,128]{4,3,2,1,0:T(8,128)(2,1)S(1)}, bf16[2,2,8,16,128]{4,3,2,1,0:T(8,128)(2,1)S(1)}, u32[]{:S(2)}, u32[]{:S(2)}) collective-permute-start(bf16[2,2,8,16,128]{4,3,2,1,0:T(8,128)(2,1)S(1)} %pad_maximum_fusion.3), channel_id=1, source_target_pairs={{8,16},{24,32},{40,48},{56,64},{72,80},{88,96},{104,112},{16,8},{3... | collective-permute-start | bytes 393224 | tf_op jit(solution)/shard_map/ppermute | solution.py:196
  16.9 4.1 %collective-permute-start.4 = (bf16[2,2,8,32,128]{4,3,2,1,0:T(8,128)(2,1)S(1)}, bf16[2,2,8,32,128]{4,3,2,1,0:T(8,128)(2,1)S(1)}, u32[]{:S(2)}, u32[]{:S(2)}) collective-permute-start(bf16[2,2,8,32,128]{4,3,2,1,0:T(8,128)(2,1)S(1)} %pad_maximum_fusion.2), channel_id=1, source_target_pairs={{0,8},{8,0},{16,24},{24,16},{32,40},{40,32},{48,56},{56,48},{64,72... | collective-permute-start | bytes 786440 | tf_op jit(solution)/shard_map/ppermute | solution.py:200
  21.2 1.4 %collective-permute-start.5 = (bf16[10,56,128]{2,1,0:T(8,128)(2,1)S(1)}, bf16[10,56,128]{2,1,0:T(8,128)(2,1)S(1)}, u32[]{:S(2)}, u32[]{:S(2)}) collective-permute-start(bf16[10,56,128]{2,1,0:T(8,128)(2,1)S(1)} %shard_map.86), channel_id=1, source_target_pairs={{384,256},{385,257},{386,258},{387,259},{388,260},{389,261},{390,2... | collective-permute-start | bytes 430088 | tf_op jit(solution)/shard_map/ppermute | solution.py:339
  21.9 1.4 %collective-permute-start.8 = (bf16[10,56,128]{2,1,0:T(8,128)(2,1)S(1)}, bf16[10,56,128]{2,1,0:T(8,128)(2,1)S(1)}, u32[]{:S(2)}, u32[]{:S(2)}) collective-permute-start(bf16[10,56,128]{2,1,0:T(8,128)(2,1)S(1)} %shard_map.90), channel_id=1, source_target_pairs={{384,256},{385,257},{386,258},{387,259},{388,260},{389,261},{390,2... | collective-permute-start | bytes 430088 | tf_op jit(solution)/shard_map/ppermute | solution.py:339
  22.6 1.4 %collective-permute-start.6 = (bf16[16,24,128]{2,1,0:T(8,128)(2,1)S(1)}, bf16[16,24,128]{2,1,0:T(8,128)(2,1)S(1)}, u32[]{:S(2)}, u32[]{:S(2)}) collective-permute-start(bf16[16,24,128]{2,1,0:T(8,128)(2,1)S(1)} %shard_map.87), channel_id=1, source_target_pairs={{256,128},{257,129},{258,130},{259,131},{260,132},{261,133},{262,1... | collective-permute-start | bytes 294920 | tf_op jit(solution)/shard_map/ppermute | solution.py:339
  23.3 2.0 %collective-permute-start.9 = (bf16[16,24,128]{2,1,0:T(8,128)(2,1)S(1)}, bf16[16,24,128]{2,1,0:T(8,128)(2,1)S(1)}, u32[]{:S(2)}, u32[]{:S(2)}) collective-permute-start(bf16[16,24,128]{2,1,0:T(8,128)(2,1)S(1)} %shard_map.91), channel_id=1, source_target_pairs={{256,128},{257,129},{258,130},{259,131},{260,132},{261,133},{262,1... | collective-permute-start | bytes 294920 | tf_op jit(solution)/shard_map/ppermute | solution.py:339
  24.1 17.3 %collective-permute-start.7 = (bf16[12,24,128]{2,1,0:T(8,128)(2,1)S(1)}, bf16[12,24,128]{2,1,0:T(8,128)(2,1)S(1)}, u32[]{:S(2)}, u32[]{:S(2)}) collective-permute-start(bf16[12,24,128]{2,1,0:T(8,128)(2,1)S(1)} %shard_map.88), channel_id=1, source_target_pairs={{128,0},{129,1},{130,2},{131,3},{132,4},{133,5},{134,6},{135,7},{1... | collective-permute-start | bytes 221192 | tf_op jit(solution)/shard_map/ppermute | solution.py:339
  25.4 17.9 %copy-start = (bf16[1,2,8,16,128]{4,3,2,1,0:T(8,128)(2,1)S(1)}, bf16[1,2,8,16,128]{4,3,2,1,0:T(8,128)(2,1)}, u32[]{:S(2)}) copy-start(bf16[1,2,8,16,128]{4,3,2,1,0:T(8,128)(2,1)} %param.7) | copy-start | bytes 196612
  25.4 17.9 %collective-permute-start.10 = (bf16[12,24,128]{2,1,0:T(8,128)(2,1)S(1)}, bf16[12,24,128]{2,1,0:T(8,128)(2,1)S(1)}, u32[]{:S(2)}, u32[]{:S(2)}) collective-permute-start(bf16[12,24,128]{2,1,0:T(8,128)(2,1)S(1)} %shard_map.92), channel_id=1, source_target_pairs={{128,0},{129,1},{130,2},{131,3},{132,4},{133,5},{134,6},{135,7},{1... | collective-permute-start | bytes 221192 | tf_op jit(solution)/shard_map/ppermute | solution.py:339
  101.2 7.4 %collective-permute-start.11 = (bf16[32,1,36,128]{3,2,1,0:T(8,128)(2,1)S(1)}, bf16[32,1,36,128]{3,2,1,0:T(8,128)(2,1)S(1)}, u32[]{:S(2)}, u32[]{:S(2)}) collective-permute-start(bf16[32,1,36,128]{3,2,1,0:T(8,128)(2,1)S(1)} %all_to_all.17), channel_id=1, source_target_pairs={{0,8},{8,0},{1,9},{9,1},{2,10},{10,2},{3,11},{11,3},{4,12},{12,4},... | collective-permute-start | bytes 884744 | tf_op jit(solution)/shard_map/ppermute | solution.py:251

commit v10 on v8

--- a/solution.py
+++ b/solution.py
@@ -10,8 +10,7 @@
 
 ROW = ("row_0", "row_1")
 COL = ("col_0", "col_1")
-NEAR = ("row_1", "col_1")
-FAR = ("row_0", "col_0")
+PLANE = ("row_0", "col_1")
 VMEM = pl.BlockSpec(memory_space=pltpu.VMEM)
 SMEM = pl.BlockSpec(memory_space=pltpu.SMEM)
 PARAMS = pltpu.CompilerParams(vmem_limit_bytes=24 * 1024 * 1024)
@@ -175,19 +174,21 @@
 
 def last_kernel(*refs, micros, early):
     last, masks, first, second, scale, inputs, act, *rest = refs
-    out, partial, frame, pairs, pack = rest[-5:]
+    out, keep, give, frame, pairs, pack = rest[-6:]
     ready = rest[: 3 * early]
-    received = rest[3 * early : -5]
+    received = rest[3 * early : -6]
     units = [[ref[...] for ref in ready[3 * m : 3 * m + 3]] for m in range(early)]
     scratch = (frame, pairs, pack)
     units.append(settle(last, masks, micros - 1, received, first, second, scale, *scratch))
     for micro, (tile, _, _) in enumerate(units):
         out[micro] = tile
     width = scale.shape[1]
-    for which, cells in enumerate((inputs, act)):
-        total = filter_grad(cells, [u[1 + which] for u in units]).astype(jnp.bfloat16)
-        for k in range(9):
-            partial[which, k] = total[:, k * width : (k + 1) * width]
+    firsts, seconds = [filter_grad(c, [u[1 + k] for u in units]) for k, c in enumerate((inputs, act))]
+    for k in range(9):
+        part = slice(k * width, (k + 1) * width)
+        pair = (firsts[:, part], seconds[:, part])
+        keep[k] = jnp.where(last[1] > 0, pair[0], pair[1]).astype(jnp.bfloat16)
+        give[k] = jnp.where(last[1] > 0, pair[1], pair[0]).astype(jnp.bfloat16)
 
 
 def cross(cells, axis):
@@ -220,16 +221,53 @@
     return lax.all_to_all(jnp.broadcast_to(block[None], (count, *block.shape)), axes, 0, 0, tiled=True)
 
 
-def total_of(x, factor):
-    near, stack = (lax.axis_size(NEAR), lax.axis_size("row_0"))
-    width = x.shape[-1]
-    part = sum_of_blocks(x.reshape(near, -1, width), NEAR).astype(jnp.bfloat16)
-    part = part.reshape(stack, 1, -1, width)
-    twice = jnp.broadcast_to(part, (stack, lax.axis_size("col_0"), *part.shape[2:]))
-    own = sum_of_blocks(twice.reshape(-1, *part.shape[2:]), FAR)
-    own = (own * factor).astype(jnp.bfloat16)
-    part = copies(own, "row_0").reshape(-1, width)
-    return copies(part, NEAR).reshape(x.shape).astype(jnp.float32)
+def write_kernel(first_core, half, other, out, lines, done, *, chunks):
+    pieces, rows, _ = half.shape
+    size = pieces // chunks * rows
+    moves = []
+    for core in range(2):
+        mine = first_core[0] > 0 if core == 0 else first_core[0] == 0
+        for k in range(pieces):
+            value = jnp.where(mine, half[k].astype(jnp.float32), other[k].astype(jnp.float32))
+            start = (core * pieces + k) * rows
+            lines[start : start + rows] = value
+            if (start + rows) % size == 0:
+                part = pl.ds(start + rows - size, size)
+                move = pltpu.make_async_copy(lines.at[part], out.at[part], done.at[len(moves)])
+                move.start()
+                moves.append(move)
+    for move in moves:
+        move.wait()
+
+
+def total_of(keep, give, factor):
+    width = keep.shape[-1]
+    pieces = lax.axis_size(PLANE)
+    swapped = [(0, 1), (1, 0)]
+    taken = lax.ppermute(give, "row_1", swapped)
+    both = keep.astype(jnp.float32) + taken.astype(jnp.float32)
+    blocks = both.astype(jnp.bfloat16).reshape(pieces, -1, width)
+    part = sum_of_blocks(blocks, PLANE).astype(jnp.bfloat16)
+    beyond = lax.ppermute(part, "col_0", swapped)
+    own = (part.astype(jnp.float32) + beyond.astype(jnp.float32)) * factor
+    half = copies(own.astype(jnp.bfloat16), PLANE)
+    half = half.reshape(pieces, -1, width)
+    other = lax.ppermute(half, "row_1", swapped)
+    first_core = (lax.axis_index("row_1") == 0).astype(jnp.int32).reshape(1)
+    lines = 2 * keep.size // width
+    chunks = 4
+    return pl.pallas_call(
+        functools.partial(write_kernel, chunks=chunks),
+        name="write",
+        in_specs=[SMEM, VMEM, VMEM],
+        out_specs=pl.BlockSpec(memory_space=pltpu.MemorySpace.HBM),
+        out_shape=jax.ShapeDtypeStruct((lines, width), jnp.float32),
+        scratch_shapes=[
+            pltpu.VMEM((lines, width), jnp.float32),
+            pltpu.SemaphoreType.DMA((2 * chunks,)),
+        ],
+        compiler_params=PARAMS,
+    )(first_core, half, other)
 
 
 def section_backward(section_input, first_pre, second_pre, out_grad, kernels, bn_scale, bn_shift):
@@ -320,21 +358,23 @@
             compiler_params=PARAMS,
         )(*common, *arrived[micro])
     taken = ready + arrived[-1]
-    input_grad, partial = pl.pallas_call(
+    first_core = (lax.axis_index("row_1") == 0).astype(jnp.int32).reshape(1)
+    input_grad, keep, give = pl.pallas_call(
         functools.partial(last_kernel, micros=micros, early=micros - 1),
         name="last",
         in_specs=[SMEM] + [VMEM] * (6 + len(taken)),
-        out_specs=[VMEM] * 2,
+        out_specs=[VMEM] * 3,
         out_shape=[
             jax.ShapeDtypeStruct(out_grad.shape, bf16),
-            jax.ShapeDtypeStruct((2, 9, width, width), bf16),
+            jax.ShapeDtypeStruct((9, width, width), bf16),
+            jax.ShapeDtypeStruct((9, width, width), bf16),
         ],
         scratch_shapes=scratch,
         compiler_params=PARAMS,
-    )(*common, section_input[0], act, *taken)
+    )(jnp.concatenate([last, first_core]), *common[1:], section_input[0], act, *taken)
     pixels = micros * rows_here * lax.axis_size(ROW) * cols_here * lax.axis_size(COL)
     factor = 1.0 / jnp.sqrt(jnp.float32(pixels))
-    total = total_of(partial, factor).reshape(2, 3, 3, width, width)
+    total = total_of(keep, give, factor).reshape(2, 3, 3, width, width)
     return (input_grad[None], total[None])
 
 

time: 114 us -> 111 us (0.974)
  blocking collectives: 67.6 us -> 42.7 us
  starting transfers between devices: 21.7 us -> 35.5 us
  waiting for transfers between devices: 17.2 us -> 24.2 us
  Pallas kernels: 3.69 us -> 5.33 us
    all_to_all x2 -> x1, blocking collectives: 42.2 us -> 27.4 us  [sum_of_blocks(): parts = lax.all_to_all(blocks, axes, 0, 0, tiled=True)]
    ppermute x0 -> x3, starting transfers between devices: none -> 13.9 us  [the longest x1 6.53 us: total_of(): other = lax.ppermute(half, 'row_1', swapped)]
    all_to_all x2 -> x1, blocking collectives: 25.4 us -> 15.4 us  [copies(): lax.all_to_all(jnp.broadcast_to(block[None], (count, *block.shape)), axes...]
    ppermute x0 -> x3, waiting for transfers between devices: none -> 7.07 us  [the longest x1 4.65 us: total_of(): beyond = lax.ppermute(part, 'col_0', swapped)]
  transfers between devices with their start and end apart: 11 -> 14, of which waited for: 3 -> 6; matrix products, arithmetic and copies ran while one was open for 1% -> 1% of each run, Pallas kernels for 1% -> 1%
where the time goes in v10:
time: 111 us; the launch traced here: 110 us
  blocking collectives  42.7 us (38%)
  starting transfers between devices  35.5 us (32%)
  waiting for transfers between devices  24.2 us (22%)
  Pallas kernels  5.33 us (5%)
    all_to_all x1, blocking collectives, sum_of_blocks(): parts = lax.all_to_all(blocks, axes, 0, 0, tiled=True)  27.4 us
    ppermute x6, waiting for transfers between devices, section_backward(): sent.append(lax.ppermute(result, 'section', pair))  15.7 us
    all_to_all x1, blocking collectives, copies(): lax.all_to_all(jnp.broadcast_to(block[None], (count, *block.shape)), axes...  15.4 us
    ppermute x2, starting transfers between devices, swap(): lax.ppermute(cells, axis, [(i, i ^ 1) for i in range(lax.axis_size(axis))])  8.31 us
    ppermute x3, starting transfers between devices, cross(): return lax.ppermute(cells, axis, pairs + [(j, i) for i, j in pairs])  7.97 us
    ppermute x1, starting transfers between devices, total_of(): other = lax.ppermute(half, 'row_1', swapped)  6.53 us
    ppermute x6, starting transfers between devices, section_backward(): sent.append(lax.ppermute(result, 'section', pair))  5.39 us
    ppermute x1, waiting for transfers between devices, total_of(): beyond = lax.ppermute(part, 'col_0', swapped)  4.65 us
  transfers between devices with their start and end apart: 14, of which 6 were waited for; matrix products, arithmetic and copies ran while one was open for 1% of the time, Pallas kernels for 1%

profile of v10, /device:TPU:1, one launch (start us, length us, event | category | flops | bytes accessed | tf_op | source)
XLA Modules:
  0.0 110.2 jit_solution(17226764862452445216)
XLA Ops:
  0.7 1.6 %prepare.1 = (bf16[2,2,8,16,128]{4,3,2,1,0:T(8,128)(2,1)S(1)}, bf16[2,2,8,8,128]{4,3,2,1,0:T(8,128)(2,1)S(1)}, bf16[2,2,8,8,128]{4,3,2,1,0:T(8,128)(2,1)S(1)}, b...) custom-call(s32[2]{0:T(128)S(1)} %pad_add_fusion.1.flags, bf16[2,8,16,128]{3,2,1,0:T(8,128)(2,1)} %bitcast.46, ...), custom_call_target="tpu_custom_call" | custom-call | tf_op jit(solution)/shard_map/prepare/pallas_call | solution.py:281
  2.4 0.7 collective-permute-start
  3.0 6.4 %collective-permute-start.1 = (bf16[2,2,8,8,128]{4,3,2,1,0:T(8,128)(2,1)S(1)}, bf16[2,2,8,8,128]{4,3,2,1,0:T(8,128)(2,1)S(1)}, u32[]{:S(2)}, u32[]{:S(2)}) collective-permute-start(bf16[2,2,8,8,128]{4,3,2,1,0:T(8,128)(2,1)S(1)} %get-tuple-element.16), channel_id=1, source_target_pairs={{0,1},{1,0},{2,3},{3,2},{4,5},{5,4},{6,7},{7,6},{8,9},{9,8},{10,11... | collective-permute-start | bytes 196616 | tf_op jit(solution)/shard_map/ppermute | solution.py:201
  9.4 5.1 %collective-permute-start.3 = (bf16[2,2,8,16,128]{4,3,2,1,0:T(8,128)(2,1)S(1)}, bf16[2,2,8,16,128]{4,3,2,1,0:T(8,128)(2,1)S(1)}, u32[]{:S(2)}, u32[]{:S(2)}) collective-permute-start(bf16[2,2,8,16,128]{4,3,2,1,0:T(8,128)(2,1)S(1)} %get-tuple-element.18), channel_id=1, source_target_pairs={{8,16},{24,32},{40,48},{56,64},{72,80},{88,96},{104,112},{16,8},{3... | collective-permute-start | bytes 393224 | tf_op jit(solution)/shard_map/ppermute | solution.py:197
  14.7 2.2 %collective-permute-start.2 = (bf16[2,2,8,16,128]{4,3,2,1,0:T(8,128)(2,1)S(1)}, bf16[2,2,8,16,128]{4,3,2,1,0:T(8,128)(2,1)S(1)}, u32[]{:S(2)}, u32[]{:S(2)}) collective-permute-start(bf16[2,2,8,16,128]{4,3,2,1,0:T(8,128)(2,1)S(1)} %pad_maximum_fusion.3), channel_id=1, source_target_pairs={{8,16},{24,32},{40,48},{56,64},{72,80},{88,96},{104,112},{16,8},{3... | collective-permute-start | bytes 393224 | tf_op jit(solution)/shard_map/ppermute | solution.py:197
  16.9 1.9 %collective-permute-start.4 = (bf16[2,2,8,32,128]{4,3,2,1,0:T(8,128)(2,1)S(1)}, bf16[2,2,8,32,128]{4,3,2,1,0:T(8,128)(2,1)S(1)}, u32[]{:S(2)}, u32[]{:S(2)}) collective-permute-start(bf16[2,2,8,32,128]{4,3,2,1,0:T(8,128)(2,1)S(1)} %pad_maximum_fusion.2), channel_id=1, source_target_pairs={{0,8},{8,0},{16,24},{24,16},{32,40},{40,32},{48,56},{56,48},{64,72... | collective-permute-start | bytes 786440 | tf_op jit(solution)/shard_map/ppermute | solution.py:201
  19.0 0.2 copy.12
  19.3 0.2 copy.11
  19.6 1.4 %collective-permute-done.2 = bf16[2,2,8,16,128]{4,3,2,1,0:T(8,128)(2,1)S(1)} collective-permute-done((bf16[2,2,8,16,128]{4,3,2,1,0:T(8,128)(2,1)S(1)}, bf16[2,2,8,16,128]{4,3,2,1,0:T(8,128)(2,1)S(1)}, u32[]{:S(2)}, u32[]{:S(2)}) %collective-permute-start.2) | collective-permute-done | bytes 131104 | tf_op jit(solution)/shard_map/ppermute | solution.py:197
  21.0 0.1 broadcast_select_fusion.1
  21.1 0.1 pad_maximum_fusion.refs_1_
  21.2 0.7 collective-permute-start.5
  21.9 0.7 collective-permute-start.8
  22.6 0.7 collective-permute-start.6
  23.3 0.7 collective-permute-start.9
  24.1 1.3 %collective-permute-start.7 = (bf16[12,24,128]{2,1,0:T(8,128)(2,1)S(1)}, bf16[12,24,128]{2,1,0:T(8,128)(2,1)S(1)}, u32[]{:S(2)}, u32[]{:S(2)}) collective-permute-start(bf16[12,24,128]{2,1,0:T(8,128)(2,1)S(1)} %shard_map.88), channel_id=1, source_target_pairs={{128,0},{129,1},{130,2},{131,3},{132,4},{133,5},{134,6},{135,7},{1... | collective-permute-start | bytes 221192 | tf_op jit(solution)/shard_map/ppermute | solution.py:344
  25.4 1.4 %collective-permute-start.10 = (bf16[12,24,128]{2,1,0:T(8,128)(2,1)S(1)}, bf16[12,24,128]{2,1,0:T(8,128)(2,1)S(1)}, u32[]{:S(2)}, u32[]{:S(2)}) collective-permute-start(bf16[12,24,128]{2,1,0:T(8,128)(2,1)S(1)} %shard_map.92), channel_id=1, source_target_pairs={{128,0},{129,1},{130,2},{131,3},{132,4},{133,5},{134,6},{135,7},{1... | collective-permute-start | bytes 221192 | tf_op jit(solution)/shard_map/ppermute | solution.py:344
  26.8 0.1 pad_add_fusion.refs_0_
  26.9 14.5 %collective-permute-done.7.refs_7_ = bf16[12,24,128]{2,1,0:T(8,128)(2,1)S(1)} collective-permute-done((bf16[12,24,128]{2,1,0:T(8,128)(2,1)S(1)}, bf16[12,24,128]{2,1,0:T(8,128)(2,1)S(1)}, u32[]{:S(2)}, u32[]{:S(2)}) %collective-permute-start.7) | collective-permute-done | bytes 73760 | tf_op jit(solution)/shard_map/ppermute | solution.py:344
  41.4 0.6 shard_map.89
  42.0 1.2 %collective-permute-done.10.refs_12_ = bf16[12,24,128]{2,1,0:T(8,128)(2,1)S(1)} collective-permute-done((bf16[12,24,128]{2,1,0:T(8,128)(2,1)S(1)}, bf16[12,24,128]{2,1,0:T(8,128)(2,1)S(1)}, u32[]{:S(2)}, u32[]{:S(2)}) %collective-permute-start.10) | collective-permute-done | bytes 73760 | tf_op jit(solution)/shard_map/ppermute | solution.py:344
  43.3 1.9 %last.1 = (bf16[2,8,16,128]{3,2,1,0:T(8,128)(2,1)}, bf16[9,128,128]{2,1,0:T(8,128)(2,1)S(1)}, bf16[9,128,128]{2,1,0:T(8,128)(2,1)S(1)}) custom-call(s32[2]{0:T(128)S(1)} %pad_add_fusion.refs_0_, bf16[2,2,24,32,128]{4,3,2,1,0:T(8,128)(2,1)S(1)} %pad_maximum_fusion.refs_1_, bf16[384,384]{1,0:T(8,128)(2,1)S(1)} %bitcast.45, bf16[384,384]{1,0:T(8,128)(2,1)S(1)} %bitcast.37, ...), custom_call_target="tpu_custom_call" | custom-call | tf_op jit(solution)/shard_map/last/pallas_call | solution.py:362
  45.2 3.7 %collective-permute-start.11 = (bf16[9,128,128]{2,1,0:T(8,128)(2,1)S(1)}, bf16[9,128,128]{2,1,0:T(8,128)(2,1)S(1)}, u32[]{:S(2)}, u32[]{:S(2)}) collective-permute-start(bf16[9,128,128]{2,1,0:T(8,128)(2,1)S(1)} %get-tuple-element.27), channel_id=1, source_target_pairs={{0,8},{8,0},{1,9},{9,1},{2,10},{10,2},{3,11},{11,3},{4,12},{12,4},... | collective-permute-start | bytes 884744 | tf_op jit(solution)/shard_map/ppermute | solution.py:247
  48.8 1.2 %collective-permute-done.11 = bf16[9,128,128]{2,1,0:T(8,128)(2,1)S(1)} collective-permute-done((bf16[9,128,128]{2,1,0:T(8,128)(2,1)S(1)}, bf16[9,128,128]{2,1,0:T(8,128)(2,1)S(1)}, u32[]{:S(2)}, u32[]{:S(2)}) %collective-permute-start.11) | collective-permute-done | bytes 294944 | tf_op jit(solution)/shard_map/ppermute | solution.py:247
  50.0 0.1 add_convert_fusion
  50.2 27.4 %all_to_all.10 = bf16[32,36,128]{2,1,0:T(8,128)(2,1)S(1)} all-to-all(bf16[32,36,128]{2,1,0:T(8,128)(2,1)S(1)} %reshape.54), channel_id=1, replica_groups=mesh['section'=4,'row_0'=8,'row_1'=2,'col_0'=2,'col_1'=4] {'row_0','col_1'}, dimensions={0} | all-to-all | bytes 589824 | tf_op jit(solution)/shard_map/all_to_all | solution.py:215
  77.6 3.7 %collective-permute-start.12 = (bf16[36,128]{1,0:T(8,128)(2,1)S(1)}, bf16[36,128]{1,0:T(8,128)(2,1)S(1)}, u32[]{:S(2)}, u32[]{:S(2)}) collective-permute-start(bf16[36,128]{1,0:T(8,128)(2,1)S(1)} %reduce_sum.12), channel_id=1, source_target_pairs={{0,4},{4,0},{1,5},{5,1},{2,6},{6,2},{3,7},{7,3},{8,12},{12,8},{9,1... | collective-permute-start | bytes 27656 | tf_op jit(solution)/shard_map/ppermute | solution.py:251
  81.3 4.6 %collective-permute-done.12 = bf16[36,128]{1,0:T(8,128)(2,1)S(1)} collective-permute-done((bf16[36,128]{1,0:T(8,128)(2,1)S(1)}, bf16[36,128]{1,0:T(8,128)(2,1)S(1)}, u32[]{:S(2)}, u32[]{:S(2)}) %collective-permute-start.12) | collective-permute-done | bytes 9248 | tf_op jit(solution)/shard_map/ppermute | solution.py:251
  86.0 15.4 %all_to_all.11.half = bf16[32,36,128]{2,1,0:T(8,128)(2,1)S(1)} all-to-all(bf16[32,36,128]{2,1,0:T(8,128)(2,1)S(1)} %broadcast_in_dim.10), channel_id=1, replica_groups=mesh['section'=4,'row_0'=8,'row_1'=2,'col_0'=2,'col_1'=4] {'row_0','col_1'}, dimensions={0} | all-to-all | bytes 589824 | tf_op jit(solution)/shard_map/all_to_all | solution.py:221
  101.4 6.5 %collective-permute-start.13 = (bf16[32,36,128]{2,1,0:T(8,128)(2,1)S(1)}, bf16[32,36,128]{2,1,0:T(8,128)(2,1)S(1)}, u32[]{:S(2)}, u32[]{:S(2)}) collective-permute-start(bf16[32,36,128]{2,1,0:T(8,128)(2,1)S(1)} %all_to_all.11.half), channel_id=1, source_target_pairs={{0,8},{8,0},{1,9},{9,1},{2,10},{10,2},{3,11},{11,3},{4,12},{12,4},... | collective-permute-start | bytes 884744 | tf_op jit(solution)/shard_map/ppermute | solution.py:255
  107.9 1.2 %collective-permute-done.13.other = bf16[32,36,128]{2,1,0:T(8,128)(2,1)S(1)} collective-permute-done((bf16[32,36,128]{2,1,0:T(8,128)(2,1)S(1)}, bf16[32,36,128]{2,1,0:T(8,128)(2,1)S(1)}, u32[]{:S(2)}, u32[]{:S(2)}) %collective-permute-start.13) | collective-permute-done | bytes 294944 | tf_op jit(solution)/shard_map/ppermute | solution.py:255
  109.2 1.1 write.1
  (32 shorter events, 0.7 us)
Async XLA Ops:
  0.6 18.2 %copy-start.1 = (bf16[1,2,3,3,128,128]{5,4,3,2,1,0:T(8,128)(2,1)S(1)}, bf16[1,2,3,3,128,128]{5,4,3,2,1,0:T(8,128)(2,1)}, u32[]{:S(2)}) copy-start(bf16[1,2,3,3,128,128]{5,4,3,2,1,0:T(8,128)(2,1)} %param.11) | copy-start | bytes 1769476
  2.4 12.2 %collective-permute-start = (bf16[2,2,8,8,128]{4,3,2,1,0:T(8,128)(2,1)S(1)}, bf16[2,2,8,8,128]{4,3,2,1,0:T(8,128)(2,1)S(1)}, u32[]{:S(2)}, u32[]{:S(2)}) collective-permute-start(bf16[2,2,8,8,128]{4,3,2,1,0:T(8,128)(2,1)S(1)} %get-tuple-element.15), channel_id=1, source_target_pairs={{1,2},{3,4},{5,6},{2,1},{4,3},{6,5},{9,10},{11,12},{13,14},{10,9},... | collective-permute-start | bytes 196616 | tf_op jit(solution)/shard_map/ppermute | solution.py:197
  3.0 11.6 %collective-permute-start.1 = (bf16[2,2,8,8,128]{4,3,2,1,0:T(8,128)(2,1)S(1)}, bf16[2,2,8,8,128]{4,3,2,1,0:T(8,128)(2,1)S(1)}, u32[]{:S(2)}, u32[]{:S(2)}) collective-permute-start(bf16[2,2,8,8,128]{4,3,2,1,0:T(8,128)(2,1)S(1)} %get-tuple-element.16), channel_id=1, source_target_pairs={{0,1},{1,0},{2,3},{3,2},{4,5},{5,4},{6,7},{7,6},{8,9},{9,8},{10,11... | collective-permute-start | bytes 196616 | tf_op jit(solution)/shard_map/ppermute | solution.py:201
  9.4 11.6 %collective-permute-start.3 = (bf16[2,2,8,16,128]{4,3,2,1,0:T(8,128)(2,1)S(1)}, bf16[2,2,8,16,128]{4,3,2,1,0:T(8,128)(2,1)S(1)}, u32[]{:S(2)}, u32[]{:S(2)}) collective-permute-start(bf16[2,2,8,16,128]{4,3,2,1,0:T(8,128)(2,1)S(1)} %get-tuple-element.18), channel_id=1, source_target_pairs={{8,16},{24,32},{40,48},{56,64},{72,80},{88,96},{104,112},{16,8},{3... | collective-permute-start | bytes 393224 | tf_op jit(solution)/shard_map/ppermute | solution.py:197
  14.7 6.3 %collective-permute-start.2 = (bf16[2,2,8,16,128]{4,3,2,1,0:T(8,128)(2,1)S(1)}, bf16[2,2,8,16,128]{4,3,2,1,0:T(8,128)(2,1)S(1)}, u32[]{:S(2)}, u32[]{:S(2)}) collective-permute-start(bf16[2,2,8,16,128]{4,3,2,1,0:T(8,128)(2,1)S(1)} %pad_maximum_fusion.3), channel_id=1, source_target_pairs={{8,16},{24,32},{40,48},{56,64},{72,80},{88,96},{104,112},{16,8},{3... | collective-permute-start | bytes 393224 | tf_op jit(solution)/shard_map/ppermute | solution.py:197
  16.9 4.1 %collective-permute-start.4 = (bf16[2,2,8,32,128]{4,3,2,1,0:T(8,128)(2,1)S(1)}, bf16[2,2,8,32,128]{4,3,2,1,0:T(8,128)(2,1)S(1)}, u32[]{:S(2)}, u32[]{:S(2)}) collective-permute-start(bf16[2,2,8,32,128]{4,3,2,1,0:T(8,128)(2,1)S(1)} %pad_maximum_fusion.2), channel_id=1, source_target_pairs={{0,8},{8,0},{16,24},{24,16},{32,40},{40,32},{48,56},{56,48},{64,72... | collective-permute-start | bytes 786440 | tf_op jit(solution)/shard_map/ppermute | solution.py:201
  21.2 1.4 %collective-permute-start.5 = (bf16[10,56,128]{2,1,0:T(8,128)(2,1)S(1)}, bf16[10,56,128]{2,1,0:T(8,128)(2,1)S(1)}, u32[]{:S(2)}, u32[]{:S(2)}) collective-permute-start(bf16[10,56,128]{2,1,0:T(8,128)(2,1)S(1)} %shard_map.86), channel_id=1, source_target_pairs={{384,256},{385,257},{386,258},{387,259},{388,260},{389,261},{390,2... | collective-permute-start | bytes 430088 | tf_op jit(solution)/shard_map/ppermute | solution.py:344
  21.9 1.4 %collective-permute-start.8 = (bf16[10,56,128]{2,1,0:T(8,128)(2,1)S(1)}, bf16[10,56,128]{2,1,0:T(8,128)(2,1)S(1)}, u32[]{:S(2)}, u32[]{:S(2)}) collective-permute-start(bf16[10,56,128]{2,1,0:T(8,128)(2,1)S(1)} %shard_map.90), channel_id=1, source_target_pairs={{384,256},{385,257},{386,258},{387,259},{388,260},{389,261},{390,2... | collective-permute-start | bytes 430088 | tf_op jit(solution)/shard_map/ppermute | solution.py:344
  22.6 1.4 %collective-permute-start.6 = (bf16[16,24,128]{2,1,0:T(8,128)(2,1)S(1)}, bf16[16,24,128]{2,1,0:T(8,128)(2,1)S(1)}, u32[]{:S(2)}, u32[]{:S(2)}) collective-permute-start(bf16[16,24,128]{2,1,0:T(8,128)(2,1)S(1)} %shard_map.87), channel_id=1, source_target_pairs={{256,128},{257,129},{258,130},{259,131},{260,132},{261,133},{262,1... | collective-permute-start | bytes 294920 | tf_op jit(solution)/shard_map/ppermute | solution.py:344
  23.3 2.0 %collective-permute-start.9 = (bf16[16,24,128]{2,1,0:T(8,128)(2,1)S(1)}, bf16[16,24,128]{2,1,0:T(8,128)(2,1)S(1)}, u32[]{:S(2)}, u32[]{:S(2)}) collective-permute-start(bf16[16,24,128]{2,1,0:T(8,128)(2,1)S(1)} %shard_map.91), channel_id=1, source_target_pairs={{256,128},{257,129},{258,130},{259,131},{260,132},{261,133},{262,1... | collective-permute-start | bytes 294920 | tf_op jit(solution)/shard_map/ppermute | solution.py:344
  24.1 17.3 %collective-permute-start.7 = (bf16[12,24,128]{2,1,0:T(8,128)(2,1)S(1)}, bf16[12,24,128]{2,1,0:T(8,128)(2,1)S(1)}, u32[]{:S(2)}, u32[]{:S(2)}) collective-permute-start(bf16[12,24,128]{2,1,0:T(8,128)(2,1)S(1)} %shard_map.88), channel_id=1, source_target_pairs={{128,0},{129,1},{130,2},{131,3},{132,4},{133,5},{134,6},{135,7},{1... | collective-permute-start | bytes 221192 | tf_op jit(solution)/shard_map/ppermute | solution.py:344
  25.4 17.9 %copy-start = (bf16[1,2,8,16,128]{4,3,2,1,0:T(8,128)(2,1)S(1)}, bf16[1,2,8,16,128]{4,3,2,1,0:T(8,128)(2,1)}, u32[]{:S(2)}) copy-start(bf16[1,2,8,16,128]{4,3,2,1,0:T(8,128)(2,1)} %param.7) | copy-start | bytes 196612
  25.4 17.9 %collective-permute-start.10 = (bf16[12,24,128]{2,1,0:T(8,128)(2,1)S(1)}, bf16[12,24,128]{2,1,0:T(8,128)(2,1)S(1)}, u32[]{:S(2)}, u32[]{:S(2)}) collective-permute-start(bf16[12,24,128]{2,1,0:T(8,128)(2,1)S(1)} %shard_map.92), channel_id=1, source_target_pairs={{128,0},{129,1},{130,2},{131,3},{132,4},{133,5},{134,6},{135,7},{1... | collective-permute-start | bytes 221192 | tf_op jit(solution)/shard_map/ppermute | solution.py:344
  45.2 4.9 %collective-permute-start.11 = (bf16[9,128,128]{2,1,0:T(8,128)(2,1)S(1)}, bf16[9,128,128]{2,1,0:T(8,128)(2,1)S(1)}, u32[]{:S(2)}, u32[]{:S(2)}) collective-permute-start(bf16[9,128,128]{2,1,0:T(8,128)(2,1)S(1)} %get-tuple-element.27), channel_id=1, source_target_pairs={{0,8},{8,0},{1,9},{9,1},{2,10},{10,2},{3,11},{11,3},{4,12},{12,4},... | collective-permute-start | bytes 884744 | tf_op jit(solution)/shard_map/ppermute | solution.py:247
  77.6 8.3 %collective-permute-start.12 = (bf16[36,128]{1,0:T(8,128)(2,1)S(1)}, bf16[36,128]{1,0:T(8,128)(2,1)S(1)}, u32[]{:S(2)}, u32[]{:S(2)}) collective-permute-start(bf16[36,128]{1,0:T(8,128)(2,1)S(1)} %reduce_sum.12), channel_id=1, source_target_pairs={{0,4},{4,0},{1,5},{5,1},{2,6},{6,2},{3,7},{7,3},{8,12},{12,8},{9,1... | collective-permute-start | bytes 27656 | tf_op jit(solution)/shard_map/ppermute | solution.py:251
  101.4 7.8 %collective-permute-start.13 = (bf16[32,36,128]{2,1,0:T(8,128)(2,1)S(1)}, bf16[32,36,128]{2,1,0:T(8,128)(2,1)S(1)}, u32[]{:S(2)}, u32[]{:S(2)}) collective-permute-start(bf16[32,36,128]{2,1,0:T(8,128)(2,1)S(1)} %all_to_all.11.half), channel_id=1, source_target_pairs={{0,8},{8,0},{1,9},{9,1},{2,10},{10,2},{3,11},{11,3},{4,12},{12,4},... | collective-permute-start | bytes 884744 | tf_op jit(solution)/shard_map/ppermute | solution.py:255

commit v11 on v10

--- a/solution.py
+++ b/solution.py
@@ -10,7 +10,7 @@
 
 ROW = ("row_0", "row_1")
 COL = ("col_0", "col_1")
-PLANE = ("row_0", "col_1")
+PLANE = ("row_0", "col_0", "col_1")
 VMEM = pl.BlockSpec(memory_space=pltpu.VMEM)
 SMEM = pl.BlockSpec(memory_space=pltpu.SMEM)
 PARAMS = pltpu.CompilerParams(vmem_limit_bytes=24 * 1024 * 1024)
@@ -142,7 +142,7 @@
         for j in range(3):
             parts = [s[j][2 - i : 2 - i + height].reshape(-1, width) for s in spread]
             sides.append(jnp.concatenate(parts, axis=0))
-    flat = cells[...].reshape(-1, width)
+    flat = cells.reshape(-1, width)
     side = jnp.concatenate(sides, axis=1)
     return lax.dot_general(
         flat, side, (((0,), (0,)), ((), ())), preferred_element_type=jnp.float32
@@ -183,12 +183,13 @@
     for micro, (tile, _, _) in enumerate(units):
         out[micro] = tile
     width = scale.shape[1]
-    firsts, seconds = [filter_grad(c, [u[1 + k] for u in units]) for k, c in enumerate((inputs, act))]
-    for k in range(9):
-        part = slice(k * width, (k + 1) * width)
-        pair = (firsts[:, part], seconds[:, part])
-        keep[k] = jnp.where(last[1] > 0, pair[0], pair[1]).astype(jnp.bfloat16)
-        give[k] = jnp.where(last[1] > 0, pair[1], pair[0]).astype(jnp.bfloat16)
+    wide = jnp.float32
+    for out_ref, mine in ((give, last[1] == 0), (keep, last[1] > 0)):
+        cells = jnp.where(mine, inputs[...].astype(wide), act[...].astype(wide))
+        windows = [jnp.where(mine, u[1].astype(wide), u[2].astype(wide)) for u in units]
+        total = filter_grad(cells.astype(jnp.bfloat16), windows).astype(jnp.bfloat16)
+        for k in range(9):
+            out_ref[k] = total[:, k * width : (k + 1) * width]
 
 
 def cross(cells, axis):
@@ -247,9 +248,7 @@
     taken = lax.ppermute(give, "row_1", swapped)
     both = keep.astype(jnp.float32) + taken.astype(jnp.float32)
     blocks = both.astype(jnp.bfloat16).reshape(pieces, -1, width)
-    part = sum_of_blocks(blocks, PLANE).astype(jnp.bfloat16)
-    beyond = lax.ppermute(part, "col_0", swapped)
-    own = (part.astype(jnp.float32) + beyond.astype(jnp.float32)) * factor
+    own = sum_of_blocks(blocks, PLANE) * factor
     half = copies(own.astype(jnp.bfloat16), PLANE)
     half = half.reshape(pieces, -1, width)
     other = lax.ppermute(half, "row_1", swapped)

time: 111 us -> 113 us (1.018)
  blocking collectives: 42.7 us -> 54.8 us
  starting transfers between devices: 35.5 us -> 30.1 us
  waiting for transfers between devices: 24.2 us -> 19.6 us
    all_to_all x1, blocking collectives: 15.4 us -> 22.8 us  [copies(): lax.all_to_all(jnp.broadcast_to(block[None], (count, *block.shape)), axes...]
    all_to_all x1, blocking collectives: 27.4 us -> 32 us  [sum_of_blocks(): parts = lax.all_to_all(blocks, axes, 0, 0, tiled=True)]
    ppermute x1 -> x0, waiting for transfers between devices: 4.65 us -> none  [total_of(): beyond = lax.ppermute(part, 'col_0', swapped)]
    ppermute x1 -> x0, starting transfers between devices: 3.66 us -> none  [total_of(): beyond = lax.ppermute(part, 'col_0', swapped)]
    ppermute x1, starting transfers between devices: 6.53 us -> 4.76 us  [total_of(): other = lax.ppermute(half, 'row_1', swapped)]
  transfers between devices with their start and end apart: 14 -> 13, of which waited for: 6 -> 5; matrix products, arithmetic and copies ran while one was open for 1% -> 1% of each run, Pallas kernels for 1% -> 1%
where the time goes in v11:
time: 113 us; the launch traced here: 112 us
  blocking collectives  54.8 us (48%)
  starting transfers between devices  30.1 us (27%)
  waiting for transfers between devices  19.6 us (17%)
  Pallas kernels  5.34 us (5%)
    all_to_all x1, blocking collectives, sum_of_blocks(): parts = lax.all_to_all(blocks, axes, 0, 0, tiled=True)  32 us
    all_to_all x1, blocking collectives, copies(): lax.all_to_all(jnp.broadcast_to(block[None], (count, *block.shape)), axes...  22.8 us
    ppermute x6, waiting for transfers between devices, section_backward(): sent.append(lax.ppermute(result, 'section', pair))  15.7 us
    ppermute x2, starting transfers between devices, swap(): lax.ppermute(cells, axis, [(i, i ^ 1) for i in range(lax.axis_size(axis))])  8.31 us
    ppermute x3, starting transfers between devices, cross(): return lax.ppermute(cells, axis, pairs + [(j, i) for i, j in pairs])  7.97 us
    ppermute x6, starting transfers between devices, section_backward(): sent.append(lax.ppermute(result, 'section', pair))  5.39 us
    ppermute x1, starting transfers between devices, total_of(): other = lax.ppermute(half, 'row_1', swapped)  4.76 us
    ppermute x1, starting transfers between devices, total_of(): taken = lax.ppermute(give, 'row_1', swapped)  3.65 us
  transfers between devices with their start and end apart: 13, of which 5 were waited for; matrix products, arithmetic and copies ran while one was open for 1% of the time, Pallas kernels for 1%

profile of v11, /device:TPU:1, one launch (start us, length us, event | category | flops | bytes accessed | tf_op | source)
XLA Modules:
  0.0 112.4 jit_solution(12897389544396865296)
XLA Ops:
  0.7 1.6 %prepare.1 = (bf16[2,2,8,16,128]{4,3,2,1,0:T(8,128)(2,1)S(1)}, bf16[2,2,8,8,128]{4,3,2,1,0:T(8,128)(2,1)S(1)}, bf16[2,2,8,8,128]{4,3,2,1,0:T(8,128)(2,1)S(1)}, b...) custom-call(s32[2]{0:T(128)S(1)} %pad_add_fusion.1.flags, bf16[2,8,16,128]{3,2,1,0:T(8,128)(2,1)} %bitcast.46, ...), custom_call_target="tpu_custom_call" | custom-call | tf_op jit(solution)/shard_map/prepare/pallas_call | solution.py:280
  2.4 0.7 collective-permute-start
  3.0 6.4 %collective-permute-start.1 = (bf16[2,2,8,8,128]{4,3,2,1,0:T(8,128)(2,1)S(1)}, bf16[2,2,8,8,128]{4,3,2,1,0:T(8,128)(2,1)S(1)}, u32[]{:S(2)}, u32[]{:S(2)}) collective-permute-start(bf16[2,2,8,8,128]{4,3,2,1,0:T(8,128)(2,1)S(1)} %get-tuple-element.16), channel_id=1, source_target_pairs={{0,1},{1,0},{2,3},{3,2},{4,5},{5,4},{6,7},{7,6},{8,9},{9,8},{10,11... | collective-permute-start | bytes 196616 | tf_op jit(solution)/shard_map/ppermute | solution.py:202
  9.4 5.1 %collective-permute-start.3 = (bf16[2,2,8,16,128]{4,3,2,1,0:T(8,128)(2,1)S(1)}, bf16[2,2,8,16,128]{4,3,2,1,0:T(8,128)(2,1)S(1)}, u32[]{:S(2)}, u32[]{:S(2)}) collective-permute-start(bf16[2,2,8,16,128]{4,3,2,1,0:T(8,128)(2,1)S(1)} %get-tuple-element.18), channel_id=1, source_target_pairs={{8,16},{24,32},{40,48},{56,64},{72,80},{88,96},{104,112},{16,8},{3... | collective-permute-start | bytes 393224 | tf_op jit(solution)/shard_map/ppermute | solution.py:198
  14.7 2.2 %collective-permute-start.2 = (bf16[2,2,8,16,128]{4,3,2,1,0:T(8,128)(2,1)S(1)}, bf16[2,2,8,16,128]{4,3,2,1,0:T(8,128)(2,1)S(1)}, u32[]{:S(2)}, u32[]{:S(2)}) collective-permute-start(bf16[2,2,8,16,128]{4,3,2,1,0:T(8,128)(2,1)S(1)} %pad_maximum_fusion.3), channel_id=1, source_target_pairs={{8,16},{24,32},{40,48},{56,64},{72,80},{88,96},{104,112},{16,8},{3... | collective-permute-start | bytes 393224 | tf_op jit(solution)/shard_map/ppermute | solution.py:198
  16.9 1.9 %collective-permute-start.4 = (bf16[2,2,8,32,128]{4,3,2,1,0:T(8,128)(2,1)S(1)}, bf16[2,2,8,32,128]{4,3,2,1,0:T(8,128)(2,1)S(1)}, u32[]{:S(2)}, u32[]{:S(2)}) collective-permute-start(bf16[2,2,8,32,128]{4,3,2,1,0:T(8,128)(2,1)S(1)} %pad_maximum_fusion.2), channel_id=1, source_target_pairs={{0,8},{8,0},{16,24},{24,16},{32,40},{40,32},{48,56},{56,48},{64,72... | collective-permute-start | bytes 786440 | tf_op jit(solution)/shard_map/ppermute | solution.py:202
  19.0 0.2 copy.12
  19.3 0.2 copy.11
  19.6 1.4 %collective-permute-done.2 = bf16[2,2,8,16,128]{4,3,2,1,0:T(8,128)(2,1)S(1)} collective-permute-done((bf16[2,2,8,16,128]{4,3,2,1,0:T(8,128)(2,1)S(1)}, bf16[2,2,8,16,128]{4,3,2,1,0:T(8,128)(2,1)S(1)}, u32[]{:S(2)}, u32[]{:S(2)}) %collective-permute-start.2) | collective-permute-done | bytes 131104 | tf_op jit(solution)/shard_map/ppermute | solution.py:198
  21.0 0.1 broadcast_select_fusion.1
  21.1 0.1 pad_maximum_fusion.refs_1_
  21.2 0.7 collective-permute-start.5
  21.9 0.7 collective-permute-start.8
  22.6 0.7 collective-permute-start.6
  23.3 0.7 collective-permute-start.9
  24.1 1.3 %collective-permute-start.7 = (bf16[12,24,128]{2,1,0:T(8,128)(2,1)S(1)}, bf16[12,24,128]{2,1,0:T(8,128)(2,1)S(1)}, u32[]{:S(2)}, u32[]{:S(2)}) collective-permute-start(bf16[12,24,128]{2,1,0:T(8,128)(2,1)S(1)} %shard_map.88), channel_id=1, source_target_pairs={{128,0},{129,1},{130,2},{131,3},{132,4},{133,5},{134,6},{135,7},{1... | collective-permute-start | bytes 221192 | tf_op jit(solution)/shard_map/ppermute | solution.py:343
  25.4 1.4 %collective-permute-start.10 = (bf16[12,24,128]{2,1,0:T(8,128)(2,1)S(1)}, bf16[12,24,128]{2,1,0:T(8,128)(2,1)S(1)}, u32[]{:S(2)}, u32[]{:S(2)}) collective-permute-start(bf16[12,24,128]{2,1,0:T(8,128)(2,1)S(1)} %shard_map.92), channel_id=1, source_target_pairs={{128,0},{129,1},{130,2},{131,3},{132,4},{133,5},{134,6},{135,7},{1... | collective-permute-start | bytes 221192 | tf_op jit(solution)/shard_map/ppermute | solution.py:343
  26.8 0.1 pad_add_fusion.refs_0_
  26.9 14.5 %collective-permute-done.7.refs_7_ = bf16[12,24,128]{2,1,0:T(8,128)(2,1)S(1)} collective-permute-done((bf16[12,24,128]{2,1,0:T(8,128)(2,1)S(1)}, bf16[12,24,128]{2,1,0:T(8,128)(2,1)S(1)}, u32[]{:S(2)}, u32[]{:S(2)}) %collective-permute-start.7) | collective-permute-done | bytes 73760 | tf_op jit(solution)/shard_map/ppermute | solution.py:343
  41.4 0.6 shard_map.89
  42.0 1.2 %collective-permute-done.10.refs_12_ = bf16[12,24,128]{2,1,0:T(8,128)(2,1)S(1)} collective-permute-done((bf16[12,24,128]{2,1,0:T(8,128)(2,1)S(1)}, bf16[12,24,128]{2,1,0:T(8,128)(2,1)S(1)}, u32[]{:S(2)}, u32[]{:S(2)}) %collective-permute-start.10) | collective-permute-done | bytes 73760 | tf_op jit(solution)/shard_map/ppermute | solution.py:343
  43.3 1.9 %last.1 = (bf16[2,8,16,128]{3,2,1,0:T(8,128)(2,1)}, bf16[9,128,128]{2,1,0:T(8,128)(2,1)S(1)}, bf16[9,128,128]{2,1,0:T(8,128)(2,1)S(1)}) custom-call(s32[2]{0:T(128)S(1)} %pad_add_fusion.refs_0_, bf16[2,2,24,32,128]{4,3,2,1,0:T(8,128)(2,1)S(1)} %pad_maximum_fusion.refs_1_, bf16[384,384]{1,0:T(8,128)(2,1)S(1)} %bitcast.45, bf16[384,384]{1,0:T(8,128)(2,1)S(1)} %bitcast.37, ...), custom_call_target="tpu_custom_call" | custom-call | tf_op jit(solution)/shard_map/last/pallas_call | solution.py:361
  45.2 3.6 %collective-permute-start.11 = (bf16[9,128,128]{2,1,0:T(8,128)(2,1)S(1)}, bf16[9,128,128]{2,1,0:T(8,128)(2,1)S(1)}, u32[]{:S(2)}, u32[]{:S(2)}) collective-permute-start(bf16[9,128,128]{2,1,0:T(8,128)(2,1)S(1)} %get-tuple-element.27), channel_id=1, source_target_pairs={{0,8},{8,0},{1,9},{9,1},{2,10},{10,2},{3,11},{11,3},{4,12},{12,4},... | collective-permute-start | bytes 884744 | tf_op jit(solution)/shard_map/ppermute | solution.py:248
  48.9 1.2 %collective-permute-done.11 = bf16[9,128,128]{2,1,0:T(8,128)(2,1)S(1)} collective-permute-done((bf16[9,128,128]{2,1,0:T(8,128)(2,1)S(1)}, bf16[9,128,128]{2,1,0:T(8,128)(2,1)S(1)}, u32[]{:S(2)}, u32[]{:S(2)}) %collective-permute-start.11) | collective-permute-done | bytes 294944 | tf_op jit(solution)/shard_map/ppermute | solution.py:248
  50.0 0.1 add_convert_fusion
  50.1 0.1 reshape.57
  50.2 32.0 %all_to_all.10 = bf16[64,18,128]{2,1,0:T(8,128)(2,1)S(1)} all-to-all(bf16[64,18,128]{2,1,0:T(8,128)(2,1)S(1)} %reshape.57), channel_id=1, replica_groups=mesh['section'=4,'row_0'=8,'row_1'=2,'col_0'=2,'col_1'=4] {'row_0','col_..., dimensions={0} | all-to-all | bytes 589824 | tf_op jit(solution)/shard_map/all_to_all | solution.py:216
  82.3 0.1 convert_reduce_fusion
  82.4 22.8 %all_to_all.11.half = bf16[64,18,128]{2,1,0:T(8,128)(2,1)S(1)} all-to-all(bf16[64,18,128]{2,1,0:T(8,128)(2,1)S(1)} %broadcast_in_dim.10), channel_id=1, replica_groups=mesh['section'=4,'row_0'=8,'row_1'=2,'col_0'=2,'col_1'=4] {'row_0','col_..., dimensions={0} | all-to-all | bytes 589824 | tf_op jit(solution)/shard_map/all_to_all | solution.py:222
  105.2 4.8 %collective-permute-start.12 = (bf16[64,18,128]{2,1,0:T(8,128)(2,1)S(1)}, bf16[64,18,128]{2,1,0:T(8,128)(2,1)S(1)}, u32[]{:S(2)}, u32[]{:S(2)}) collective-permute-start(bf16[64,18,128]{2,1,0:T(8,128)(2,1)S(1)} %all_to_all.11.half), channel_id=1, source_target_pairs={{0,8},{8,0},{1,9},{9,1},{2,10},{10,2},{3,11},{11,3},{4,12},{12,4},... | collective-permute-start | bytes 884744 | tf_op jit(solution)/shard_map/ppermute | solution.py:254
  110.0 1.3 %collective-permute-done.12.other = bf16[64,18,128]{2,1,0:T(8,128)(2,1)S(1)} collective-permute-done((bf16[64,18,128]{2,1,0:T(8,128)(2,1)S(1)}, bf16[64,18,128]{2,1,0:T(8,128)(2,1)S(1)}, u32[]{:S(2)}, u32[]{:S(2)}) %collective-permute-start.12) | collective-permute-done | bytes 294944 | tf_op jit(solution)/shard_map/ppermute | solution.py:254
  111.3 1.1 write.1
  (30 shorter events, 0.5 us)
Async XLA Ops:
  0.6 18.2 %copy-start.1 = (bf16[1,2,3,3,128,128]{5,4,3,2,1,0:T(8,128)(2,1)S(1)}, bf16[1,2,3,3,128,128]{5,4,3,2,1,0:T(8,128)(2,1)}, u32[]{:S(2)}) copy-start(bf16[1,2,3,3,128,128]{5,4,3,2,1,0:T(8,128)(2,1)} %param.11) | copy-start | bytes 1769476
  2.4 12.2 %collective-permute-start = (bf16[2,2,8,8,128]{4,3,2,1,0:T(8,128)(2,1)S(1)}, bf16[2,2,8,8,128]{4,3,2,1,0:T(8,128)(2,1)S(1)}, u32[]{:S(2)}, u32[]{:S(2)}) collective-permute-start(bf16[2,2,8,8,128]{4,3,2,1,0:T(8,128)(2,1)S(1)} %get-tuple-element.15), channel_id=1, source_target_pairs={{1,2},{3,4},{5,6},{2,1},{4,3},{6,5},{9,10},{11,12},{13,14},{10,9},... | collective-permute-start | bytes 196616 | tf_op jit(solution)/shard_map/ppermute | solution.py:198
  3.0 11.6 %collective-permute-start.1 = (bf16[2,2,8,8,128]{4,3,2,1,0:T(8,128)(2,1)S(1)}, bf16[2,2,8,8,128]{4,3,2,1,0:T(8,128)(2,1)S(1)}, u32[]{:S(2)}, u32[]{:S(2)}) collective-permute-start(bf16[2,2,8,8,128]{4,3,2,1,0:T(8,128)(2,1)S(1)} %get-tuple-element.16), channel_id=1, source_target_pairs={{0,1},{1,0},{2,3},{3,2},{4,5},{5,4},{6,7},{7,6},{8,9},{9,8},{10,11... | collective-permute-start | bytes 196616 | tf_op jit(solution)/shard_map/ppermute | solution.py:202
  9.4 11.6 %collective-permute-start.3 = (bf16[2,2,8,16,128]{4,3,2,1,0:T(8,128)(2,1)S(1)}, bf16[2,2,8,16,128]{4,3,2,1,0:T(8,128)(2,1)S(1)}, u32[]{:S(2)}, u32[]{:S(2)}) collective-permute-start(bf16[2,2,8,16,128]{4,3,2,1,0:T(8,128)(2,1)S(1)} %get-tuple-element.18), channel_id=1, source_target_pairs={{8,16},{24,32},{40,48},{56,64},{72,80},{88,96},{104,112},{16,8},{3... | collective-permute-start | bytes 393224 | tf_op jit(solution)/shard_map/ppermute | solution.py:198
  14.7 6.3 %collective-permute-start.2 = (bf16[2,2,8,16,128]{4,3,2,1,0:T(8,128)(2,1)S(1)}, bf16[2,2,8,16,128]{4,3,2,1,0:T(8,128)(2,1)S(1)}, u32[]{:S(2)}, u32[]{:S(2)}) collective-permute-start(bf16[2,2,8,16,128]{4,3,2,1,0:T(8,128)(2,1)S(1)} %pad_maximum_fusion.3), channel_id=1, source_target_pairs={{8,16},{24,32},{40,48},{56,64},{72,80},{88,96},{104,112},{16,8},{3... | collective-permute-start | bytes 393224 | tf_op jit(solution)/shard_map/ppermute | solution.py:198
  16.9 4.1 %collective-permute-start.4 = (bf16[2,2,8,32,128]{4,3,2,1,0:T(8,128)(2,1)S(1)}, bf16[2,2,8,32,128]{4,3,2,1,0:T(8,128)(2,1)S(1)}, u32[]{:S(2)}, u32[]{:S(2)}) collective-permute-start(bf16[2,2,8,32,128]{4,3,2,1,0:T(8,128)(2,1)S(1)} %pad_maximum_fusion.2), channel_id=1, source_target_pairs={{0,8},{8,0},{16,24},{24,16},{32,40},{40,32},{48,56},{56,48},{64,72... | collective-permute-start | bytes 786440 | tf_op jit(solution)/shard_map/ppermute | solution.py:202
  21.2 1.4 %collective-permute-start.5 = (bf16[10,56,128]{2,1,0:T(8,128)(2,1)S(1)}, bf16[10,56,128]{2,1,0:T(8,128)(2,1)S(1)}, u32[]{:S(2)}, u32[]{:S(2)}) collective-permute-start(bf16[10,56,128]{2,1,0:T(8,128)(2,1)S(1)} %shard_map.86), channel_id=1, source_target_pairs={{384,256},{385,257},{386,258},{387,259},{388,260},{389,261},{390,2... | collective-permute-start | bytes 430088 | tf_op jit(solution)/shard_map/ppermute | solution.py:343
  21.9 1.4 %collective-permute-start.8 = (bf16[10,56,128]{2,1,0:T(8,128)(2,1)S(1)}, bf16[10,56,128]{2,1,0:T(8,128)(2,1)S(1)}, u32[]{:S(2)}, u32[]{:S(2)}) collective-permute-start(bf16[10,56,128]{2,1,0:T(8,128)(2,1)S(1)} %shard_map.90), channel_id=1, source_target_pairs={{384,256},{385,257},{386,258},{387,259},{388,260},{389,261},{390,2... | collective-permute-start | bytes 430088 | tf_op jit(solution)/shard_map/ppermute | solution.py:343
  22.6 1.4 %collective-permute-start.6 = (bf16[16,24,128]{2,1,0:T(8,128)(2,1)S(1)}, bf16[16,24,128]{2,1,0:T(8,128)(2,1)S(1)}, u32[]{:S(2)}, u32[]{:S(2)}) collective-permute-start(bf16[16,24,128]{2,1,0:T(8,128)(2,1)S(1)} %shard_map.87), channel_id=1, source_target_pairs={{256,128},{257,129},{258,130},{259,131},{260,132},{261,133},{262,1... | collective-permute-start | bytes 294920 | tf_op jit(solution)/shard_map/ppermute | solution.py:343
  23.3 2.0 %collective-permute-start.9 = (bf16[16,24,128]{2,1,0:T(8,128)(2,1)S(1)}, bf16[16,24,128]{2,1,0:T(8,128)(2,1)S(1)}, u32[]{:S(2)}, u32[]{:S(2)}) collective-permute-start(bf16[16,24,128]{2,1,0:T(8,128)(2,1)S(1)} %shard_map.91), channel_id=1, source_target_pairs={{256,128},{257,129},{258,130},{259,131},{260,132},{261,133},{262,1... | collective-permute-start | bytes 294920 | tf_op jit(solution)/shard_map/ppermute | solution.py:343
  24.1 17.3 %collective-permute-start.7 = (bf16[12,24,128]{2,1,0:T(8,128)(2,1)S(1)}, bf16[12,24,128]{2,1,0:T(8,128)(2,1)S(1)}, u32[]{:S(2)}, u32[]{:S(2)}) collective-permute-start(bf16[12,24,128]{2,1,0:T(8,128)(2,1)S(1)} %shard_map.88), channel_id=1, source_target_pairs={{128,0},{129,1},{130,2},{131,3},{132,4},{133,5},{134,6},{135,7},{1... | collective-permute-start | bytes 221192 | tf_op jit(solution)/shard_map/ppermute | solution.py:343
  25.4 17.9 %copy-start = (bf16[1,2,8,16,128]{4,3,2,1,0:T(8,128)(2,1)S(1)}, bf16[1,2,8,16,128]{4,3,2,1,0:T(8,128)(2,1)}, u32[]{:S(2)}) copy-start(bf16[1,2,8,16,128]{4,3,2,1,0:T(8,128)(2,1)} %param.7) | copy-start | bytes 196612
  25.4 17.9 %collective-permute-start.10 = (bf16[12,24,128]{2,1,0:T(8,128)(2,1)S(1)}, bf16[12,24,128]{2,1,0:T(8,128)(2,1)S(1)}, u32[]{:S(2)}, u32[]{:S(2)}) collective-permute-start(bf16[12,24,128]{2,1,0:T(8,128)(2,1)S(1)} %shard_map.92), channel_id=1, source_target_pairs={{128,0},{129,1},{130,2},{131,3},{132,4},{133,5},{134,6},{135,7},{1... | collective-permute-start | bytes 221192 | tf_op jit(solution)/shard_map/ppermute | solution.py:343
  45.2 4.8 %collective-permute-start.11 = (bf16[9,128,128]{2,1,0:T(8,128)(2,1)S(1)}, bf16[9,128,128]{2,1,0:T(8,128)(2,1)S(1)}, u32[]{:S(2)}, u32[]{:S(2)}) collective-permute-start(bf16[9,128,128]{2,1,0:T(8,128)(2,1)S(1)} %get-tuple-element.27), channel_id=1, source_target_pairs={{0,8},{8,0},{1,9},{9,1},{2,10},{10,2},{3,11},{11,3},{4,12},{12,4},... | collective-permute-start | bytes 884744 | tf_op jit(solution)/shard_map/ppermute | solution.py:248
  105.2 6.1 %collective-permute-start.12 = (bf16[64,18,128]{2,1,0:T(8,128)(2,1)S(1)}, bf16[64,18,128]{2,1,0:T(8,128)(2,1)S(1)}, u32[]{:S(2)}, u32[]{:S(2)}) collective-permute-start(bf16[64,18,128]{2,1,0:T(8,128)(2,1)S(1)} %all_to_all.11.half), channel_id=1, source_target_pairs={{0,8},{8,0},{1,9},{9,1},{2,10},{10,2},{3,11},{11,3},{4,12},{12,4},... | collective-permute-start | bytes 884744 | tf_op jit(solution)/shard_map/ppermute | solution.py:254
